TPU v7x, 256 devices: a 4x2x16 block of a 4x16x16 slice. The times are simulated.
256 devices in a mesh: groups: 2 (over y), lon: 128 (over z, x, core).
Axes of the slice: x: 4, y: 2, z: 16, core: 2. Of those that a mesh axis runs over, the one named last changes fastest.
The devices are a block of a 4x16x16 slice.
Arguments:
- fields: bfloat16 [4, 24, 1536, 192], P('groups', None, 'lon'), parts along dimension 0, may hold values from -6 to 6
- norm_gain: float32 [192], replicated, may hold values from 0.25 to 1.75
- qkv_weight: bfloat16 [192, 576], replicated, may hold values from -2.5 to 2.5
- proj_weight: bfloat16 [192, 192], replicated, may hold values from -0.4375 to 0.4375
- bias_table: float32 [4, 6, 3312], replicated, may hold values from -4 to 4
- bias_index: int32 [144, 144], replicated, may hold values from 0 to 3311
- region_ids: int32 [2, 24], replicated, may hold values from 0 to 2
- mlp_gain: float32 [192], replicated, may hold values from 0.25 to 1.75
- up_weight: bfloat16 [192, 768], replicated, may hold values from -0.4375 to 0.4375
- down_weight: bfloat16 [768, 192], replicated, may hold values from -0.21875 to 0.21875
- merge_gain: float32 [768], replicated, may hold values from 0.25 to 1.75
- merge_weight: bfloat16 [768, 384], replicated, may hold values from -0.21875 to 0.21875
- cotangent: bfloat16 [4, 12, 768, 384], P('groups', None, 'lon'), parts along dimension 0, may hold values from -12 to 12
Outputs:
- merged: bfloat16 [4, 12, 768, 384], P('groups', None, 'lon'), parts along dimension 0
- field_grad: bfloat16 [4, 24, 1536, 192], P('groups', None, 'lon'), parts along dimension 0
- qkv_grad: float32 [384, 576], P('groups'), parts along dimension 0
- proj_grad: float32 [384, 192], P('groups'), parts along dimension 0
- up_grad: float32 [384, 768], P('groups'), parts along dimension 0
- down_grad: float32 [1536, 192], P('groups'), parts along dimension 0
- merge_grad: float32 [1536, 384], P('groups'), parts along dimension 0
- table_grad: float32 [8, 6, 3312], P('groups'), parts along dimension 0
There are 2 independent parts, one for each index of `groups`. A program takes and returns all parts, laid end to end along the dimension named above; an argument that names none is the same for every part. Nothing has to cross between parts.
All inputs are finite; a program needn't handle non-finite values.
Results may differ from a plain program's by a relative error of at most 0.019.
The roundings to bfloat16 on the way count: a program that leaves them out, or rounds other values in their place, can miss the bound.
Values may be sent and summed in bfloat16 or wider, within the bound.
No kernel may reach another device: no remote copies, remote signals or barrier semaphores. Data moves between devices by JAX's collectives and lax.ppermute only.
A program may use at most 192 MiB of HBM per device.

v0:
```python
import jax
import jax.numpy as jnp
from jax import lax
from jax.experimental import pallas as pl
from jax.experimental.pallas import tpu as pltpu
from jax.sharding import PartitionSpec as P

C = 192
MLP = 768
HEADS = 6
HEAD = 32
HALF = 6
WIN = 144
BPOS = 3312
LAT = 24
TYPES = 4
TOK = TYPES * WIN
LEVELS = 2
LANES = 128
MAIN = 128
REST = WIN - MAIN
TH = TYPES * HEADS
LOW = 256
HIGH = -(-BPOS // LOW)
MTOK = 160
EPS = 1e-5
MASKED = -1e30
F32 = jnp.float32
BF = jnp.bfloat16
CORES = 2
ACROSS = 4

TROWS = 320
O_UP = 0
O_MERGE = O_UP + 6 * C
O_DOWN = O_MERGE + 3 * MLP
O_QKV = O_DOWN + 6 * C
O_QKV_TAIL = O_QKV + 4 * C
O_PROJ = O_QKV_TAIL + C // 2
O_PROJ_TAIL = O_PROJ + C
O_TABLE = O_PROJ_TAIL + C // 2
O_END = O_TABLE + 2 * TROWS


def dot(a, b):
    return jnp.dot(a, b, preferred_element_type=F32)


def dot_nt(a, b):
    return lax.dot_general(a, b, (((1,), (1,)), ((), ())), preferred_element_type=F32)


def dot_tn(a, b):
    return lax.dot_general(a, b, (((0,), (0,)), ((), ())), preferred_element_type=F32)


def div(n, d):
    return (n * -(-(1 << 16) // d)) >> 16


def onehot(rows, cols, of_row=None, of_col=None):
    if of_row is not None:
        target = of_row(lax.broadcasted_iota(jnp.int32, (rows, 1), 0))
        place = lax.broadcasted_iota(jnp.int32, (rows, cols), 1)
    else:
        target = of_col(lax.broadcasted_iota(jnp.int32, (1, cols), 1))
        place = lax.broadcasted_iota(jnp.int32, (rows, cols), 0)
    return jnp.where(place == target, 1.0, 0.0).astype(BF)


def cell_of_token(n):
    kind = div(n, 72)
    rest = n - 72 * kind
    lat = div(rest, 12)
    return (rest - 12 * lat) * LAT + kind * 6 + lat


def token_of_group(n):
    quarter = div(n, 40)
    rest = n - 40 * quarter
    level = div(rest, 18)
    part = rest - 18 * level
    lat = div(part, 6)
    token = level * 72 + (2 * lat + (quarter >> 1)) * 12 + 2 * (part - 6 * lat) + (quarter & 1)
    return jnp.where(rest < 36, token, -1)


def group_of_token(n):
    level = div(n, 72)
    rest = n - 72 * level
    lat = div(rest, 12)
    lon = rest - 12 * lat
    return ((lat & 1) * 2 + (lon & 1)) * 40 + level * 18 + (lat >> 1) * 6 + (lon >> 1)


def cell_of_merged(n):
    kind = div(n, 40)
    rest = n - 40 * kind
    level = div(rest, 18)
    part = rest - 18 * level
    lat = div(part, 6)
    lon = part - 6 * lat
    half = jnp.where(lon < 3, 0, 1)
    row = half * 72 + (3 * kind + lat) * 6 + (lon - 3 * half) * 2 + level
    return jnp.where(rest < 36, row, -1)


def normalised(values):
    centred = values - jnp.mean(values, axis=-1, keepdims=True)
    scale = lax.rsqrt(jnp.mean(centred * centred, axis=-1, keepdims=True) + EPS)
    return centred * scale, scale


def norm_grad(grad, unit, scale, gain):
    scaled = grad * gain
    return scale * (
        scaled
        - jnp.mean(scaled, axis=-1, keepdims=True)
        - unit * jnp.mean(scaled * unit, axis=-1, keepdims=True)
    )


def rounded(values):
    return values.astype(BF).astype(F32)


def low_onehot(low):
    return jnp.where(
        lax.broadcasted_iota(jnp.int32, (LOW, low.shape[1]), 0) == low, 1.0, 0.0
    ).astype(BF)


def bias_kernel(table_ref, index_ref, region_ref, main_ref, tail_ref, part_ref, last_ref, turned_ref):
    for high in range(HIGH):
        width = min(LOW, BPOS - high * LOW)
        piece = table_ref[:, high * LOW : high * LOW + width]
        if width < LOW:
            piece = jnp.concatenate([piece, jnp.zeros((TH, LOW - width), F32)], axis=1)
        leading = rounded(piece)
        part_ref[high * TH : (high + 1) * TH, :LOW] = leading
        part_ref[high * TH : (high + 1) * TH, LOW:] = piece - leading
    turned_ref[...] = jnp.transpose(index_ref[:, MAIN:])
    parts = part_ref[...].astype(BF)

    def looked_up(index):
        low = low_onehot(index & (LOW - 1))
        high_row = index >> 8
        found = dot(parts, jnp.concatenate([low, low], axis=0))
        chosen = found[0:TH]
        for high in range(1, HIGH):
            chosen = jnp.where(high_row == high, found[high * TH : (high + 1) * TH], chosen)
        return chosen

    def row_block(block, carry):
        base = pl.multiple_of(block * 8, 8)
        rows = index_ref[pl.ds(base, 8), :MAIN]
        for part in range(2):
            index = jnp.concatenate([rows[4 * part + n : 4 * part + n + 1] for n in range(4)], axis=1)
            got = looked_up(index)
            for n in range(4):
                main_ref[pl.ds(base + 4 * part + n, TH, stride=WIN), :] = got[:, n * MAIN : (n + 1) * MAIN]
        return carry

    lax.fori_loop(0, WIN // 8, row_block, 0)
    blank = jnp.zeros((1, LOW - WIN), jnp.int32)
    for key in range(0, REST, 2):
        index = jnp.concatenate(
            [turned_ref[key : key + 1, :], blank, turned_ref[key + 1 : key + 2, :], blank], axis=1
        )
        got = looked_up(index)
        for n in range(2):
            last_ref[pl.ds(key + n, TH, stride=REST), :] = got[:, 256 * n : 256 * n + 128]
            last_ref[pl.ds(TH * REST + key + n, TH, stride=REST), :] = got[:, 256 * n + 128 : 256 * n + 256]
    for kind in range(TYPES):
        across = jnp.zeros((1, WIN), jnp.int32)
        down = jnp.zeros((WIN, 1), jnp.int32)
        column = lax.broadcasted_iota(jnp.int32, (1, WIN), 1)
        row = lax.broadcasted_iota(jnp.int32, (WIN, 1), 0)
        for group in range(12):
            label = region_ref[group // 6, 6 * kind + group % 6]
            across = jnp.where((column >= 12 * group) & (column < 12 * group + 12), label, across)
            down = jnp.where((row >= 12 * group) & (row < 12 * group + 12), label, down)
        same = down == across
        for head in range(HEADS):
            th = head * TYPES + kind
            rows = slice(th * WIN, (th + 1) * WIN)
            main_ref[rows, :] = jnp.where(same[:, :MAIN], main_ref[rows, :], MASKED)
            tail = jnp.concatenate(
                [
                    jnp.transpose(last_ref[th * REST : (th + 1) * REST, :]),
                    jnp.transpose(last_ref[(TH + th) * REST : (TH + th + 1) * REST, :REST]),
                ],
                axis=0,
            )
            tail_ref[rows, :REST] = jnp.where(same[:, MAIN:], tail, MASKED)


def bias_rows(table, index, regions):
    whole = pl.BlockSpec(memory_space=pltpu.VMEM)
    return pl.pallas_call(
        bias_kernel,
        out_shape=[jax.ShapeDtypeStruct((TH * WIN, LANES), F32)] * 2,
        in_specs=[whole, whole, pl.BlockSpec(memory_space=pltpu.SMEM)],
        out_specs=[whole, whole],
        scratch_shapes=[
            pltpu.VMEM((HIGH * TH, 2 * LOW), F32),
            pltpu.VMEM((2 * TH * REST, LANES), F32),
            pltpu.VMEM((REST, WIN), jnp.int32),
        ],
        compiler_params=pltpu.CompilerParams(vmem_limit_bytes=16 * 1024 * 1024),
        cost_estimate=pl.CostEstimate(flops=14_000_000_000, bytes_accessed=4_000_000, transcendentals=0),
        name="bias_rows",
    )(table, index, regions)


def block_kernel(
    core_ref, own_ref, east_ref, own_cotangent_ref, east_cotangent_ref,
    norm_gain_ref, qkv_ref, proj_ref, mlp_gain_ref, up_ref, down_ref, merge_gain_ref, merge_ref,
    bias_ref, bias_tail_ref, index_ref,
    keep_ref, send_ref, merged_keep_ref, merged_send_ref, field_keep_ref, field_send_ref,
    x_ref, unit_ref, scale_ref, tokens_ref, q_ref, k_ref, v_ref, p_ref, mixed_ref,
    unit_mlp_ref, scale_mlp_ref, normed_mlp_ref, hidden_ref, slope_ref, after_mlp_ref,
    group_ref, normed_merge_ref, grad_after_ref, grad_up_ref, grad_attn_ref, grad_mixed_ref,
    ds_ref, ds_tail_ref, ds_corner_ref, dq_ref, dk_ref, dv_ref, grads_ref, turned_ref,
):
    to_tokens = onehot(288, 288, of_row=cell_of_token)
    for level in range(LEVELS):
        cells = jnp.concatenate(
            [
                own_ref[level].astype(F32).reshape(144, C),
                east_ref[level].astype(F32).reshape(144, C),
            ],
            axis=0,
        ).astype(BF)
        ordered = dot(to_tokens, cells)
        for kind in range(TYPES):
            x_ref[WIN * kind + 72 * level : WIN * kind + 72 * level + 72, :] = ordered[72 * kind : 72 * kind + 72]
    unit, scale = normalised(x_ref[...])
    unit_ref[...] = unit
    scale_ref[...] = scale
    tokens = (unit * norm_gain_ref[...]).astype(BF)
    tokens_ref[...] = tokens
    q_ref[...] = dot(tokens, qkv_ref[:, 0:C]).astype(BF)
    k_ref[...] = dot(tokens, qkv_ref[:, C : 2 * C]).astype(BF)
    v_ref[...] = dot(tokens, qkv_ref[:, 2 * C :]).astype(BF)
    lane = lax.broadcasted_iota(jnp.int32, (1, C), 1)
    of_head = [
        jnp.where((lane >= HEAD * h) & (lane < HEAD * (h + 1)), 1.0, 0.0).astype(BF) for h in range(HEADS)
    ]
    temper = HEAD ** (-0.5)

    def attend(kind, carry):
        rows = pl.ds(pl.multiple_of(kind * WIN, 16), WIN)
        q, k, v = q_ref[rows, :], k_ref[rows, :], v_ref[rows, :]
        mixed = jnp.zeros((WIN, C), F32)
        for h in range(HEADS):
            th = h * TYPES + kind
            scores_at = pl.ds(pl.multiple_of(th * WIN, 16), WIN)
            bias = jnp.concatenate([bias_ref[scores_at, :], bias_tail_ref[scores_at, :REST]], axis=1)
            scores = dot_nt(q * of_head[h], k) * temper + bias
            weights = jnp.exp(scores - jnp.max(scores, axis=-1, keepdims=True))
            p = (weights * (1.0 / jnp.sum(weights, axis=-1, keepdims=True))).astype(BF)
            p_ref[th] = p
            mixed = mixed + dot(p, v * of_head[h])
        mixed_ref[rows, :] = mixed.astype(BF)
        return carry

    lax.fori_loop(0, TYPES, attend, 0)
    after_attn = rounded(x_ref[...] + rounded(dot(mixed_ref[...], proj_ref[...])))
    x_ref[...] = after_attn
    unit, scale = normalised(after_attn)
    unit_mlp_ref[...] = unit
    scale_mlp_ref[...] = scale
    normed_mlp = (unit * mlp_gain_ref[...]).astype(BF)
    normed_mlp_ref[...] = normed_mlp
    for part in range(3):
        cols = slice(256 * part, 256 * part + 256)
        u = dot(normed_mlp, up_ref[:, cols])
        below = 0.5 * (1.0 + lax.erf(u * 0.5**0.5))
        hidden_ref[:, cols] = (u * below).astype(BF)
        slope_ref[:, cols] = below + u * (jnp.exp(u * u * (-0.5)) * 0.3989422804014327)
    after_mlp_ref[...] = (x_ref[...] + dot_nt(hidden_ref[...], down_ref[...])).astype(BF)

    to_groups = onehot(160, WIN, of_row=token_of_group)
    for kind in range(TYPES):
        grouped = dot(to_groups, after_mlp_ref[WIN * kind : WIN * kind + WIN, :])
        for quarter in range(4):
            group_ref[quarter, 40 * kind : 40 * kind + 40, :] = grouped[40 * quarter : 40 * quarter + 40]
    quarters = [group_ref[n] for n in range(4)]
    mean = sum(jnp.sum(v, axis=-1, keepdims=True) for v in quarters) * (1.0 / MLP)
    centred = [v - mean for v in quarters]
    variance = sum(jnp.sum(v * v, axis=-1, keepdims=True) for v in centred) * (1.0 / MLP)
    scale_merge = lax.rsqrt(variance + EPS)
    merged = jnp.zeros((MTOK, 2 * C), F32)
    for n in range(4):
        unit = centred[n] * scale_merge
        group_ref[n] = unit
        normed_merge = (unit * merge_gain_ref[n : n + 1, :]).astype(BF)
        normed_merge_ref[n] = normed_merge
        merged = merged + dot(normed_merge, merge_ref[C * n : C * (n + 1), :])
    merged_cells = dot(onehot(144, MTOK, of_col=cell_of_merged), merged.astype(BF)).astype(BF)
    merged_keep_ref[...] = merged_cells[:72]
    merged_send_ref[...] = merged_cells[72:]
    cotangent = jnp.concatenate(
        [own_cotangent_ref[...].astype(F32), east_cotangent_ref[...].astype(F32)], axis=0
    ).astype(BF)
    grad_merged = dot(onehot(MTOK, 144, of_row=cell_of_merged), cotangent).astype(BF)

    scaled, total, along = [], 0.0, 0.0
    for n in range(4):
        grad = dot_tn(normed_merge_ref[n], grad_merged).astype(BF)
        for b in range(3):
            start = O_MERGE + MLP * b + C * n
            grads_ref[start : start + C, :] = grad[:, 128 * b : 128 * b + 128]
        value = rounded(dot_nt(grad_merged, merge_ref[C * n : C * (n + 1), :])) * merge_gain_ref[n : n + 1, :]
        total = total + jnp.sum(value, axis=-1, keepdims=True)
        along = along + jnp.sum(value * group_ref[n], axis=-1, keepdims=True)
        scaled.append(value)
    total = total * (1.0 / MLP)
    along = along * (1.0 / MLP)
    for n in range(4):
        group_ref[n] = scale_merge * (scaled[n] - total - group_ref[n] * along)
    from_groups = onehot(WIN, 160, of_row=group_of_token)
    for kind in range(TYPES):
        grouped = jnp.concatenate([group_ref[n, 40 * kind : 40 * kind + 40, :] for n in range(4)], axis=0)
        grad_after_ref[WIN * kind : WIN * kind + WIN, :] = dot(from_groups, grouped.astype(BF)).astype(BF)

    grad_after = grad_after_ref[...]
    for part in range(3):
        cols = slice(256 * part, 256 * part + 256)
        grad_up_ref[:, cols] = (rounded(dot(grad_after, down_ref[:, cols])) * slope_ref[:, cols]).astype(BF)
    grad_down = dot_tn(grad_after, hidden_ref[...]).astype(BF)
    grad_up = dot_tn(normed_mlp_ref[...], grad_up_ref[...]).astype(BF)
    for b in range(6):
        grads_ref[O_DOWN + C * b : O_DOWN + C * (b + 1), :] = grad_down[:, 128 * b : 128 * b + 128]
        grads_ref[O_UP + C * b : O_UP + C * (b + 1), :] = grad_up[:, 128 * b : 128 * b + 128]
    grad_normed = rounded(dot_nt(grad_up_ref[...], up_ref[...]))
    grad_attn = (
        grad_after.astype(F32)
        + norm_grad(grad_normed, unit_mlp_ref[...], scale_mlp_ref[...], mlp_gain_ref[...])
    ).astype(BF)
    grad_attn_ref[...] = grad_attn

    grad_proj = dot_tn(mixed_ref[...], grad_attn).astype(BF)
    grads_ref[O_PROJ : O_PROJ + C, :] = grad_proj[:, :128]
    grads_ref[O_PROJ_TAIL : O_PROJ_TAIL + C // 2, :] = jnp.concatenate(
        [grad_proj[: C // 2, 128:], grad_proj[C // 2 :, 128:]], axis=1
    )
    grad_mixed_ref[...] = dot_nt(grad_attn, proj_ref[...]).astype(BF)
    ds_corner_ref[...] = jnp.zeros(ds_corner_ref.shape, F32)

    def attend_back(kind, carry):
        rows = pl.ds(pl.multiple_of(kind * WIN, 16), WIN)
        q, k, v, grad = q_ref[rows, :], k_ref[rows, :], v_ref[rows, :], grad_mixed_ref[rows, :]
        dq = jnp.zeros((WIN, C), F32)
        dk = jnp.zeros((WIN, C), F32)
        dv = jnp.zeros((WIN, C), F32)
        for h in range(HEADS):
            th = h * TYPES + kind
            grad_head = grad * of_head[h]
            p = p_ref[th]
            wide = p.astype(F32)
            dp = rounded(dot_nt(grad_head, v))
            ds = wide * (dp - jnp.sum(wide * dp, axis=-1, keepdims=True))
            ds_ref[pl.ds(pl.multiple_of(th * WIN, 16), WIN), :] = ds[:, :MAIN]
            turned = jnp.transpose(
                jnp.concatenate([ds[:, MAIN:], jnp.zeros((WIN, LANES - REST), F32)], axis=1)
            )
            at = pl.ds(pl.multiple_of(th * REST, 16), REST)
            ds_tail_ref[at, :] = turned[:REST, :MAIN]
            ds_corner_ref[at, :REST] = turned[:REST, MAIN:]
            grad_scores = (ds * temper).astype(BF)
            dv = dv + dot_tn(p, grad_head)
            dk = dk + dot_tn(grad_scores, q * of_head[h])
            dq = dq + dot(grad_scores, k * of_head[h])
        dq_ref[rows, :] = dq.astype(BF)
        dk_ref[rows, :] = dk.astype(BF)
        dv_ref[rows, :] = dv.astype(BF)
        return carry

    lax.fori_loop(0, TYPES, attend_back, 0)
    grad_triple = jnp.concatenate([dq_ref[...], dk_ref[...], dv_ref[...]], axis=1)
    grad_qkv = dot_tn(tokens_ref[...], grad_triple).astype(BF)
    for b in range(4):
        grads_ref[O_QKV + C * b : O_QKV + C * (b + 1), :] = grad_qkv[:, 128 * b : 128 * b + 128]
    grads_ref[O_QKV_TAIL : O_QKV_TAIL + C // 2, :] = jnp.concatenate(
        [grad_qkv[: C // 2, 512:], grad_qkv[C // 2 :, 512:]], axis=1
    )
    grad_normed = rounded(dot_nt(grad_triple, qkv_ref[...]))
    x_ref[...] = grad_attn_ref[...].astype(F32) + norm_grad(
        grad_normed, unit_ref[...], scale_ref[...], norm_gain_ref[...]
    )
    to_cells = onehot(288, 288, of_col=cell_of_token)
    for level in range(LEVELS):
        ordered = jnp.concatenate(
            [x_ref[WIN * kind + 72 * level : WIN * kind + 72 * level + 72, :] for kind in range(TYPES)], axis=0
        )
        cells = dot(to_cells, ordered.astype(BF))
        field_keep_ref[level] = cells[:144].reshape(HALF, LAT, C).astype(BF)
        field_send_ref[level] = cells[144:].reshape(HALF, LAT, C).astype(BF)

    turned_ref[...] = jnp.transpose(index_ref[:, MAIN:])

    def table_terms(index, slab):
        high_row = index >> 8
        spread = [jnp.where(high_row == n, slab, 0.0) for n in range(HIGH)]
        spread.append(jnp.zeros((TROWS - HIGH * TH, index.shape[1]), F32))
        return dot_nt(jnp.concatenate(spread, axis=0).astype(BF), low_onehot(index & (LOW - 1)))

    def row_block(block, carry):
        base = pl.multiple_of(block * 8, 8)
        rows = index_ref[pl.ds(base, 8), :MAIN]
        index = jnp.concatenate([rows[n : n + 1] for n in range(8)], axis=1)
        slab = jnp.concatenate([ds_ref[pl.ds(base + n, TH, stride=WIN), :] for n in range(8)], axis=1)
        return carry + table_terms(index, slab)

    table = lax.fori_loop(0, WIN // 8, row_block, jnp.zeros((TROWS, LOW), F32))
    blank = jnp.zeros((1, LOW - WIN), jnp.int32)
    for key in range(0, REST, 4):
        index, slab = [], []
        for n in range(key, key + 4):
            index += [turned_ref[n : n + 1, :], blank]
            slab += [ds_tail_ref[pl.ds(n, TH, stride=REST), :], ds_corner_ref[pl.ds(n, TH, stride=REST), :]]
        table = table + table_terms(jnp.concatenate(index, axis=1), jnp.concatenate(slab, axis=1))
    table = table.astype(BF)
    grads_ref[O_TABLE : O_TABLE + TROWS, :] = table[:, :LANES]
    grads_ref[O_TABLE + TROWS : O_END, :] = table[:, LANES:]
    half = keep_ref.shape[0]
    grads_ref[O_END:, :] = jnp.zeros((2 * half - O_END, LANES), BF)
    core = core_ref[0]
    keep_ref[...] = grads_ref[pl.ds(pl.multiple_of(core * half, 16), half), :]
    send_ref[...] = grads_ref[pl.ds(pl.multiple_of((1 - core) * half, 16), half), :]


def block(half_rows, *args):
    shape = jax.ShapeDtypeStruct
    whole = pl.BlockSpec(memory_space=pltpu.VMEM)
    scratch = [
        ((TOK, C), F32), ((TOK, C), F32), ((TOK, 1), F32), ((TOK, C), BF), ((TOK, C), BF), ((TOK, C), BF),
        ((TOK, C), BF), ((TH, WIN, WIN), BF), ((TOK, C), BF),
        ((TOK, C), F32), ((TOK, 1), F32), ((TOK, C), BF), ((TOK, MLP), BF), ((TOK, MLP), F32), ((TOK, C), BF),
        ((4, MTOK, C), F32), ((4, MTOK, C), BF), ((TOK, C), BF), ((TOK, MLP), BF), ((TOK, C), BF), ((TOK, C), BF),
        ((TH * WIN, LANES), F32), ((TH * REST, LANES), F32), ((TH * REST, LANES), F32),
        ((TOK, C), BF), ((TOK, C), BF), ((TOK, C), BF), ((2 * half_rows, LANES), BF), ((REST, WIN), jnp.int32),
    ]
    return pl.pallas_call(
        block_kernel,
        out_shape=[
            shape((half_rows, LANES), BF),
            shape((half_rows, LANES), BF),
            shape((72, 2 * C), BF),
            shape((72, 2 * C), BF),
            shape((LEVELS, HALF, LAT, C), BF),
            shape((LEVELS, HALF, LAT, C), BF),
        ],
        in_specs=[pl.BlockSpec(memory_space=pltpu.SMEM)] + [whole] * (len(args) - 1),
        out_specs=[whole] * 6,
        scratch_shapes=[pltpu.VMEM(*item) for item in scratch],
        compiler_params=pltpu.CompilerParams(vmem_limit_bytes=40 * 1024 * 1024),
        cost_estimate=pl.CostEstimate(flops=24_000_000_000, bytes_accessed=12_000_000, transcendentals=2_000_000),
        name="block",
    )(*args)


def finish_kernel(factor, core_ref, held_ref, other_ref, qkv_ref, proj_ref, up_ref, down_ref, merge_ref, table_ref, grads_ref):
    core = core_ref[0]
    half = held_ref.shape[0]
    grads_ref[pl.ds(pl.multiple_of(core * half, 16), half), :] = held_ref[...]
    grads_ref[pl.ds(pl.multiple_of((1 - core) * half, 16), half), :] = other_ref[...]

    def part(start, rows):
        return grads_ref[start : start + rows, :].astype(F32) * factor

    for b in range(6):
        up_ref[:, 128 * b : 128 * b + 128] = part(O_UP + C * b, C)
        down_ref[:, 128 * b : 128 * b + 128] = part(O_DOWN + C * b, C)
    for b in range(3):
        merge_ref[:, 128 * b : 128 * b + 128] = part(O_MERGE + MLP * b, MLP)
    for b in range(4):
        qkv_ref[:, 128 * b : 128 * b + 128] = part(O_QKV + C * b, C)
    tail = part(O_QKV_TAIL, C // 2)
    qkv_ref[: C // 2, 512:] = tail[:, :64]
    qkv_ref[C // 2 :, 512:] = tail[:, 64:]
    proj_ref[:, :128] = part(O_PROJ, C)
    tail = part(O_PROJ_TAIL, C // 2)
    proj_ref[: C // 2, 128:] = tail[:, :64]
    proj_ref[C // 2 :, 128:] = tail[:, 64:]
    for side in range(2):
        table = part(O_TABLE + TROWS * side, TROWS)
        for high in range(HIGH):
            start = high * LOW + side * LANES
            width = min(LANES, BPOS - start)
            for head in range(HEADS):
                row = high * TH + head * TYPES
                table_ref[head, :, start : start + width] = table[row : row + TYPES, :width]


def finish(core, held, other, factor):
    shape = jax.ShapeDtypeStruct
    whole = pl.BlockSpec(memory_space=pltpu.VMEM)
    return pl.pallas_call(
        lambda *refs: finish_kernel(factor, *refs),
        out_shape=[
            shape((C, 3 * C), F32),
            shape((C, C), F32),
            shape((C, MLP), F32),
            shape((C, MLP), F32),
            shape((MLP, 2 * C), F32),
            shape((HEADS, TYPES, BPOS), F32),
        ],
        in_specs=[pl.BlockSpec(memory_space=pltpu.SMEM), whole, whole],
        out_specs=[whole] * 6,
        scratch_shapes=[pltpu.VMEM((2 * held.shape[0], LANES), BF)],
        compiler_params=pltpu.CompilerParams(vmem_limit_bytes=16 * 1024 * 1024),
        name="finish",
    )(core, held, other)


def passed_along(value, axis, steps):
    count = lax.axis_size(axis)
    return lax.ppermute(value, axis, [(source, (source + steps) % count) for source in range(count)])


def groups_of(count, apart, size):
    return [
        [start * apart * size + offset + member * apart for member in range(size)]
        for start in range(count // (apart * size))
        for offset in range(apart)
    ]


def summed_over(keep, send, axis):
    count = lax.axis_size(axis)
    along = count // (CORES * ACROSS)
    pairs = [(i, i ^ 1) for i in range(count)]
    held = (keep.astype(F32) + lax.ppermute(send, axis, pairs).astype(F32)).astype(BF)

    def exchanged(value, apart, size):
        return lax.all_to_all(value, axis, 0, 0, axis_index_groups=groups_of(count, apart, size))

    def reduced(value, apart, size):
        got = exchanged(value.reshape(size, -1, LANES), apart, size)
        return jnp.sum(got.astype(F32), axis=0).astype(BF)

    def gathered(value, apart, size):
        return exchanged(jnp.broadcast_to(value[None], (size, *value.shape)), apart, size).reshape(-1, LANES)

    held = reduced(held, CORES, ACROSS)
    held = reduced(held, CORES * ACROSS, along)
    held = gathered(held, CORES * ACROSS, along)
    held = gathered(held, CORES, ACROSS)
    return held, lax.ppermute(held, axis, pairs)


def local(
    fields,
    norm_gain,
    qkv_weight,
    proj_weight,
    bias_table,
    bias_index,
    region_ids,
    mlp_gain,
    up_weight,
    down_weight,
    merge_gain,
    merge_weight,
    cotangent,
):
    count = lax.axis_size("lon")
    core = (lax.axis_index("lon") % CORES).astype(jnp.int32).reshape(1)
    by_lon = fields.transpose(0, 2, 1, 3)
    by_lat = cotangent.transpose(1, 2, 0, 3)
    east = passed_along(by_lon[:, :HALF], "lon", -1)
    east_cotangent = passed_along(by_lat[:, : HALF // 2], "lon", -1)
    bias, bias_tail = bias_rows(bias_table.transpose(1, 0, 2).reshape(TH, BPOS), bias_index, region_ids)
    half_rows = -(-O_END // (count * 8)) * 8 * count // CORES
    keep, send, merged_keep, merged_send, field_keep, field_send = block(
        half_rows,
        core,
        by_lon[:, HALF:],
        east,
        by_lat[:, HALF // 2 :].reshape(72, 2 * C),
        east_cotangent.reshape(72, 2 * C),
        norm_gain.reshape(1, C),
        qkv_weight,
        proj_weight,
        mlp_gain.reshape(1, C),
        up_weight,
        down_weight.T,
        merge_gain.reshape(4, C),
        merge_weight,
        bias,
        bias_tail,
        bias_index,
    )
    held, other = summed_over(keep, send, "lon")
    half = (12, HALF // 2, LEVELS, 2 * C)
    merged_west = passed_along(merged_send, "lon", 1)
    field_west = passed_along(field_send, "lon", 1)
    merged = jnp.concatenate([merged_west.reshape(half), merged_keep.reshape(half)], axis=1)
    field_grad = jnp.concatenate([field_west, field_keep], axis=1)
    factor = float(LEVELS * LAT * fields.shape[2] * count) ** (-0.5)
    qkv_grad, proj_grad, up_grad, down_grad, merge_grad, table_grad = finish(core, held, other, factor)
    return (
        merged.transpose(2, 0, 1, 3),
        field_grad.transpose(0, 2, 1, 3),
        qkv_grad,
        proj_grad,
        up_grad,
        down_grad.T,
        merge_grad,
        table_grad.transpose(1, 0, 2),
    )


def solution(mesh):
    whole = P("groups", None, "lon", None)
    return jax.shard_map(
        local,
        mesh=mesh,
        in_specs=(whole, *[P()] * 11, whole),
        out_specs=(whole, whole, *[P("groups", None)] * 5, P("groups", None, None)),
        check_vma=False,
    )
```

profile of v0, /device:TPU:168, one launch (start us, length us, event | category | flops | bytes accessed | tf_op | source)
XLA Modules:
  0.0 163.5 jit_solution(8891552996257691672)
XLA Ops:
  0.6 0.9 fusion.1
  1.6 1.5 collective-permute-start.1
  3.0 1.0 fusion
  4.0 0.7 collective-permute-start
  4.8 1.1 reshape.60.table_ref
  5.8 0.0 copy-start.4
  5.9 0.9 copy-done.4
  6.8 0.0 copy-start.6
  6.8 0.7 copy-done.6
  7.4 0.0 copy-start.13
  7.4 0.0 copy-start
  7.4 0.0 copy-start.1
  7.4 0.0 copy-start.2
  7.4 0.0 copy-start.3
  7.5 0.0 copy-start.5
  7.5 0.0 copy-start.7
  7.5 0.0 copy-start.8
  7.5 13.7 %bias_rows.1 = (f32[3456,128]{1,0:T(8,128)S(1)}, f32[3456,128]{1,0:T(8,128)S(1)}) custom-call(f32[24,3312]{1,0:T(8,128)S(1)} %reshape.60.table_ref, s32[144,144]{1,0:T(8,128)S(1)} %copy-done.4, s32[2,24]{1,0:T(2,128)S(1)} %copy-done.6), custom_call_target="tpu_custom_call" | custom-call | flops 14000000000 | bytes 4000000 | tf_op jit(solution)/shard_map/bias_rows/pallas_call | solution.py:200
  21.2 0.0 copy-start.9
  21.2 1.2 copy-done.9
  22.4 0.0 copy-start.11
  22.4 1.2 copy-done.11
  23.6 0.0 copy-done.13
  23.6 0.1 reshape.59.merge_gain_ref
  23.8 0.0 collective-permute-done.1
  23.8 0.0 collective-permute-done.east_ref
  23.8 0.0 copy-done
  23.8 0.0 copy-done.1
  23.8 0.0 copy-done.2
  23.8 0.0 copy-done.3
  23.8 0.0 copy-done.5
  23.9 0.0 copy-done.7
  23.9 0.0 copy-done.8
  23.9 0.0 copy-start.10
  23.9 1.5 copy-done.10
  25.4 0.0 copy-start.12
  25.4 1.5 copy-done.12
  26.8 27.4 %block.1 = (bf16[3584,128]{1,0:T(8,128)(2,1)S(1)}, bf16[3584,128]{1,0:T(8,128)(2,1)S(1)}, bf16[72,384]{1,0:T(8,128)(2,1)S(1)}, bf16[72,384]{1,0:T(8,128)(2,1)S(1...) custom-call(s32[1]{0:T(128)} %bitcast.core_ref.refs_0_, ...), custom_call_target="tpu_custom_call" | custom-call | flops 24000000000 | bytes 12000000 | tf_op jit(solution)/shard_map/block/pallas_call | solution.py:446
  54.2 0.1 collective-permute-start.4
  54.3 2.4 %collective-permute-done.4 = bf16[3584,128]{1,0:T(8,128)(2,1)S(1)} collective-permute-done((bf16[3584,128]{1,0:T(8,128)(2,1)S(1)}, bf16[3584,128]{1,0:T(8,128)(2,1)S(1)}, u32[]{:S(2)}, u32[]{:S(2)}) %collective-permute-start.4) | collective-permute-done | bytes 917536 | tf_op jit(solution)/shard_map/ppermute | solution.py:536
  56.8 0.2 add_convert_fusion
  57.0 17.1 %all_to_all.20 = bf16[4,896,128]{2,1,0:T(8,128)(2,1)S(1)} all-to-all(bf16[4,896,128]{2,1,0:T(8,128)(2,1)S(1)} %bitcast.22), channel_id=1, replica_groups={{0,2,4,6},{1,3,5,7},{8,10,12,14},{9,11,13,15},{16,18,20,22},{17,19,21,2..., dimensions={0} | all-to-all | bytes 1835008 | tf_op jit(solution)/shard_map/all_to_all | solution.py:539
  74.1 0.2 reduce_sum.24
  74.3 41.7 %all_to_all.21 = bf16[16,56,128]{2,1,0:T(8,128)(2,1)S(1)} all-to-all(bf16[16,56,128]{2,1,0:T(8,128)(2,1)S(1)} %bitcast.23), channel_id=1, replica_groups={{0,8,16,24,32,40,48,56,64,72,80,88,96,104,112,120},{1,9,17,25,33,41,49,..., dimensions={0} | all-to-all | bytes 458752 | tf_op jit(solution)/shard_map/all_to_all | solution.py:539
  116.1 21.7 %all_to_all.22 = bf16[16,56,128]{2,1,0:T(8,128)(2,1)S(1)} all-to-all(bf16[16,56,128]{2,1,0:T(8,128)(2,1)S(1)} %broadcast_in_dim.6), channel_id=1, replica_groups={{0,8,16,24,32,40,48,56,64,72,80,88,96,104,112,120},{1,9,17,25,33,41,49,..., dimensions={0} | all-to-all | bytes 458752 | tf_op jit(solution)/shard_map/all_to_all | solution.py:539
  137.8 0.1 broadcast_in_dim.15
  138.0 15.6 %all_to_all.23 = bf16[4,896,128]{2,1,0:T(8,128)(2,1)S(1)} all-to-all(bf16[4,896,128]{2,1,0:T(8,128)(2,1)S(1)} %broadcast_in_dim.15), channel_id=1, replica_groups={{0,2,4,6},{1,3,5,7},{8,10,12,14},{9,11,13,15},{16,18,20,22},{17,19,21,2..., dimensions={0} | all-to-all | bytes 1835008 | tf_op jit(solution)/shard_map/all_to_all | solution.py:539
  153.5 0.0 collective-permute-start.5
  153.5 0.5 collective-permute-start.2
  154.1 0.3 collective-permute-start.3
  154.4 4.9 %collective-permute-done.2 = bf16[72,384]{1,0:T(8,128)(2,1)S(1)} collective-permute-done((bf16[72,384]{1,0:T(8,128)(2,1)S(1)}, bf16[72,384]{1,0:T(8,128)(2,1)S(1)}, u32[]{:S(2)}, u32[]{:S(2)}) %collective-permute-start.2) | collective-permute-done | bytes 55328 | tf_op jit(solution)/shard_map/ppermute | solution.py:521
  159.3 0.8 maximum_bitcast_fusion.1
  160.1 0.8 collective-permute-done.3
  160.9 0.8 maximum_bitcast_fusion
  161.6 0.0 collective-permute-done.5.refs_2_
  161.6 1.9 %finish.1 = (f32[192,576]{1,0:T(8,128)}, f32[192,192]{1,0:T(8,128)}, f32[192,768]{1,0:T(8,128)}, f32[192,768]{1,0:T(8,128)}, f32[768,384]{1,0:T(8,128)}, /*index=5*/f32[6,4,3312]{2,1,0:T(4,128)}) custom-call(s32[1]{0:T(128)} %bitcast.core_ref.refs_0_, bf16[3584,128]{1,0:T(8,128)(2,1)S(1)} %bitcast.18, bf16[3584,128]{1,0:T(8,128)(2,1)S(1)} %collective-permute-done.5.refs_2_), custom_call_target="tpu_custom_call" | custom-call | tf_op jit(solution)/shard_map/finish/pallas_call | solution.py:501
  (6 shorter events, 0.2 us)
Async XLA Ops:
  1.6 22.2 %collective-permute-start.1 = (bf16[12,3,2,384]{3,2,1,0:T(2,128)(2,1)S(1)}, bf16[12,3,2,384]{3,2,1,0:T(2,128)(2,1)S(1)}, u32[]{:S(2)}, u32[]{:S(2)}) collective-permute-start(bf16[12,3,2,384]{3,2,1,0:T(2,128)(2,1)S(1)} %get-tuple-element.38), channel_id=1, source_target_pairs={{0,127},{1,0},{2,1},{3,2},{4,3},{5,4},{6,5},{7,6},{8,7},{9,8},{10,... | collective-permute-start | bytes 165896 | tf_op jit(solution)/shard_map/ppermute | solution.py:521
  4.0 19.8 %collective-permute-start = (bf16[2,6,24,192]{3,2,1,0:T(8,128)(2,1)S(1)}, bf16[2,6,24,192]{3,2,1,0:T(8,128)(2,1)S(1)}, u32[]{:S(2)}, u32[]{:S(2)}) collective-permute-start(bf16[2,6,24,192]{3,2,1,0:T(8,128)(2,1)S(1)} %get-tuple-element.36), channel_id=1, source_target_pairs={{0,127},{1,0},{2,1},{3,2},{4,3},{5,4},{6,5},{7,6},{8,7},{9,8},{10,... | collective-permute-start | bytes 331784 | tf_op jit(solution)/shard_map/ppermute | solution.py:521
  5.8 0.9 copy-start.4
  6.8 0.7 copy-start.6
  7.4 16.2 %copy-start.13 = (f32[768]{0:T(1024)S(1)}, f32[768]{0:T(1024)}, u32[]{:S(2)}) copy-start(f32[768]{0:T(1024)} %param.23) | copy-start | bytes 9220
  7.4 16.4 %copy-start = (bf16[768,384]{1,0:T(8,128)(2,1)S(1)}, bf16[768,384]{1,0:T(8,128)(2,1)}, u32[]{:S(2)}) copy-start(bf16[768,384]{1,0:T(8,128)(2,1)} %merge_ref.1) | copy-start | bytes 1769476
  7.4 16.4 %copy-start.1 = (bf16[192,768]{1,0:T(8,128)(2,1)S(1)}, bf16[192,768]{1,0:T(8,128)(2,1)}, u32[]{:S(2)}) copy-start(bf16[192,768]{1,0:T(8,128)(2,1)} %up_ref.1) | copy-start | bytes 884740
  7.4 16.4 %copy-start.2 = (bf16[768,192]{0,1:T(8,128)(2,1)S(1)}, bf16[768,192]{0,1:T(8,128)(2,1)}, u32[]{:S(2)}) copy-start(bf16[768,192]{0,1:T(8,128)(2,1)} %param.22) | copy-start | bytes 884740
  7.4 16.4 %copy-start.3 = (bf16[192,576]{1,0:T(8,128)(2,1)S(1)}, bf16[192,576]{1,0:T(8,128)(2,1)}, u32[]{:S(2)}) copy-start(bf16[192,576]{1,0:T(8,128)(2,1)} %qkv_ref.1) | copy-start | bytes 663556
  7.5 16.4 %copy-start.5 = (bf16[192,192]{1,0:T(8,128)(2,1)S(1)}, bf16[192,192]{1,0:T(8,128)(2,1)}, u32[]{:S(2)}) copy-start(bf16[192,192]{1,0:T(8,128)(2,1)} %proj_ref.1) | copy-start | bytes 221188
  7.5 16.4 %copy-start.7 = (f32[192]{0:T(256)S(1)}, f32[192]{0:T(256)}, u32[]{:S(2)}) copy-start(f32[192]{0:T(256)} %param.14) | copy-start | bytes 2308
  7.5 16.4 %copy-start.8 = (f32[192]{0:T(256)S(1)}, f32[192]{0:T(256)}, u32[]{:S(2)}) copy-start(f32[192]{0:T(256)} %param.20) | copy-start | bytes 2308
  21.2 1.3 copy-start.9
  22.4 1.2 copy-start.11
  23.9 1.5 copy-start.10
  25.4 1.5 copy-start.12
  54.2 2.6 %collective-permute-start.4 = (bf16[3584,128]{1,0:T(8,128)(2,1)S(1)}, bf16[3584,128]{1,0:T(8,128)(2,1)S(1)}, u32[]{:S(2)}, u32[]{:S(2)}) collective-permute-start(bf16[3584,128]{1,0:T(8,128)(2,1)S(1)} %get-tuple-element.29), channel_id=1, source_target_pairs={{0,1},{1,0},{2,3},{3,2},{4,5},{5,4},{6,7},{7,6},{8,9},{9,8},{10,11... | collective-permute-start | bytes 2752520 | tf_op jit(solution)/shard_map/ppermute | solution.py:536
  153.5 8.1 %collective-permute-start.5 = (bf16[3584,128]{1,0:T(8,128)(2,1)S(1)}, bf16[3584,128]{1,0:T(8,128)(2,1)S(1)}, u32[]{:S(2)}, u32[]{:S(2)}) collective-permute-start(bf16[3584,128]{1,0:T(8,128)(2,1)S(1)} %bitcast.17), channel_id=1, source_target_pairs={{0,1},{1,0},{2,3},{3,2},{4,5},{5,4},{6,7},{7,6},{8,9},{9,8},{10,11... | collective-permute-start | bytes 2752520 | tf_op jit(solution)/shard_map/ppermute | solution.py:552
  153.5 5.7 %collective-permute-start.2 = (bf16[72,384]{1,0:T(8,128)(2,1)S(1)}, bf16[72,384]{1,0:T(8,128)(2,1)S(1)}, u32[]{:S(2)}, u32[]{:S(2)}) collective-permute-start(bf16[72,384]{1,0:T(8,128)(2,1)S(1)} %get-tuple-element.24), channel_id=1, source_target_pairs={{0,1},{1,2},{2,3},{3,4},{4,5},{5,6},{6,7},{7,8},{8,9},{9,10},{10,1... | collective-permute-start | bytes 165896 | tf_op jit(solution)/shard_map/ppermute | solution.py:521
  154.1 6.8 %collective-permute-start.3 = (bf16[2,6,24,192]{3,2,1,0:T(8,128)(2,1)S(1)}, bf16[2,6,24,192]{3,2,1,0:T(8,128)(2,1)S(1)}, u32[]{:S(2)}, u32[]{:S(2)}) collective-permute-start(bf16[2,6,24,192]{3,2,1,0:T(8,128)(2,1)S(1)} %get-tuple-element.26), channel_id=1, source_target_pairs={{0,1},{1,2},{2,3},{3,4},{4,5},{5,6},{6,7},{7,8},{8,9},{9,10},{10,1... | collective-permute-start | bytes 331784 | tf_op jit(solution)/shard_map/ppermute | solution.py:521
where the time goes:
time: 164 us
  blocking collectives  96.1 us (59%)
  Pallas kernels  42.9 us (26%)
  local copies, waits for them, and re-layouts  10.4 us (6%)
  waiting for transfers between devices  8.12 us (5%)
  starting transfers between devices  3.15 us (2%)
  other arithmetic  2.06 us (1%)
    all_to_all x4, blocking collectives, exchanged(): lax.all_to_all(value, axis, 0, 0, axis_index_groups=groups_of(count, apar...  96.1 us
    pallas_call x1, Pallas kernels, block(): pl.pallas_call(block_kernel, out_shape=[shape((half_rows, LANES), BF), sh...  27.4 us
    pallas_call x1, Pallas kernels, bias_rows(): pl.pallas_call(bias_kernel, out_shape=[jax.ShapeDtypeStruct((TH * WIN, LA...  13.7 us
    unnamed x28, local copies, waits for them, and re-layouts  7.04 us
    ppermute x4, waiting for transfers between devices, passed_along(): lax.ppermute(value, axis, [(source, (source + steps) % count) for source...  5.67 us
  transfers between devices with their start and end apart: 6, of which 3 were waited for; matrix products, arithmetic and copies ran while one was open for 2% of the time, Pallas kernels for 8%

commit v1 on v0

--- a/solution.py
+++ b/solution.py
@@ -125,22 +125,38 @@
 
 
 def low_onehot(low):
-    return jnp.where(
-        lax.broadcasted_iota(jnp.int32, (LOW, low.shape[1]), 0) == low, 1.0, 0.0
-    ).astype(BF)
-
-
-def bias_kernel(table_ref, index_ref, region_ref, main_ref, tail_ref, part_ref, last_ref, turned_ref):
+    place = lax.broadcasted_iota(jnp.int32, (LOW, 1), 0).astype(F32).astype(BF)
+    hit = jnp.broadcast_to(place, (LOW, low.shape[1])) == low.astype(F32).astype(BF)
+    return jnp.where(hit, jnp.array(1, BF), jnp.array(0, BF))
+
+
+def bias_kernel(table_ref, index_ref, region_ref, main_ref, tail_ref, part_ref, last_ref, turned_ref, mask_ref):
     for high in range(HIGH):
         width = min(LOW, BPOS - high * LOW)
-        piece = table_ref[:, high * LOW : high * LOW + width]
-        if width < LOW:
-            piece = jnp.concatenate([piece, jnp.zeros((TH, LOW - width), F32)], axis=1)
-        leading = rounded(piece)
-        part_ref[high * TH : (high + 1) * TH, :LOW] = leading
-        part_ref[high * TH : (high + 1) * TH, LOW:] = piece - leading
+        for head in range(HEADS):
+            piece = table_ref[head, :, high * LOW : high * LOW + width]
+            if width < LOW:
+                piece = jnp.concatenate([piece, jnp.zeros((TYPES, LOW - width), F32)], axis=1)
+            leading = rounded(piece)
+            row = high * TH + head * TYPES
+            part_ref[row : row + TYPES, :LOW] = leading
+            part_ref[row : row + TYPES, LOW:] = piece - leading
     turned_ref[...] = jnp.transpose(index_ref[:, MAIN:])
     parts = part_ref[...].astype(BF)
+
+    kind_of = lax.broadcasted_iota(jnp.int32, (TH, 1), 0) & (TYPES - 1)
+    column = lax.broadcasted_iota(jnp.int32, (1, LANES), 1)
+    labels = []
+    for group in range(12):
+        label = jnp.zeros((TH, 1), jnp.int32)
+        for kind in range(TYPES):
+            label = jnp.where(kind_of == kind, region_ref[group // 6, 6 * kind + group % 6], label)
+        labels.append(label)
+    keys = jnp.zeros((TH, LANES), jnp.int32)
+    for group in range(11):
+        keys = jnp.where((column >= 12 * group) & (column < 12 * group + 12), labels[group], keys)
+    for group in range(12):
+        mask_ref[TH * group : TH * (group + 1), :] = jnp.where(keys == labels[group], 0.0, MASKED)
 
     def looked_up(index):
         low = low_onehot(index & (LOW - 1))
@@ -158,41 +174,31 @@
             index = jnp.concatenate([rows[4 * part + n : 4 * part + n + 1] for n in range(4)], axis=1)
             got = looked_up(index)
             for n in range(4):
-                main_ref[pl.ds(base + 4 * part + n, TH, stride=WIN), :] = got[:, n * MAIN : (n + 1) * MAIN]
+                row = base + 4 * part + n
+                mask = mask_ref[pl.ds(pl.multiple_of(div(row, 12) * TH, 8), TH), :]
+                main_ref[pl.ds(row, TH, stride=WIN), :] = got[:, n * MAIN : (n + 1) * MAIN] + mask
         return carry
 
-    lax.fori_loop(0, WIN // 8, row_block, 0)
-    blank = jnp.zeros((1, LOW - WIN), jnp.int32)
-    for key in range(0, REST, 2):
-        index = jnp.concatenate(
-            [turned_ref[key : key + 1, :], blank, turned_ref[key + 1 : key + 2, :], blank], axis=1
-        )
-        got = looked_up(index)
-        for n in range(2):
-            last_ref[pl.ds(key + n, TH, stride=REST), :] = got[:, 256 * n : 256 * n + 128]
-            last_ref[pl.ds(TH * REST + key + n, TH, stride=REST), :] = got[:, 256 * n + 128 : 256 * n + 256]
-    for kind in range(TYPES):
-        across = jnp.zeros((1, WIN), jnp.int32)
-        down = jnp.zeros((WIN, 1), jnp.int32)
-        column = lax.broadcasted_iota(jnp.int32, (1, WIN), 1)
-        row = lax.broadcasted_iota(jnp.int32, (WIN, 1), 0)
-        for group in range(12):
-            label = region_ref[group // 6, 6 * kind + group % 6]
-            across = jnp.where((column >= 12 * group) & (column < 12 * group + 12), label, across)
-            down = jnp.where((row >= 12 * group) & (row < 12 * group + 12), label, down)
-        same = down == across
-        for head in range(HEADS):
-            th = head * TYPES + kind
-            rows = slice(th * WIN, (th + 1) * WIN)
-            main_ref[rows, :] = jnp.where(same[:, :MAIN], main_ref[rows, :], MASKED)
-            tail = jnp.concatenate(
-                [
-                    jnp.transpose(last_ref[th * REST : (th + 1) * REST, :]),
-                    jnp.transpose(last_ref[(TH + th) * REST : (TH + th + 1) * REST, :REST]),
-                ],
-                axis=0,
-            )
-            tail_ref[rows, :REST] = jnp.where(same[:, MAIN:], tail, MASKED)
+    lax.fori_loop(0, WIN // 8, row_block, 0, unroll=6)
+    for start in range(0, REST, 4):
+        got = looked_up(jnp.concatenate([turned_ref[start + n : start + n + 1, :MAIN] for n in range(4)], axis=1))
+        for n in range(4):
+            group = (MAIN + start + n) // 12
+            mask = mask_ref[TH * group : TH * (group + 1), :]
+            last_ref[pl.ds(start + n, TH, stride=REST), :] = got[:, n * MAIN : (n + 1) * MAIN] + mask
+    got = looked_up(jnp.concatenate([turned_ref[n : n + 1, MAIN:] for n in range(REST)], axis=1))
+    apart = jnp.where(labels[10] == labels[11], 0.0, MASKED)
+    split = 132 - MAIN
+    for n in range(REST):
+        half = got[:, LANES * (n // 8) : LANES * (n // 8 + 1)]
+        half = half if n % 8 == 0 else pltpu.roll(half, LANES - REST * (n % 8), 1)
+        other = (column < split) if n >= split else (column >= split)
+        last_ref[pl.ds(TH * REST + n, TH, stride=REST), :] = half + jnp.where(other, apart, 0.0)
+    for th in range(TH):
+        rows = slice(th * WIN, th * WIN + MAIN)
+        tail_ref[rows, :REST] = jnp.transpose(last_ref[th * REST : (th + 1) * REST, :])
+        rows = slice(th * WIN + MAIN, (th + 1) * WIN)
+        tail_ref[rows, :REST] = jnp.transpose(last_ref[(TH + th) * REST : (TH + th + 1) * REST, :])[:REST]
 
 
 def bias_rows(table, index, regions):
@@ -206,6 +212,7 @@
             pltpu.VMEM((HIGH * TH, 2 * LOW), F32),
             pltpu.VMEM((2 * TH * REST, LANES), F32),
             pltpu.VMEM((REST, WIN), jnp.int32),
+            pltpu.VMEM((12 * TH, LANES), F32),
         ],
         compiler_params=pltpu.CompilerParams(vmem_limit_bytes=16 * 1024 * 1024),
         cost_estimate=pl.CostEstimate(flops=14_000_000_000, bytes_accessed=4_000_000, transcendentals=0),
@@ -221,13 +228,13 @@
     x_ref, unit_ref, scale_ref, tokens_ref, q_ref, k_ref, v_ref, p_ref, mixed_ref,
     unit_mlp_ref, scale_mlp_ref, normed_mlp_ref, hidden_ref, slope_ref, after_mlp_ref,
     group_ref, normed_merge_ref, grad_after_ref, grad_up_ref, grad_attn_ref, grad_mixed_ref,
-    ds_ref, ds_tail_ref, ds_corner_ref, dq_ref, dk_ref, dv_ref, grads_ref, turned_ref,
+    ds_ref, ds_tail_ref, ds_corner_ref, triple_ref, grads_ref, turned_ref, cells_ref,
 ):
     to_tokens = onehot(288, 288, of_row=cell_of_token)
     for level in range(LEVELS):
         cells = jnp.concatenate(
             [
-                own_ref[level].astype(F32).reshape(144, C),
+                own_ref[level, HALF:].astype(F32).reshape(144, C),
                 east_ref[level].astype(F32).reshape(144, C),
             ],
             axis=0,
@@ -253,15 +260,16 @@
         rows = pl.ds(pl.multiple_of(kind * WIN, 16), WIN)
         q, k, v = q_ref[rows, :], k_ref[rows, :], v_ref[rows, :]
         mixed = jnp.zeros((WIN, C), F32)
+        products = dot_nt(jnp.concatenate([q * of_head[h] for h in range(HEADS)], axis=0), k)
         for h in range(HEADS):
             th = h * TYPES + kind
             scores_at = pl.ds(pl.multiple_of(th * WIN, 16), WIN)
             bias = jnp.concatenate([bias_ref[scores_at, :], bias_tail_ref[scores_at, :REST]], axis=1)
-            scores = dot_nt(q * of_head[h], k) * temper + bias
+            scores = products[WIN * h : WIN * (h + 1)] * temper + bias
             weights = jnp.exp(scores - jnp.max(scores, axis=-1, keepdims=True))
-            p = (weights * (1.0 / jnp.sum(weights, axis=-1, keepdims=True))).astype(BF)
+            p = weights * (1.0 / jnp.sum(weights, axis=-1, keepdims=True))
             p_ref[th] = p
-            mixed = mixed + dot(p, v * of_head[h])
+            mixed = mixed + dot(p.astype(BF), v * of_head[h])
         mixed_ref[rows, :] = mixed.astype(BF)
         return carry
 
@@ -295,16 +303,21 @@
     for n in range(4):
         unit = centred[n] * scale_merge
         group_ref[n] = unit
-        normed_merge = (unit * merge_gain_ref[n : n + 1, :]).astype(BF)
+        normed_merge = (unit * merge_gain_ref[:, C * n : C * (n + 1)]).astype(BF)
         normed_merge_ref[n] = normed_merge
         merged = merged + dot(normed_merge, merge_ref[C * n : C * (n + 1), :])
-    merged_cells = dot(onehot(144, MTOK, of_col=cell_of_merged), merged.astype(BF)).astype(BF)
-    merged_keep_ref[...] = merged_cells[:72]
-    merged_send_ref[...] = merged_cells[72:]
-    cotangent = jnp.concatenate(
-        [own_cotangent_ref[...].astype(F32), east_cotangent_ref[...].astype(F32)], axis=0
-    ).astype(BF)
-    grad_merged = dot(onehot(MTOK, 144, of_row=cell_of_merged), cotangent).astype(BF)
+    merged_cells = dot(onehot(144, MTOK, of_col=cell_of_merged), merged.astype(BF))
+    for lat in range(12):
+        for lon in range(HALF // 2):
+            row = (lat * 3 + lon) * 2
+            merged_keep_ref[lat, lon] = merged_cells[row : row + 2].astype(BF)
+            merged_send_ref[lat, lon] = merged_cells[72 + row : 74 + row].astype(BF)
+    for lat in range(12):
+        for lon in range(HALF // 2):
+            row = (lat * 3 + lon) * 2
+            cells_ref[row : row + 2, :] = own_cotangent_ref[lat, 3 + lon].astype(F32)
+            cells_ref[72 + row : 74 + row, :] = east_cotangent_ref[lat, lon].astype(F32)
+    grad_merged = dot(onehot(MTOK, 144, of_row=cell_of_merged), cells_ref[...].astype(BF)).astype(BF)
 
     scaled, total, along = [], 0.0, 0.0
     for n in range(4):
@@ -312,7 +325,7 @@
         for b in range(3):
             start = O_MERGE + MLP * b + C * n
             grads_ref[start : start + C, :] = grad[:, 128 * b : 128 * b + 128]
-        value = rounded(dot_nt(grad_merged, merge_ref[C * n : C * (n + 1), :])) * merge_gain_ref[n : n + 1, :]
+        value = rounded(dot_nt(grad_merged, merge_ref[C * n : C * (n + 1), :])) * merge_gain_ref[:, C * n : C * (n + 1)]
         total = total + jnp.sum(value, axis=-1, keepdims=True)
         along = along + jnp.sum(value * group_ref[n], axis=-1, keepdims=True)
         scaled.append(value)
@@ -349,37 +362,35 @@
     grad_mixed_ref[...] = dot_nt(grad_attn, proj_ref[...]).astype(BF)
     ds_corner_ref[...] = jnp.zeros(ds_corner_ref.shape, F32)
 
+    last_keys = onehot(REST, WIN, of_row=lambda n: n + MAIN)
+
     def attend_back(kind, carry):
         rows = pl.ds(pl.multiple_of(kind * WIN, 16), WIN)
-        q, k, v, grad = q_ref[rows, :], k_ref[rows, :], v_ref[rows, :], grad_mixed_ref[rows, :]
-        dq = jnp.zeros((WIN, C), F32)
-        dk = jnp.zeros((WIN, C), F32)
-        dv = jnp.zeros((WIN, C), F32)
+        v, grad = v_ref[rows, :], grad_mixed_ref[rows, :]
+        q_turned, k_turned, grad_turned = (jnp.transpose(a) for a in (q_ref[rows, :], k_ref[rows, :], grad))
+        products = dot_nt(jnp.concatenate([grad * of_head[h] for h in range(HEADS)], axis=0), v)
+        dq, dk, dv = [], [], []
         for h in range(HEADS):
             th = h * TYPES + kind
-            grad_head = grad * of_head[h]
+            lanes = slice(HEAD * h, HEAD * (h + 1))
             p = p_ref[th]
-            wide = p.astype(F32)
-            dp = rounded(dot_nt(grad_head, v))
-            ds = wide * (dp - jnp.sum(wide * dp, axis=-1, keepdims=True))
+            weighted = p * products[WIN * h : WIN * (h + 1)]
+            ds = weighted - p * jnp.sum(weighted, axis=-1, keepdims=True)
             ds_ref[pl.ds(pl.multiple_of(th * WIN, 16), WIN), :] = ds[:, :MAIN]
-            turned = jnp.transpose(
-                jnp.concatenate([ds[:, MAIN:], jnp.zeros((WIN, LANES - REST), F32)], axis=1)
-            )
+            ds = ds.astype(BF)
+            turned = dot_nt(jnp.concatenate([k_turned[lanes], last_keys], axis=0), ds)
             at = pl.ds(pl.multiple_of(th * REST, 16), REST)
-            ds_tail_ref[at, :] = turned[:REST, :MAIN]
-            ds_corner_ref[at, :REST] = turned[:REST, MAIN:]
-            grad_scores = (ds * temper).astype(BF)
-            dv = dv + dot_tn(p, grad_head)
-            dk = dk + dot_tn(grad_scores, q * of_head[h])
-            dq = dq + dot(grad_scores, k * of_head[h])
-        dq_ref[rows, :] = dq.astype(BF)
-        dk_ref[rows, :] = dk.astype(BF)
-        dv_ref[rows, :] = dv.astype(BF)
+            ds_tail_ref[at, :] = turned[HEAD:, :MAIN]
+            ds_corner_ref[at, :REST] = turned[HEAD:, MAIN:]
+            dq.append(turned[:HEAD])
+            dk.append(dot(q_turned[lanes], ds))
+            dv.append(dot(grad_turned[lanes], p.astype(BF)))
+        triple = jnp.concatenate([a * temper for a in dq + dk] + dv, axis=0).astype(BF)
+        triple_ref[rows, :] = jnp.transpose(triple)
         return carry
 
     lax.fori_loop(0, TYPES, attend_back, 0)
-    grad_triple = jnp.concatenate([dq_ref[...], dk_ref[...], dv_ref[...]], axis=1)
+    grad_triple = triple_ref[...]
     grad_qkv = dot_tn(tokens_ref[...], grad_triple).astype(BF)
     for b in range(4):
         grads_ref[O_QKV + C * b : O_QKV + C * (b + 1), :] = grad_qkv[:, 128 * b : 128 * b + 128]
@@ -414,7 +425,7 @@
         slab = jnp.concatenate([ds_ref[pl.ds(base + n, TH, stride=WIN), :] for n in range(8)], axis=1)
         return carry + table_terms(index, slab)
 
-    table = lax.fori_loop(0, WIN // 8, row_block, jnp.zeros((TROWS, LOW), F32))
+    table = lax.fori_loop(0, WIN // 8, row_block, jnp.zeros((TROWS, LOW), F32), unroll=6)
     blank = jnp.zeros((1, LOW - WIN), jnp.int32)
     for key in range(0, REST, 4):
         index, slab = [], []
@@ -437,26 +448,27 @@
     whole = pl.BlockSpec(memory_space=pltpu.VMEM)
     scratch = [
         ((TOK, C), F32), ((TOK, C), F32), ((TOK, 1), F32), ((TOK, C), BF), ((TOK, C), BF), ((TOK, C), BF),
-        ((TOK, C), BF), ((TH, WIN, WIN), BF), ((TOK, C), BF),
+        ((TOK, C), BF), ((TH, WIN, WIN), F32), ((TOK, C), BF),
         ((TOK, C), F32), ((TOK, 1), F32), ((TOK, C), BF), ((TOK, MLP), BF), ((TOK, MLP), F32), ((TOK, C), BF),
         ((4, MTOK, C), F32), ((4, MTOK, C), BF), ((TOK, C), BF), ((TOK, MLP), BF), ((TOK, C), BF), ((TOK, C), BF),
         ((TH * WIN, LANES), F32), ((TH * REST, LANES), F32), ((TH * REST, LANES), F32),
-        ((TOK, C), BF), ((TOK, C), BF), ((TOK, C), BF), ((2 * half_rows, LANES), BF), ((REST, WIN), jnp.int32),
+        ((TOK, 3 * C), BF), ((2 * half_rows, LANES), BF), ((REST, WIN), jnp.int32),
+        ((144, 2 * C), F32),
     ]
     return pl.pallas_call(
         block_kernel,
         out_shape=[
             shape((half_rows, LANES), BF),
             shape((half_rows, LANES), BF),
-            shape((72, 2 * C), BF),
-            shape((72, 2 * C), BF),
+            shape((12, HALF // 2, LEVELS, 2 * C), BF),
+            shape((12, HALF // 2, LEVELS, 2 * C), BF),
             shape((LEVELS, HALF, LAT, C), BF),
             shape((LEVELS, HALF, LAT, C), BF),
         ],
         in_specs=[pl.BlockSpec(memory_space=pltpu.SMEM)] + [whole] * (len(args) - 1),
         out_specs=[whole] * 6,
         scratch_shapes=[pltpu.VMEM(*item) for item in scratch],
-        compiler_params=pltpu.CompilerParams(vmem_limit_bytes=40 * 1024 * 1024),
+        compiler_params=pltpu.CompilerParams(vmem_limit_bytes=24 * 1024 * 1024),
         cost_estimate=pl.CostEstimate(flops=24_000_000_000, bytes_accessed=12_000_000, transcendentals=2_000_000),
         name="block",
     )(*args)
@@ -529,7 +541,7 @@
     ]
 
 
-def summed_over(keep, send, axis):
+def summed_over(keep, send, axis, others):
     count = lax.axis_size(axis)
     along = count // (CORES * ACROSS)
     pairs = [(i, i ^ 1) for i in range(count)]
@@ -546,10 +558,11 @@
         return exchanged(jnp.broadcast_to(value[None], (size, *value.shape)), apart, size).reshape(-1, LANES)
 
     held = reduced(held, CORES, ACROSS)
+    held, *others = lax.optimization_barrier((held, *others))
     held = reduced(held, CORES * ACROSS, along)
     held = gathered(held, CORES * ACROSS, along)
     held = gathered(held, CORES, ACROSS)
-    return held, lax.ppermute(held, axis, pairs)
+    return held, lax.ppermute(held, axis, pairs), others
 
 
 def local(
@@ -573,32 +586,34 @@
     by_lat = cotangent.transpose(1, 2, 0, 3)
     east = passed_along(by_lon[:, :HALF], "lon", -1)
     east_cotangent = passed_along(by_lat[:, : HALF // 2], "lon", -1)
-    bias, bias_tail = bias_rows(bias_table.transpose(1, 0, 2).reshape(TH, BPOS), bias_index, region_ids)
+    table, core, merge_gain = lax.optimization_barrier(
+        (bias_table.transpose(1, 0, 2), core, merge_gain.reshape(1, 4 * C))
+    )
+    bias, bias_tail = bias_rows(table, bias_index, region_ids)
     half_rows = -(-O_END // (count * 8)) * 8 * count // CORES
     keep, send, merged_keep, merged_send, field_keep, field_send = block(
         half_rows,
         core,
-        by_lon[:, HALF:],
+        by_lon,
         east,
-        by_lat[:, HALF // 2 :].reshape(72, 2 * C),
-        east_cotangent.reshape(72, 2 * C),
+        by_lat,
+        east_cotangent,
         norm_gain.reshape(1, C),
         qkv_weight,
         proj_weight,
         mlp_gain.reshape(1, C),
         up_weight,
         down_weight.T,
-        merge_gain.reshape(4, C),
+        merge_gain,
         merge_weight,
         bias,
         bias_tail,
         bias_index,
     )
-    held, other = summed_over(keep, send, "lon")
-    half = (12, HALF // 2, LEVELS, 2 * C)
     merged_west = passed_along(merged_send, "lon", 1)
     field_west = passed_along(field_send, "lon", 1)
-    merged = jnp.concatenate([merged_west.reshape(half), merged_keep.reshape(half)], axis=1)
+    held, other, (merged_west, field_west) = summed_over(keep, send, "lon", (merged_west, field_west))
+    merged = jnp.concatenate([merged_west, merged_keep], axis=1)
     field_grad = jnp.concatenate([field_west, field_keep], axis=1)
     factor = float(LEVELS * LAT * fields.shape[2] * count) ** (-0.5)
     qkv_grad, proj_grad, up_grad, down_grad, merge_grad, table_grad = finish(core, held, other, factor)

time: 164 us -> 145 us (0.88)
  blocking collectives: 96.1 us -> 67.8 us
  waiting for transfers between devices: 8.12 us -> 29 us
  Pallas kernels: 42.9 us -> 30.3 us
  local copies, waits for them, and re-layouts: 10.4 us -> 5.23 us
  starting transfers between devices: 3.15 us -> 7.96 us
    all_to_all x4 -> x3, blocking collectives: 96.1 us -> 67.8 us  [exchanged(): lax.all_to_all(value, axis, 0, 0, axis_index_groups=groups_of(count, apar...]
    all_to_all x0 -> x1, waiting for transfers between devices: none -> 13 us  [exchanged(): lax.all_to_all(value, axis, 0, 0, axis_index_groups=groups_of(count, apar...]
    pallas_call x1, Pallas kernels: 27.4 us -> 19.1 us  [block(): pl.pallas_call(block_kernel, out_shape=[shape((half_rows, LANES), BF), sh...]
    ppermute x4, waiting for transfers between devices: 5.67 us -> 12.6 us  [passed_along(): lax.ppermute(value, axis, [(source, (source + steps) % count) for source...]
    unnamed x28 -> x26, local copies, waits for them, and re-layouts: 7.04 us -> 2.61 us
    pallas_call x1, Pallas kernels: 13.7 us -> 9.25 us  [bias_rows(): pl.pallas_call(bias_kernel, out_shape=[jax.ShapeDtypeStruct((TH * WIN, LA...]
    all_to_all x0 -> x1, starting transfers between devices: none -> 3.6 us  [exchanged(): lax.all_to_all(value, axis, 0, 0, axis_index_groups=groups_of(count, apar...]
  transfers between devices with their start and end apart: 6 -> 7, of which waited for: 3 -> 4; matrix products, arithmetic and copies ran while one was open for 2% -> 2% of each run, Pallas kernels for 8% -> 6%
where the time goes in v1:
time: 145 us; the launch traced here: 144 us
  blocking collectives  67.8 us (47%)
  Pallas kernels  30.3 us (21%)
  waiting for transfers between devices  29 us (20%)
  starting transfers between devices  7.96 us (5%)
  local copies, waits for them, and re-layouts  5.23 us (4%)
  other arithmetic  2.98 us (2%)
    all_to_all x3, blocking collectives, exchanged(): lax.all_to_all(value, axis, 0, 0, axis_index_groups=groups_of(count, apar...  67.8 us
    pallas_call x1, Pallas kernels, block(): pl.pallas_call(block_kernel, out_shape=[shape((half_rows, LANES), BF), sh...  19.1 us
    all_to_all x1, waiting for transfers between devices, exchanged(): lax.all_to_all(value, axis, 0, 0, axis_index_groups=groups_of(count, apar...  13 us
    ppermute x4, waiting for transfers between devices, passed_along(): lax.ppermute(value, axis, [(source, (source + steps) % count) for source...  12.6 us
    pallas_call x1, Pallas kernels, bias_rows(): pl.pallas_call(bias_kernel, out_shape=[jax.ShapeDtypeStruct((TH * WIN, LA...  9.25 us
    ppermute x4, starting transfers between devices, passed_along(): lax.ppermute(value, axis, [(source, (source + steps) % count) for source...  4.22 us
    all_to_all x1, starting transfers between devices, exchanged(): lax.all_to_all(value, axis, 0, 0, axis_index_groups=groups_of(count, apar...  3.6 us
  transfers between devices with their start and end apart: 7, of which 4 were waited for; matrix products, arithmetic and copies ran while one was open for 2% of the time, Pallas kernels for 6%

profile of v1, /device:TPU:168, one launch (start us, length us, event | category | flops | bytes accessed | tf_op | source)
XLA Modules:
  0.0 144.1 jit_solution(15727149709120660714)
XLA Ops:
  0.6 0.9 slice.9
  1.5 1.5 %collective-permute-start.1 = (bf16[12,3,2,384]{3,2,1,0:T(2,128)(2,1)S(1)}, bf16[12,3,2,384]{3,2,1,0:T(2,128)(2,1)S(1)}, u32[]{:S(2)}, u32[]{:S(2)}) collective-permute-start(bf16[12,3,2,384]{3,2,1,0:T(2,128)(2,1)S(1)} %slice.9), channel_id=1, source_target_pairs={{0,127},{1,0},{2,1},{3,2},{4,3},{5,4},{6,5},{7,6},{8,7},{9,8},{10,... | collective-permute-start | bytes 165896 | tf_op jit(solution)/shard_map/ppermute | solution.py:533
  3.0 0.9 slice.8
  3.9 0.7 collective-permute-start
  4.6 0.7 reshape.40.merge_gain_ref
  5.3 0.0 copy-start.3
  5.3 1.0 copy-done.3
  6.3 0.0 copy-start.7
  6.3 0.9 copy-done.7
  7.2 0.0 copy-start.10
  7.2 0.7 copy-done.10
  7.9 0.0 copy-start
  7.9 0.0 copy-start.1
  7.9 0.0 copy-start.2
  7.9 0.0 copy-start.4
  7.9 0.0 copy-start.5
  7.9 0.0 copy-start.6
  7.9 0.0 copy-start.8
  7.9 0.0 copy-start.9
  7.9 0.0 copy-start.11
  7.9 0.0 copy-start.12
  7.9 9.2 %bias_rows.1 = (f32[3456,128]{1,0:T(8,128)S(1)}, f32[3456,128]{1,0:T(8,128)S(1)}) custom-call(f32[6,4,3312]{2,1,0:T(4,128)S(1)} %bitcast.23, s32[144,144]{1,0:T(8,128)S(1)} %copy-done.7, s32[2,24]{1,0:T(2,128)S(1)} %copy-done.10), custom_call_target="tpu_custom_call" | custom-call | flops 14000000000 | bytes 4000000 | tf_op jit(solution)/shard_map/bias_rows/pallas_call | solution.py:206
  17.2 0.0 collective-permute-done.1.east_cotangent_ref
  17.2 0.0 collective-permute-done.east_ref
  17.2 0.0 copy-done
  17.2 0.0 copy-done.1
  17.2 0.0 copy-done.2
  17.2 0.0 copy-done.4
  17.3 0.0 copy-done.5
  17.3 0.0 copy-done.6
  17.3 0.0 copy-done.8
  17.3 0.0 copy-done.9
  17.3 0.0 copy-done.11
  17.3 0.0 copy-done.12
  17.3 19.1 %block.1 = (bf16[3584,128]{1,0:T(8,128)(2,1)S(1)}, bf16[3584,128]{1,0:T(8,128)(2,1)S(1)}, bf16[12,3,2,384]{3,2,1,0:T(2,128)(2,1)S(1)}, bf16[12,3,2,384]{3,2,1,0:...) custom-call(s32[1]{0:T(128)} %bitcast.1.core_ref.refs_0_, ...), custom_call_target="tpu_custom_call" | custom-call | flops 24000000000 | bytes 12000000 | tf_op jit(solution)/shard_map/block/pallas_call | solution.py:458
  36.4 0.1 collective-permute-start.2
  36.6 2.4 %collective-permute-done.2 = bf16[3584,128]{1,0:T(8,128)(2,1)S(1)} collective-permute-done((bf16[3584,128]{1,0:T(8,128)(2,1)S(1)}, bf16[3584,128]{1,0:T(8,128)(2,1)S(1)}, u32[]{:S(2)}, u32[]{:S(2)}) %collective-permute-start.2) | collective-permute-done | bytes 917536 | tf_op jit(solution)/shard_map/ppermute | solution.py:548
  39.0 1.2 add_convert_fusion
  40.2 3.6 %all-to-all-start = ((bf16[4,896,128]{2,1,0:T(8,128)(2,1)}), bf16[4,896,128]{2,1,0:T(8,128)(2,1)S(1)}, u32[]{:S(2)}, u32[]{:S(2)}) async-start(bf16[4,896,128]{2,1,0:T(8,128)(2,1)} %bitcast.7), calls=%async_computation | async-start | bytes 1835008 | tf_op jit(solution)/shard_map/all_to_all | solution.py:551
  43.8 0.2 collective-permute-start.4
  44.1 1.8 %collective-permute-start.3 = (bf16[12,3,2,384]{3,2,1,0:T(2,128)(2,1)S(1)}, bf16[12,3,2,384]{3,2,1,0:T(2,128)(2,1)S(1)}, u32[]{:S(2)}, u32[]{:S(2)}) collective-permute-start(bf16[12,3,2,384]{3,2,1,0:T(2,128)(2,1)S(1)} %get-tuple-element.35), channel_id=1, source_target_pairs={{0,1},{1,2},{2,3},{3,4},{4,5},{5,6},{6,7},{7,8},{8,9},{9,10},{10,1... | collective-permute-start | bytes 165896 | tf_op jit(solution)/shard_map/ppermute | solution.py:533
  45.8 13.0 %all-to-all-done = bf16[4,896,128]{2,1,0:T(8,128)(2,1)S(1)} async-done(((bf16[4,896,128]{2,1,0:T(8,128)(2,1)}), bf16[4,896,128]{2,1,0:T(8,128)(2,1)S(1)}, u32[]{:S(2)}, u32[]{:S(2)}) %all-to-all-start) | async-done | bytes 917536 | tf_op jit(solution)/shard_map/all_to_all | solution.py:551
  58.8 0.2 reduce_sum.24
  59.0 12.6 %collective-permute-done.3 = bf16[12,3,2,384]{3,2,1,0:T(2,128)(2,1)S(1)} collective-permute-done((bf16[12,3,2,384]{3,2,1,0:T(2,128)(2,1)S(1)}, bf16[12,3,2,384]{3,2,1,0:T(2,128)(2,1)S(1)}, u32[]{:S(2)}, u32[]{:S(2)}) %collective-permute-start.3) | collective-permute-done | bytes 55328 | tf_op jit(solution)/shard_map/ppermute | solution.py:533
  71.6 0.0 collective-permute-done.4
  71.7 30.5 %all_to_all.20 = bf16[16,56,128]{2,1,0:T(8,128)(2,1)S(1)} all-to-all(bf16[16,56,128]{2,1,0:T(8,128)(2,1)S(1)} %bitcast.27), channel_id=1, replica_groups={{0,8,16,24,32,40,48,56,64,72,80,88,96,104,112,120},{1,9,17,25,33,41,49,..., dimensions={0} | all-to-all | bytes 458752 | tf_op jit(solution)/shard_map/all_to_all | solution.py:551
  102.2 21.7 %all_to_all.21 = bf16[16,56,128]{2,1,0:T(8,128)(2,1)S(1)} all-to-all(bf16[16,56,128]{2,1,0:T(8,128)(2,1)S(1)} %broadcast_in_dim.6), channel_id=1, replica_groups={{0,8,16,24,32,40,48,56,64,72,80,88,96,104,112,120},{1,9,17,25,33,41,49,..., dimensions={0} | all-to-all | bytes 458752 | tf_op jit(solution)/shard_map/all_to_all | solution.py:551
  124.0 0.1 broadcast_in_dim.15
  124.1 15.6 %all_to_all.22 = bf16[4,896,128]{2,1,0:T(8,128)(2,1)S(1)} all-to-all(bf16[4,896,128]{2,1,0:T(8,128)(2,1)S(1)} %broadcast_in_dim.15), channel_id=1, replica_groups={{0,2,4,6},{1,3,5,7},{8,10,12,14},{9,11,13,15},{16,18,20,22},{17,19,21,2..., dimensions={0} | all-to-all | bytes 1835008 | tf_op jit(solution)/shard_map/all_to_all | solution.py:551
  139.7 0.0 collective-permute-start.5
  139.7 0.8 maximum_bitcast_fusion.1
  140.5 0.8 maximum_bitcast_fusion
  141.2 0.9 collective-permute-done.5.refs_2_
  142.1 1.9 %finish.1 = (f32[192,576]{1,0:T(8,128)}, f32[192,192]{1,0:T(8,128)}, f32[192,768]{1,0:T(8,128)}, f32[192,768]{1,0:T(8,128)}, f32[768,384]{1,0:T(8,128)}, /*index=5*/f32[6,4,3312]{2,1,0:T(4,128)}) custom-call(s32[1]{0:T(128)} %bitcast.1.core_ref.refs_0_, bf16[3584,128]{1,0:T(8,128)(2,1)S(1)} %bitcast.18, bf16[3584,128]{1,0:T(8,128)(2,1)S(1)} %collective-permute-done.5.refs_2_), custom_call_target="tpu_custom_call" | custom-call | tf_op jit(solution)/shard_map/finish/pallas_call | solution.py:513
  (2 shorter events, 0.1 us)
Async XLA Ops:
  1.5 15.7 %collective-permute-start.1 = (bf16[12,3,2,384]{3,2,1,0:T(2,128)(2,1)S(1)}, bf16[12,3,2,384]{3,2,1,0:T(2,128)(2,1)S(1)}, u32[]{:S(2)}, u32[]{:S(2)}) collective-permute-start(bf16[12,3,2,384]{3,2,1,0:T(2,128)(2,1)S(1)} %slice.9), channel_id=1, source_target_pairs={{0,127},{1,0},{2,1},{3,2},{4,3},{5,4},{6,5},{7,6},{8,7},{9,8},{10,... | collective-permute-start | bytes 165896 | tf_op jit(solution)/shard_map/ppermute | solution.py:533
  3.9 13.3 %collective-permute-start = (bf16[2,6,24,192]{3,2,1,0:T(8,128)(2,1)S(1)}, bf16[2,6,24,192]{3,2,1,0:T(8,128)(2,1)S(1)}, u32[]{:S(2)}, u32[]{:S(2)}) collective-permute-start(bf16[2,6,24,192]{3,2,1,0:T(8,128)(2,1)S(1)} %slice.8), channel_id=1, source_target_pairs={{0,127},{1,0},{2,1},{3,2},{4,3},{5,4},{6,5},{7,6},{8,7},{9,8},{10,... | collective-permute-start | bytes 331784 | tf_op jit(solution)/shard_map/ppermute | solution.py:533
  5.3 1.0 copy-start.3
  6.3 0.9 copy-start.7
  7.2 0.7 copy-start.10
  7.9 9.4 %copy-start = (bf16[2,24,12,192]{3,1,2,0:T(8,128)(2,1)S(1)}, bf16[2,24,12,192]{3,1,2,0:T(8,128)(2,1)}, u32[]{:S(2)}) copy-start(bf16[2,24,12,192]{3,1,2,0:T(8,128)(2,1)} %param.13) | copy-start | bytes 663556
  7.9 9.4 %copy-start.1 = (bf16[2,12,6,384]{3,0,2,1:T(2,128)(2,1)S(1)}, bf16[2,12,6,384]{3,0,2,1:T(2,128)(2,1)}, u32[]{:S(2)}) copy-start(bf16[2,12,6,384]{3,0,2,1:T(2,128)(2,1)} %param.25) | copy-start | bytes 331780
  7.9 9.4 %copy-start.2 = (bf16[768,384]{1,0:T(8,128)(2,1)S(1)}, bf16[768,384]{1,0:T(8,128)(2,1)}, u32[]{:S(2)}) copy-start(bf16[768,384]{1,0:T(8,128)(2,1)} %merge_ref.1) | copy-start | bytes 1769476
  7.9 9.4 %copy-start.4 = (bf16[192,768]{1,0:T(8,128)(2,1)S(1)}, bf16[192,768]{1,0:T(8,128)(2,1)}, u32[]{:S(2)}) copy-start(bf16[192,768]{1,0:T(8,128)(2,1)} %up_ref.1) | copy-start | bytes 884740
  7.9 9.4 %copy-start.5 = (bf16[768,192]{0,1:T(8,128)(2,1)S(1)}, bf16[768,192]{0,1:T(8,128)(2,1)}, u32[]{:S(2)}) copy-start(bf16[768,192]{0,1:T(8,128)(2,1)} %param.22) | copy-start | bytes 884740
  7.9 9.4 %copy-start.6 = (bf16[192,576]{1,0:T(8,128)(2,1)S(1)}, bf16[192,576]{1,0:T(8,128)(2,1)}, u32[]{:S(2)}) copy-start(bf16[192,576]{1,0:T(8,128)(2,1)} %qkv_ref.1) | copy-start | bytes 663556
  7.9 9.4 %copy-start.8 = (s32[144,144]{1,0:T(8,128)S(1)}, s32[144,144]{1,0:T(8,128)}, u32[]{:S(2)}) copy-start(s32[144,144]{1,0:T(8,128)} %index_ref.3) | copy-start | bytes 248836
  7.9 9.4 %copy-start.9 = (bf16[192,192]{1,0:T(8,128)(2,1)S(1)}, bf16[192,192]{1,0:T(8,128)(2,1)}, u32[]{:S(2)}) copy-start(bf16[192,192]{1,0:T(8,128)(2,1)} %proj_ref.1) | copy-start | bytes 221188
  7.9 9.4 %copy-start.11 = (f32[192]{0:T(256)S(1)}, f32[192]{0:T(256)}, u32[]{:S(2)}) copy-start(f32[192]{0:T(256)} %param.14) | copy-start | bytes 2308
  7.9 9.4 %copy-start.12 = (f32[192]{0:T(256)S(1)}, f32[192]{0:T(256)}, u32[]{:S(2)}) copy-start(f32[192]{0:T(256)} %param.20) | copy-start | bytes 2308
  36.4 2.6 %collective-permute-start.2 = (bf16[3584,128]{1,0:T(8,128)(2,1)S(1)}, bf16[3584,128]{1,0:T(8,128)(2,1)S(1)}, u32[]{:S(2)}, u32[]{:S(2)}) collective-permute-start(bf16[3584,128]{1,0:T(8,128)(2,1)S(1)} %get-tuple-element.34), channel_id=1, source_target_pairs={{0,1},{1,0},{2,3},{3,2},{4,5},{5,4},{6,7},{7,6},{8,9},{9,8},{10,11... | collective-permute-start | bytes 2752520 | tf_op jit(solution)/shard_map/ppermute | solution.py:548
  40.2 18.6 %all-to-all-start = ((bf16[4,896,128]{2,1,0:T(8,128)(2,1)}), bf16[4,896,128]{2,1,0:T(8,128)(2,1)S(1)}, u32[]{:S(2)}, u32[]{:S(2)}) async-start(bf16[4,896,128]{2,1,0:T(8,128)(2,1)} %bitcast.7), calls=%async_computation | async-start | bytes 1835008 | tf_op jit(solution)/shard_map/all_to_all | solution.py:551
  43.8 27.9 %collective-permute-start.4 = (bf16[2,6,24,192]{3,2,1,0:T(8,128)(2,1)S(1)}, bf16[2,6,24,192]{3,2,1,0:T(8,128)(2,1)S(1)}, u32[]{:S(2)}, u32[]{:S(2)}) collective-permute-start(bf16[2,6,24,192]{3,2,1,0:T(8,128)(2,1)S(1)} %get-tuple-element.36), channel_id=1, source_target_pairs={{0,1},{1,2},{2,3},{3,4},{4,5},{5,6},{6,7},{7,8},{8,9},{9,10},{10,1... | collective-permute-start | bytes 331784 | tf_op jit(solution)/shard_map/ppermute | solution.py:533
  44.1 27.6 %collective-permute-start.3 = (bf16[12,3,2,384]{3,2,1,0:T(2,128)(2,1)S(1)}, bf16[12,3,2,384]{3,2,1,0:T(2,128)(2,1)S(1)}, u32[]{:S(2)}, u32[]{:S(2)}) collective-permute-start(bf16[12,3,2,384]{3,2,1,0:T(2,128)(2,1)S(1)} %get-tuple-element.35), channel_id=1, source_target_pairs={{0,1},{1,2},{2,3},{3,4},{4,5},{5,6},{6,7},{7,8},{8,9},{9,10},{10,1... | collective-permute-start | bytes 165896 | tf_op jit(solution)/shard_map/ppermute | solution.py:533
  139.7 2.5 %collective-permute-start.5 = (bf16[3584,128]{1,0:T(8,128)(2,1)S(1)}, bf16[3584,128]{1,0:T(8,128)(2,1)S(1)}, u32[]{:S(2)}, u32[]{:S(2)}) collective-permute-start(bf16[3584,128]{1,0:T(8,128)(2,1)S(1)} %bitcast.17), channel_id=1, source_target_pairs={{0,1},{1,0},{2,3},{3,2},{4,5},{5,4},{6,7},{7,6},{8,9},{9,8},{10,11... | collective-permute-start | bytes 2752520 | tf_op jit(solution)/shard_map/ppermute | solution.py:565

commit v2 on v1

--- a/solution.py
+++ b/solution.py
@@ -130,7 +130,9 @@
     return jnp.where(hit, jnp.array(1, BF), jnp.array(0, BF))
 
 
-def bias_kernel(table_ref, index_ref, region_ref, main_ref, tail_ref, part_ref, last_ref, turned_ref, mask_ref):
+def bias_kernel(table_ref, index_ref, regions_ref, main_ref, tail_ref, part_ref, last_ref, turned_ref, mask_ref, region_ref, sem):
+    copy = pltpu.make_async_copy(regions_ref, region_ref, sem)
+    copy.start()
     for high in range(HIGH):
         width = min(LOW, BPOS - high * LOW)
         for head in range(HEADS):
@@ -144,6 +146,25 @@
     turned_ref[...] = jnp.transpose(index_ref[:, MAIN:])
     parts = part_ref[...].astype(BF)
 
+    def looked_up(index):
+        low = low_onehot(index & (LOW - 1))
+        high_row = index >> 8
+        found = dot(parts, jnp.concatenate([low, low], axis=0))
+        chosen = found[0:TH]
+        for high in range(1, HIGH):
+            chosen = jnp.where(high_row == high, found[high * TH : (high + 1) * TH], chosen)
+        return chosen
+
+    for start in range(0, REST, 4):
+        got = looked_up(jnp.concatenate([turned_ref[start + n : start + n + 1, :MAIN] for n in range(4)], axis=1))
+        for n in range(4):
+            last_ref[pl.ds(start + n, TH, stride=REST), :] = got[:, n * MAIN : (n + 1) * MAIN]
+    got = looked_up(jnp.concatenate([turned_ref[n : n + 1, MAIN:] for n in range(REST)], axis=1))
+    for n in range(REST):
+        half = got[:, LANES * (n // 8) : LANES * (n // 8 + 1)]
+        half = half if n % 8 == 0 else pltpu.roll(half, LANES - REST * (n % 8), 1)
+        last_ref[pl.ds(TH * REST + n, TH, stride=REST), :] = half
+    copy.wait()
     kind_of = lax.broadcasted_iota(jnp.int32, (TH, 1), 0) & (TYPES - 1)
     column = lax.broadcasted_iota(jnp.int32, (1, LANES), 1)
     labels = []
@@ -158,15 +179,6 @@
     for group in range(12):
         mask_ref[TH * group : TH * (group + 1), :] = jnp.where(keys == labels[group], 0.0, MASKED)
 
-    def looked_up(index):
-        low = low_onehot(index & (LOW - 1))
-        high_row = index >> 8
-        found = dot(parts, jnp.concatenate([low, low], axis=0))
-        chosen = found[0:TH]
-        for high in range(1, HIGH):
-            chosen = jnp.where(high_row == high, found[high * TH : (high + 1) * TH], chosen)
-        return chosen
-
     def row_block(block, carry):
         base = pl.multiple_of(block * 8, 8)
         rows = index_ref[pl.ds(base, 8), :MAIN]
@@ -180,20 +192,15 @@
         return carry
 
     lax.fori_loop(0, WIN // 8, row_block, 0, unroll=6)
-    for start in range(0, REST, 4):
-        got = looked_up(jnp.concatenate([turned_ref[start + n : start + n + 1, :MAIN] for n in range(4)], axis=1))
-        for n in range(4):
-            group = (MAIN + start + n) // 12
-            mask = mask_ref[TH * group : TH * (group + 1), :]
-            last_ref[pl.ds(start + n, TH, stride=REST), :] = got[:, n * MAIN : (n + 1) * MAIN] + mask
-    got = looked_up(jnp.concatenate([turned_ref[n : n + 1, MAIN:] for n in range(REST)], axis=1))
     apart = jnp.where(labels[10] == labels[11], 0.0, MASKED)
     split = 132 - MAIN
     for n in range(REST):
-        half = got[:, LANES * (n // 8) : LANES * (n // 8 + 1)]
-        half = half if n % 8 == 0 else pltpu.roll(half, LANES - REST * (n % 8), 1)
+        group = (MAIN + n) // 12
+        rows = pl.ds(n, TH, stride=REST)
+        last_ref[rows, :] = last_ref[rows, :] + mask_ref[TH * group : TH * (group + 1), :]
+        rows = pl.ds(TH * REST + n, TH, stride=REST)
         other = (column < split) if n >= split else (column >= split)
-        last_ref[pl.ds(TH * REST + n, TH, stride=REST), :] = half + jnp.where(other, apart, 0.0)
+        last_ref[rows, :] = last_ref[rows, :] + jnp.where(other, apart, 0.0)
     for th in range(TH):
         rows = slice(th * WIN, th * WIN + MAIN)
         tail_ref[rows, :REST] = jnp.transpose(last_ref[th * REST : (th + 1) * REST, :])
@@ -201,23 +208,64 @@
         tail_ref[rows, :REST] = jnp.transpose(last_ref[(TH + th) * REST : (TH + th + 1) * REST, :])[:REST]
 
 
+def stage_kernel(fields_ref, cotangent_ref, table_ref, index_ref, gain_ref, field_ref, half_ref, table_out, index_out, gain_out, sems):
+    copies = [
+        pltpu.make_async_copy(source, target, sems.at[n])
+        for n, (source, target) in enumerate(
+            [
+                (fields_ref.at[:, :HALF], field_ref),
+                (cotangent_ref.at[:, : HALF // 2], half_ref),
+                (table_ref, table_out),
+                (index_ref, index_out),
+                (gain_ref, gain_out.at[0]),
+            ]
+        )
+    ]
+    for copy in copies:
+        copy.start()
+    for copy in copies:
+        copy.wait()
+
+
+def stage(fields, cotangent, table, index, gain):
+    shape = jax.ShapeDtypeStruct
+    whole = pl.BlockSpec(memory_space=pltpu.VMEM)
+    return pl.pallas_call(
+        stage_kernel,
+        out_shape=[
+            shape((LEVELS, HALF, LAT, C), BF),
+            shape((12, HALF // 2, LEVELS, 2 * C), BF),
+            shape(table.shape, F32),
+            shape(index.shape, jnp.int32),
+            shape((1, 4 * C), F32),
+        ],
+        in_specs=[pl.BlockSpec(memory_space=pltpu.HBM)] * 5,
+        out_specs=[whole] * 5,
+        scratch_shapes=[pltpu.SemaphoreType.DMA((5,))],
+        compiler_params=pltpu.CompilerParams(vmem_limit_bytes=4 * 1024 * 1024),
+        name="stage",
+    )(*(pltpu.with_memory_space_constraint(a, pltpu.HBM) for a in (fields, cotangent, table, index, gain)))
+
+
 def bias_rows(table, index, regions):
     whole = pl.BlockSpec(memory_space=pltpu.VMEM)
     return pl.pallas_call(
         bias_kernel,
         out_shape=[jax.ShapeDtypeStruct((TH * WIN, LANES), F32)] * 2,
-        in_specs=[whole, whole, pl.BlockSpec(memory_space=pltpu.SMEM)],
+        in_specs=[whole, whole, pl.BlockSpec(memory_space=pltpu.HBM)],
         out_specs=[whole, whole],
         scratch_shapes=[
             pltpu.VMEM((HIGH * TH, 2 * LOW), F32),
             pltpu.VMEM((2 * TH * REST, LANES), F32),
             pltpu.VMEM((REST, WIN), jnp.int32),
             pltpu.VMEM((12 * TH, LANES), F32),
+            pltpu.SMEM((LEVELS, LAT), jnp.int32),
+            pltpu.SemaphoreType.DMA,
         ],
         compiler_params=pltpu.CompilerParams(vmem_limit_bytes=16 * 1024 * 1024),
         cost_estimate=pl.CostEstimate(flops=14_000_000_000, bytes_accessed=4_000_000, transcendentals=0),
         name="bias_rows",
-    )(table, index, regions)
+    )(table, index, pltpu.with_memory_space_constraint(regions, pltpu.HBM))
 
 
 def block_kernel(
@@ -437,7 +485,8 @@
     grads_ref[O_TABLE : O_TABLE + TROWS, :] = table[:, :LANES]
     grads_ref[O_TABLE + TROWS : O_END, :] = table[:, LANES:]
     half = keep_ref.shape[0]
-    grads_ref[O_END:, :] = jnp.zeros((2 * half - O_END, LANES), BF)
+    if 2 * half > O_END:
+        grads_ref[O_END:, :] = jnp.zeros((2 * half - O_END, LANES), BF)
     core = core_ref[0]
     keep_ref[...] = grads_ref[pl.ds(pl.multiple_of(core * half, 16), half), :]
     send_ref[...] = grads_ref[pl.ds(pl.multiple_of((1 - core) * half, 16), half), :]
@@ -474,11 +523,19 @@
     )(*args)
 
 
-def finish_kernel(factor, core_ref, held_ref, other_ref, qkv_ref, proj_ref, up_ref, down_ref, merge_ref, table_ref, grads_ref):
+def finish_kernel(
+    factor, core_ref, held_ref, other_ref, merged_west_ref, merged_keep_ref, field_west_ref, field_keep_ref,
+    merged_ref, field_ref, qkv_ref, proj_ref, up_ref, down_ref, merge_ref, table_ref, grads_ref,
+):
     core = core_ref[0]
     half = held_ref.shape[0]
     grads_ref[pl.ds(pl.multiple_of(core * half, 16), half), :] = held_ref[...]
     grads_ref[pl.ds(pl.multiple_of((1 - core) * half, 16), half), :] = other_ref[...]
+
+    merged_ref[:, : HALF // 2] = merged_west_ref[...]
+    merged_ref[:, HALF // 2 :] = merged_keep_ref[...]
+    field_ref[:, :HALF] = field_west_ref[...]
+    field_ref[:, HALF:] = field_keep_ref[...]
 
     def part(start, rows):
         return grads_ref[start : start + rows, :].astype(F32) * factor
@@ -507,12 +564,14 @@
                 table_ref[head, :, start : start + width] = table[row : row + TYPES, :width]
 
 
-def finish(core, held, other, factor):
+def finish(core, held, other, cells, factor):
     shape = jax.ShapeDtypeStruct
     whole = pl.BlockSpec(memory_space=pltpu.VMEM)
     return pl.pallas_call(
         lambda *refs: finish_kernel(factor, *refs),
         out_shape=[
+            shape((12, HALF, LEVELS, 2 * C), BF),
+            shape((LEVELS, 2 * HALF, LAT, C), BF),
             shape((C, 3 * C), F32),
             shape((C, C), F32),
             shape((C, MLP), F32),
@@ -520,12 +579,12 @@
             shape((MLP, 2 * C), F32),
             shape((HEADS, TYPES, BPOS), F32),
         ],
-        in_specs=[pl.BlockSpec(memory_space=pltpu.SMEM), whole, whole],
-        out_specs=[whole] * 6,
+        in_specs=[pl.BlockSpec(memory_space=pltpu.SMEM)] + [whole] * 6,
+        out_specs=[whole] * 8,
         scratch_shapes=[pltpu.VMEM((2 * held.shape[0], LANES), BF)],
         compiler_params=pltpu.CompilerParams(vmem_limit_bytes=16 * 1024 * 1024),
         name="finish",
-    )(core, held, other)
+    )(core, held, other, *cells)
 
 
 def passed_along(value, axis, steps):
@@ -541,28 +600,28 @@
     ]
 
 
-def summed_over(keep, send, axis, others):
+def summed_over(keep, send, axis):
     count = lax.axis_size(axis)
     along = count // (CORES * ACROSS)
     pairs = [(i, i ^ 1) for i in range(count)]
-    held = (keep.astype(F32) + lax.ppermute(send, axis, pairs).astype(F32)).astype(BF)
+    arrived = lax.ppermute(send, axis, pairs)
+    held = (keep.astype(F32) + arrived.astype(F32)).astype(BF)
 
     def exchanged(value, apart, size):
         return lax.all_to_all(value, axis, 0, 0, axis_index_groups=groups_of(count, apart, size))
 
     def reduced(value, apart, size):
-        got = exchanged(value.reshape(size, -1, LANES), apart, size)
+        got = exchanged(value.reshape(size, -1, *value.shape[1:]), apart, size)
         return jnp.sum(got.astype(F32), axis=0).astype(BF)
 
     def gathered(value, apart, size):
-        return exchanged(jnp.broadcast_to(value[None], (size, *value.shape)), apart, size).reshape(-1, LANES)
+        return exchanged(jnp.broadcast_to(value[None], (size, *value.shape)), apart, size).reshape(-1, *value.shape[1:])
 
     held = reduced(held, CORES, ACROSS)
-    held, *others = lax.optimization_barrier((held, *others))
-    held = reduced(held, CORES * ACROSS, along)
-    held = gathered(held, CORES * ACROSS, along)
+    held = reduced(held.reshape(-1, 2, LANES), CORES * ACROSS, along)
+    held = gathered(held, CORES * ACROSS, along).reshape(-1, LANES)
     held = gathered(held, CORES, ACROSS)
-    return held, lax.ppermute(held, axis, pairs), others
+    return held, lax.ppermute(held, axis, pairs)
 
 
 def local(
@@ -584,13 +643,14 @@
     core = (lax.axis_index("lon") % CORES).astype(jnp.int32).reshape(1)
     by_lon = fields.transpose(0, 2, 1, 3)
     by_lat = cotangent.transpose(1, 2, 0, 3)
-    east = passed_along(by_lon[:, :HALF], "lon", -1)
-    east_cotangent = passed_along(by_lat[:, : HALF // 2], "lon", -1)
-    table, core, merge_gain = lax.optimization_barrier(
-        (bias_table.transpose(1, 0, 2), core, merge_gain.reshape(1, 4 * C))
-    )
-    bias, bias_tail = bias_rows(table, bias_index, region_ids)
-    half_rows = -(-O_END // (count * 8)) * 8 * count // CORES
+    field_head, cotangent_head, table, index, merge_gain = stage(
+        by_lon, by_lat, bias_table.transpose(1, 0, 2), bias_index, merge_gain
+    )
+    east = passed_along(field_head, "lon", -1)
+    east_cotangent = passed_along(cotangent_head, "lon", -1)
+    table, core = lax.optimization_barrier((table, core))
+    bias, bias_tail = bias_rows(table, index, region_ids)
+    half_rows = -(-O_END // (count * 2)) * 2 * count // CORES
     keep, send, merged_keep, merged_send, field_keep, field_send = block(
         half_rows,
         core,
@@ -608,15 +668,15 @@
         merge_weight,
         bias,
         bias_tail,
-        bias_index,
+        index,
     )
     merged_west = passed_along(merged_send, "lon", 1)
     field_west = passed_along(field_send, "lon", 1)
-    held, other, (merged_west, field_west) = summed_over(keep, send, "lon", (merged_west, field_west))
-    merged = jnp.concatenate([merged_west, merged_keep], axis=1)
-    field_grad = jnp.concatenate([field_west, field_keep], axis=1)
+    held, other = summed_over(keep, send, "lon")
     factor = float(LEVELS * LAT * fields.shape[2] * count) ** (-0.5)
-    qkv_grad, proj_grad, up_grad, down_grad, merge_grad, table_grad = finish(core, held, other, factor)
+    merged, field_grad, qkv_grad, proj_grad, up_grad, down_grad, merge_grad, table_grad = finish(
+        core, held, other, (merged_west, merged_keep, field_west, field_keep), factor
+    )
     return (
         merged.transpose(2, 0, 1, 3),
         field_grad.transpose(0, 2, 1, 3),
@@ -631,6 +691,7 @@
 
 def solution(mesh):
     whole = P("groups", None, "lon", None)
+
     return jax.shard_map(
         local,
         mesh=mesh,

time: 145 us -> 137 us (0.945)
  blocking collectives: 67.8 us -> 90.2 us
  waiting for transfers between devices: 29 us -> 8.89 us
  local copies, waits for them, and re-layouts: 5.23 us -> 0.26 us
  starting transfers between devices: 7.96 us -> 3.14 us
  other arithmetic: 2.98 us -> 0.58 us
    all_to_all x3 -> x4, blocking collectives: 67.8 us -> 90.2 us  [exchanged(): lax.all_to_all(value, axis, 0, 0, axis_index_groups=groups_of(count, apar...]
    all_to_all x1 -> x0, waiting for transfers between devices: 13 us -> none  [exchanged(): lax.all_to_all(value, axis, 0, 0, axis_index_groups=groups_of(count, apar...]
    ppermute x4, waiting for transfers between devices: 12.6 us -> 6.58 us  [passed_along(): lax.ppermute(value, axis, [(source, (source + steps) % count) for source...]
    all_to_all x1 -> x0, starting transfers between devices: 3.6 us -> none  [exchanged(): lax.all_to_all(value, axis, 0, 0, axis_index_groups=groups_of(count, apar...]
    unnamed x26 -> x18, local copies, waits for them, and re-layouts: 2.61 us -> 0.05 us
    slice x2 -> x0, local copies, waits for them, and re-layouts: 1.78 us -> none  [the longest x1 0.92 us: local(): east = passed_along(by_lon[:, :HALF], 'lon', -1)]
    transpose x2 -> x0, other arithmetic: 1.56 us -> none  [the longest x1 0.79 us: local(): merged.transpose(2, 0, 1, 3)]
  transfers between devices with their start and end apart: 7 -> 6, of which waited for: 4 -> 2; matrix products, arithmetic and copies ran while one was open for 2% -> 0% of each run, Pallas kernels for 6% -> 7%
where the time goes in v2:
time: 137 us; the launch traced here: 135 us
  blocking collectives  90.2 us (66%)
  Pallas kernels  31.2 us (23%)
  waiting for transfers between devices  8.89 us (6%)
  starting transfers between devices  3.14 us (2%)
    all_to_all x4, blocking collectives, exchanged(): lax.all_to_all(value, axis, 0, 0, axis_index_groups=groups_of(count, apar...  90.2 us
    pallas_call x1, Pallas kernels, block(): pl.pallas_call(block_kernel, out_shape=[shape((half_rows, LANES), BF), sh...  19 us
    pallas_call x1, Pallas kernels, bias_rows(): pl.pallas_call(bias_kernel, out_shape=[jax.ShapeDtypeStruct((TH * WIN, LA...  9.05 us
    ppermute x4, waiting for transfers between devices, passed_along(): lax.ppermute(value, axis, [(source, (source + steps) % count) for source...  6.58 us
    ppermute x4, starting transfers between devices, passed_along(): lax.ppermute(value, axis, [(source, (source + steps) % count) for source...  2.78 us
  transfers between devices with their start and end apart: 6, of which 2 were waited for; matrix products, arithmetic and copies ran while one was open for 0% of the time, Pallas kernels for 7%

profile of v2, /device:TPU:168, one launch (start us, length us, event | category | flops | bytes accessed | tf_op | source)
XLA Modules:
  0.0 135.0 jit_solution(10791329211589214010)
XLA Ops:
  0.6 1.2 stage.1
  1.8 1.5 %collective-permute-start.1 = (bf16[12,3,2,384]{3,2,1,0:T(2,128)(2,1)S(1)}, bf16[12,3,2,384]{3,2,1,0:T(2,128)(2,1)S(1)}, u32[]{:S(2)}, u32[]{:S(2)}) collective-permute-start(bf16[12,3,2,384]{3,2,1,0:T(2,128)(2,1)S(1)} %get-tuple-element.34), channel_id=1, source_target_pairs={{0,127},{1,0},{2,1},{3,2},{4,3},{5,4},{6,5},{7,6},{8,7},{9,8},{10,... | collective-permute-start | bytes 165896 | tf_op jit(solution)/shard_map/ppermute | solution.py:592
  3.3 0.6 collective-permute-start
  3.9 0.0 copy-start
  3.9 0.0 copy-start.1
  3.9 0.0 copy-start.2
  3.9 0.0 copy-start.3
  3.9 0.0 copy-start.4
  3.9 0.0 copy-start.5
  3.9 0.0 copy-start.6
  3.9 0.0 copy-start.7
  3.9 0.0 copy-start.8
  3.9 9.0 %bias_rows.1 = (f32[3456,128]{1,0:T(8,128)S(1)}, f32[3456,128]{1,0:T(8,128)S(1)}) custom-call(f32[6,4,3312]{2,1,0:T(4,128)S(1)} %get-tuple-element.36.table_ref, s32[144,144]{1,0:T(8,128)S(1)} %get-tuple-element.37.index_ref, s32[2,24]{1,0:T(2,128)} %regions_ref.1), custom_call_target="tpu_custom_call" | custom-call | flops 14000000000 | bytes 4000000 | tf_op jit(solution)/shard_map/bias_rows/pallas_call | solution.py:252
  13.0 0.0 collective-permute-done.1.east_cotangent_ref
  13.0 0.0 collective-permute-done.east_ref
  13.0 0.0 copy-done
  13.0 0.0 copy-done.1
  13.0 0.0 copy-done.2
  13.1 0.0 copy-done.3
  13.1 0.0 copy-done.4
  13.1 0.0 copy-done.5
  13.1 0.0 copy-done.6
  13.1 0.0 copy-done.7
  13.1 0.0 copy-done.8
  13.1 19.0 %block.1 = (bf16[3200,128]{1,0:T(8,128)(2,1)S(1)}, bf16[3200,128]{1,0:T(8,128)(2,1)S(1)}, bf16[12,3,2,384]{3,2,1,0:T(2,128)(2,1)S(1)}, bf16[12,3,2,384]{3,2,1,0:...) custom-call(s32[1]{0:T(128)} %bitcast.3.core_ref.refs_0_, ...), custom_call_target="tpu_custom_call" | custom-call | flops 24000000000 | bytes 12000000 | tf_op jit(solution)/shard_map/block/pallas_call | solution.py:507
  32.1 0.4 collective-permute-start.2
  32.4 2.3 %collective-permute-done.2 = bf16[3200,128]{1,0:T(8,128)(2,1)S(1)} collective-permute-done((bf16[3200,128]{1,0:T(8,128)(2,1)S(1)}, bf16[3200,128]{1,0:T(8,128)(2,1)S(1)}, u32[]{:S(2)}, u32[]{:S(2)}) %collective-permute-start.2) | collective-permute-done | bytes 819232 | tf_op jit(solution)/shard_map/ppermute | solution.py:607
  34.8 0.2 add_convert_fusion
  35.0 16.0 %all_to_all.20 = bf16[4,800,128]{2,1,0:T(8,128)(2,1)S(1)} all-to-all(bf16[4,800,128]{2,1,0:T(8,128)(2,1)S(1)} %bitcast.24), channel_id=1, replica_groups={{0,2,4,6},{1,3,5,7},{8,10,12,14},{9,11,13,15},{16,18,20,22},{17,19,21,2..., dimensions={0} | all-to-all | bytes 1638400 | tf_op jit(solution)/shard_map/all_to_all | solution.py:611
  51.0 0.2 reduce_sum.24
  51.2 41.3 %all_to_all.21 = bf16[16,25,2,128]{3,2,1,0:T(2,128)(2,1)S(1)} all-to-all(bf16[16,25,2,128]{3,2,1,0:T(2,128)(2,1)S(1)} %bitcast.25), channel_id=1, replica_groups={{0,8,16,24,32,40,48,56,64,72,80,88,96,104,112,120},{1,9,17,25,33,41,49,..., dimensions={0} | all-to-all | bytes 409600 | tf_op jit(solution)/shard_map/all_to_all | solution.py:611
  92.5 0.2 reduce_sum.25
  92.6 0.1 broadcast_in_dim.6
  92.8 20.8 %all_to_all.22 = bf16[16,25,2,128]{3,2,1,0:T(2,128)(2,1)S(1)} all-to-all(bf16[16,25,2,128]{3,2,1,0:T(2,128)(2,1)S(1)} %broadcast_in_dim.6), channel_id=1, replica_groups={{0,8,16,24,32,40,48,56,64,72,80,88,96,104,112,120},{1,9,17,25,33,41,49,..., dimensions={0} | all-to-all | bytes 409600 | tf_op jit(solution)/shard_map/all_to_all | solution.py:611
  113.5 0.1 broadcast_in_dim.15
  113.6 12.1 %all_to_all.23 = bf16[4,800,128]{2,1,0:T(8,128)(2,1)S(1)} all-to-all(bf16[4,800,128]{2,1,0:T(8,128)(2,1)S(1)} %broadcast_in_dim.15), channel_id=1, replica_groups={{0,2,4,6},{1,3,5,7},{8,10,12,14},{9,11,13,15},{16,18,20,22},{17,19,21,2..., dimensions={0} | all-to-all | bytes 1638400 | tf_op jit(solution)/shard_map/all_to_all | solution.py:611
  125.7 0.0 collective-permute-start.3
  125.7 0.5 collective-permute-start.5
  126.2 0.2 collective-permute-start.4
  126.4 6.6 %collective-permute-done.4.refs_3_ = bf16[12,3,2,384]{3,2,1,0:T(2,128)(2,1)S(1)} collective-permute-done((bf16[12,3,2,384]{3,2,1,0:T(2,128)(2,1)S(1)}, bf16[12,3,2,384]{3,2,1,0:T(2,128)(2,1)S(1)}, u32[]{:S(2)}, u32[]{:S(2)}) %collective-permute-start.4) | collective-permute-done | bytes 55328 | tf_op jit(solution)/shard_map/ppermute | solution.py:592
  133.0 0.0 collective-permute-done.5.refs_5_
  133.0 0.0 collective-permute-done.3.refs_2_
  133.0 2.0 %finish.1 = (bf16[12,6,2,384]{3,2,1,0:T(2,128)(2,1)}, bf16[2,12,24,192]{3,2,1,0:T(8,128)(2,1)}, f32[192,576]{1,0:T(8,128)}, f32[192,192]{1,0:T(8,128)}, f32[192,...) custom-call(s32[1]{0:T(128)} %bitcast.3.core_ref.refs_0_, ...), custom_call_target="tpu_custom_call" | custom-call | tf_op jit(solution)/shard_map/finish/pallas_call | solution.py:570
Async XLA Ops:
  1.8 11.2 %collective-permute-start.1 = (bf16[12,3,2,384]{3,2,1,0:T(2,128)(2,1)S(1)}, bf16[12,3,2,384]{3,2,1,0:T(2,128)(2,1)S(1)}, u32[]{:S(2)}, u32[]{:S(2)}) collective-permute-start(bf16[12,3,2,384]{3,2,1,0:T(2,128)(2,1)S(1)} %get-tuple-element.34), channel_id=1, source_target_pairs={{0,127},{1,0},{2,1},{3,2},{4,3},{5,4},{6,5},{7,6},{8,7},{9,8},{10,... | collective-permute-start | bytes 165896 | tf_op jit(solution)/shard_map/ppermute | solution.py:592
  3.3 9.7 %collective-permute-start = (bf16[2,6,24,192]{3,2,1,0:T(8,128)(2,1)S(1)}, bf16[2,6,24,192]{3,2,1,0:T(8,128)(2,1)S(1)}, u32[]{:S(2)}, u32[]{:S(2)}) collective-permute-start(bf16[2,6,24,192]{3,2,1,0:T(8,128)(2,1)S(1)} %get-tuple-element.33), channel_id=1, source_target_pairs={{0,127},{1,0},{2,1},{3,2},{4,3},{5,4},{6,5},{7,6},{8,7},{9,8},{10,... | collective-permute-start | bytes 331784 | tf_op jit(solution)/shard_map/ppermute | solution.py:592
  3.9 9.1 %copy-start = (bf16[2,24,12,192]{3,1,2,0:T(8,128)(2,1)S(1)}, bf16[2,24,12,192]{3,1,2,0:T(8,128)(2,1)}, u32[]{:S(2)}) copy-start(bf16[2,24,12,192]{3,1,2,0:T(8,128)(2,1)} %param.13) | copy-start | bytes 663556
  3.9 9.2 %copy-start.1 = (bf16[2,12,6,384]{3,0,2,1:T(2,128)(2,1)S(1)}, bf16[2,12,6,384]{3,0,2,1:T(2,128)(2,1)}, u32[]{:S(2)}) copy-start(bf16[2,12,6,384]{3,0,2,1:T(2,128)(2,1)} %param.25) | copy-start | bytes 331780
  3.9 9.2 %copy-start.2 = (bf16[768,384]{1,0:T(8,128)(2,1)S(1)}, bf16[768,384]{1,0:T(8,128)(2,1)}, u32[]{:S(2)}) copy-start(bf16[768,384]{1,0:T(8,128)(2,1)} %merge_ref.1) | copy-start | bytes 1769476
  3.9 9.2 %copy-start.3 = (bf16[192,768]{1,0:T(8,128)(2,1)S(1)}, bf16[192,768]{1,0:T(8,128)(2,1)}, u32[]{:S(2)}) copy-start(bf16[192,768]{1,0:T(8,128)(2,1)} %up_ref.1) | copy-start | bytes 884740
  3.9 9.2 %copy-start.4 = (bf16[768,192]{0,1:T(8,128)(2,1)S(1)}, bf16[768,192]{0,1:T(8,128)(2,1)}, u32[]{:S(2)}) copy-start(bf16[768,192]{0,1:T(8,128)(2,1)} %param.22) | copy-start | bytes 884740
  3.9 9.2 %copy-start.5 = (bf16[192,576]{1,0:T(8,128)(2,1)S(1)}, bf16[192,576]{1,0:T(8,128)(2,1)}, u32[]{:S(2)}) copy-start(bf16[192,576]{1,0:T(8,128)(2,1)} %qkv_ref.1) | copy-start | bytes 663556
  3.9 9.2 %copy-start.6 = (bf16[192,192]{1,0:T(8,128)(2,1)S(1)}, bf16[192,192]{1,0:T(8,128)(2,1)}, u32[]{:S(2)}) copy-start(bf16[192,192]{1,0:T(8,128)(2,1)} %proj_ref.1) | copy-start | bytes 221188
  3.9 9.2 %copy-start.7 = (f32[192]{0:T(256)S(1)}, f32[192]{0:T(256)}, u32[]{:S(2)}) copy-start(f32[192]{0:T(256)} %param.14) | copy-start | bytes 2308
  3.9 9.2 %copy-start.8 = (f32[192]{0:T(256)S(1)}, f32[192]{0:T(256)}, u32[]{:S(2)}) copy-start(f32[192]{0:T(256)} %param.20) | copy-start | bytes 2308
  32.1 2.7 %collective-permute-start.2 = (bf16[3200,128]{1,0:T(8,128)(2,1)S(1)}, bf16[3200,128]{1,0:T(8,128)(2,1)S(1)}, u32[]{:S(2)}, u32[]{:S(2)}) collective-permute-start(bf16[3200,128]{1,0:T(8,128)(2,1)S(1)} %get-tuple-element.41), channel_id=1, source_target_pairs={{0,1},{1,0},{2,3},{3,2},{4,5},{5,4},{6,7},{7,6},{8,9},{9,8},{10,11... | collective-permute-start | bytes 2457608 | tf_op jit(solution)/shard_map/ppermute | solution.py:607
  125.7 7.3 %collective-permute-start.3 = (bf16[3200,128]{1,0:T(8,128)(2,1)S(1)}, bf16[3200,128]{1,0:T(8,128)(2,1)S(1)}, u32[]{:S(2)}, u32[]{:S(2)}) collective-permute-start(bf16[3200,128]{1,0:T(8,128)(2,1)S(1)} %bitcast.15), channel_id=1, source_target_pairs={{0,1},{1,0},{2,3},{3,2},{4,5},{5,4},{6,7},{7,6},{8,9},{9,8},{10,11... | collective-permute-start | bytes 2457608 | tf_op jit(solution)/shard_map/ppermute | solution.py:624
  125.7 7.3 %collective-permute-start.5 = (bf16[2,6,24,192]{3,2,1,0:T(8,128)(2,1)S(1)}, bf16[2,6,24,192]{3,2,1,0:T(8,128)(2,1)S(1)}, u32[]{:S(2)}, u32[]{:S(2)}) collective-permute-start(bf16[2,6,24,192]{3,2,1,0:T(8,128)(2,1)S(1)} %get-tuple-element.44), channel_id=1, source_target_pairs={{0,1},{1,2},{2,3},{3,4},{4,5},{5,6},{6,7},{7,8},{8,9},{9,10},{10,1... | collective-permute-start | bytes 331784 | tf_op jit(solution)/shard_map/ppermute | solution.py:592
  126.2 6.8 %collective-permute-start.4 = (bf16[12,3,2,384]{3,2,1,0:T(2,128)(2,1)S(1)}, bf16[12,3,2,384]{3,2,1,0:T(2,128)(2,1)S(1)}, u32[]{:S(2)}, u32[]{:S(2)}) collective-permute-start(bf16[12,3,2,384]{3,2,1,0:T(2,128)(2,1)S(1)} %get-tuple-element.42), channel_id=1, source_target_pairs={{0,1},{1,2},{2,3},{3,4},{4,5},{5,6},{6,7},{7,8},{8,9},{9,10},{10,1... | collective-permute-start | bytes 165896 | tf_op jit(solution)/shard_map/ppermute | solution.py:592

commit v3 on v2

--- a/solution.py
+++ b/solution.py
@@ -139,17 +139,15 @@
             piece = table_ref[head, :, high * LOW : high * LOW + width]
             if width < LOW:
                 piece = jnp.concatenate([piece, jnp.zeros((TYPES, LOW - width), F32)], axis=1)
-            leading = rounded(piece)
             row = high * TH + head * TYPES
-            part_ref[row : row + TYPES, :LOW] = leading
-            part_ref[row : row + TYPES, LOW:] = piece - leading
+            part_ref[row : row + TYPES, :] = piece
     turned_ref[...] = jnp.transpose(index_ref[:, MAIN:])
     parts = part_ref[...].astype(BF)
 
     def looked_up(index):
         low = low_onehot(index & (LOW - 1))
         high_row = index >> 8
-        found = dot(parts, jnp.concatenate([low, low], axis=0))
+        found = dot(parts, low)
         chosen = found[0:TH]
         for high in range(1, HIGH):
             chosen = jnp.where(high_row == high, found[high * TH : (high + 1) * TH], chosen)
@@ -191,7 +189,7 @@
                 main_ref[pl.ds(row, TH, stride=WIN), :] = got[:, n * MAIN : (n + 1) * MAIN] + mask
         return carry
 
-    lax.fori_loop(0, WIN // 8, row_block, 0, unroll=6)
+    lax.fori_loop(0, WIN // 8, row_block, 0, unroll=True)
     apart = jnp.where(labels[10] == labels[11], 0.0, MASKED)
     split = 132 - MAIN
     for n in range(REST):
@@ -213,8 +211,8 @@
         pltpu.make_async_copy(source, target, sems.at[n])
         for n, (source, target) in enumerate(
             [
-                (fields_ref.at[:, :HALF], field_ref),
-                (cotangent_ref.at[:, : HALF // 2], half_ref),
+                (fields_ref.at[:, HALF:], field_ref),
+                (cotangent_ref.at[:, HALF // 2 :], half_ref),
                 (table_ref, table_out),
                 (index_ref, index_out),
                 (gain_ref, gain_out.at[0]),
@@ -255,7 +253,7 @@
         in_specs=[whole, whole, pl.BlockSpec(memory_space=pltpu.HBM)],
         out_specs=[whole, whole],
         scratch_shapes=[
-            pltpu.VMEM((HIGH * TH, 2 * LOW), F32),
+            pltpu.VMEM((HIGH * TH, LOW), F32),
             pltpu.VMEM((2 * TH * REST, LANES), F32),
             pltpu.VMEM((REST, WIN), jnp.int32),
             pltpu.VMEM((12 * TH, LANES), F32),
@@ -269,21 +267,21 @@
 
 
 def block_kernel(
-    core_ref, own_ref, east_ref, own_cotangent_ref, east_cotangent_ref,
+    core_ref, own_ref, west_ref, own_cotangent_ref, west_cotangent_ref,
     norm_gain_ref, qkv_ref, proj_ref, mlp_gain_ref, up_ref, down_ref, merge_gain_ref, merge_ref,
     bias_ref, bias_tail_ref, index_ref,
-    keep_ref, send_ref, merged_keep_ref, merged_send_ref, field_keep_ref, field_send_ref,
-    x_ref, unit_ref, scale_ref, tokens_ref, q_ref, k_ref, v_ref, p_ref, mixed_ref,
+    keep_ref, send_ref, merged_ref, triple_ref, grad_attn_ref, unit_ref, scale_ref,
+    x_ref, tokens_ref, q_ref, k_ref, v_ref, p_ref, mixed_ref,
     unit_mlp_ref, scale_mlp_ref, normed_mlp_ref, hidden_ref, slope_ref, after_mlp_ref,
-    group_ref, normed_merge_ref, grad_after_ref, grad_up_ref, grad_attn_ref, grad_mixed_ref,
-    ds_ref, ds_tail_ref, ds_corner_ref, triple_ref, grads_ref, turned_ref, cells_ref,
+    group_ref, normed_merge_ref, grad_after_ref, grad_up_ref, grad_mixed_ref,
+    ds_ref, ds_tail_ref, ds_corner_ref, grads_ref, turned_ref, cells_ref,
 ):
     to_tokens = onehot(288, 288, of_row=cell_of_token)
     for level in range(LEVELS):
         cells = jnp.concatenate(
             [
-                own_ref[level, HALF:].astype(F32).reshape(144, C),
-                east_ref[level].astype(F32).reshape(144, C),
+                west_ref[level].astype(F32).reshape(144, C),
+                own_ref[level, :HALF].astype(F32).reshape(144, C),
             ],
             axis=0,
         ).astype(BF)
@@ -321,7 +319,7 @@
         mixed_ref[rows, :] = mixed.astype(BF)
         return carry
 
-    lax.fori_loop(0, TYPES, attend, 0)
+    lax.fori_loop(0, TYPES, attend, 0, unroll=True)
     after_attn = rounded(x_ref[...] + rounded(dot(mixed_ref[...], proj_ref[...])))
     x_ref[...] = after_attn
     unit, scale = normalised(after_attn)
@@ -354,17 +352,12 @@
         normed_merge = (unit * merge_gain_ref[:, C * n : C * (n + 1)]).astype(BF)
         normed_merge_ref[n] = normed_merge
         merged = merged + dot(normed_merge, merge_ref[C * n : C * (n + 1), :])
-    merged_cells = dot(onehot(144, MTOK, of_col=cell_of_merged), merged.astype(BF))
+    merged_ref[...] = merged.astype(BF)
     for lat in range(12):
         for lon in range(HALF // 2):
             row = (lat * 3 + lon) * 2
-            merged_keep_ref[lat, lon] = merged_cells[row : row + 2].astype(BF)
-            merged_send_ref[lat, lon] = merged_cells[72 + row : 74 + row].astype(BF)
-    for lat in range(12):
-        for lon in range(HALF // 2):
-            row = (lat * 3 + lon) * 2
-            cells_ref[row : row + 2, :] = own_cotangent_ref[lat, 3 + lon].astype(F32)
-            cells_ref[72 + row : 74 + row, :] = east_cotangent_ref[lat, lon].astype(F32)
+            cells_ref[row : row + 2, :] = west_cotangent_ref[lat, lon].astype(F32)
+            cells_ref[72 + row : 74 + row, :] = own_cotangent_ref[lat, lon].astype(F32)
     grad_merged = dot(onehot(MTOK, 144, of_row=cell_of_merged), cells_ref[...].astype(BF)).astype(BF)
 
     scaled, total, along = [], 0.0, 0.0
@@ -437,7 +430,7 @@
         triple_ref[rows, :] = jnp.transpose(triple)
         return carry
 
-    lax.fori_loop(0, TYPES, attend_back, 0)
+    lax.fori_loop(0, TYPES, attend_back, 0, unroll=True)
     grad_triple = triple_ref[...]
     grad_qkv = dot_tn(tokens_ref[...], grad_triple).astype(BF)
     for b in range(4):
@@ -445,19 +438,6 @@
     grads_ref[O_QKV_TAIL : O_QKV_TAIL + C // 2, :] = jnp.concatenate(
         [grad_qkv[: C // 2, 512:], grad_qkv[C // 2 :, 512:]], axis=1
     )
-    grad_normed = rounded(dot_nt(grad_triple, qkv_ref[...]))
-    x_ref[...] = grad_attn_ref[...].astype(F32) + norm_grad(
-        grad_normed, unit_ref[...], scale_ref[...], norm_gain_ref[...]
-    )
-    to_cells = onehot(288, 288, of_col=cell_of_token)
-    for level in range(LEVELS):
-        ordered = jnp.concatenate(
-            [x_ref[WIN * kind + 72 * level : WIN * kind + 72 * level + 72, :] for kind in range(TYPES)], axis=0
-        )
-        cells = dot(to_cells, ordered.astype(BF))
-        field_keep_ref[level] = cells[:144].reshape(HALF, LAT, C).astype(BF)
-        field_send_ref[level] = cells[144:].reshape(HALF, LAT, C).astype(BF)
-
     turned_ref[...] = jnp.transpose(index_ref[:, MAIN:])
 
     def table_terms(index, slab):
@@ -473,7 +453,7 @@
         slab = jnp.concatenate([ds_ref[pl.ds(base + n, TH, stride=WIN), :] for n in range(8)], axis=1)
         return carry + table_terms(index, slab)
 
-    table = lax.fori_loop(0, WIN // 8, row_block, jnp.zeros((TROWS, LOW), F32), unroll=6)
+    table = lax.fori_loop(0, WIN // 8, row_block, jnp.zeros((TROWS, LOW), F32), unroll=9)
     blank = jnp.zeros((1, LOW - WIN), jnp.int32)
     for key in range(0, REST, 4):
         index, slab = [], []
@@ -496,12 +476,12 @@
     shape = jax.ShapeDtypeStruct
     whole = pl.BlockSpec(memory_space=pltpu.VMEM)
     scratch = [
-        ((TOK, C), F32), ((TOK, C), F32), ((TOK, 1), F32), ((TOK, C), BF), ((TOK, C), BF), ((TOK, C), BF),
+        ((TOK, C), F32), ((TOK, C), BF), ((TOK, C), BF), ((TOK, C), BF),
         ((TOK, C), BF), ((TH, WIN, WIN), F32), ((TOK, C), BF),
         ((TOK, C), F32), ((TOK, 1), F32), ((TOK, C), BF), ((TOK, MLP), BF), ((TOK, MLP), F32), ((TOK, C), BF),
-        ((4, MTOK, C), F32), ((4, MTOK, C), BF), ((TOK, C), BF), ((TOK, MLP), BF), ((TOK, C), BF), ((TOK, C), BF),
+        ((4, MTOK, C), F32), ((4, MTOK, C), BF), ((TOK, C), BF), ((TOK, MLP), BF), ((TOK, C), BF),
         ((TH * WIN, LANES), F32), ((TH * REST, LANES), F32), ((TH * REST, LANES), F32),
-        ((TOK, 3 * C), BF), ((2 * half_rows, LANES), BF), ((REST, WIN), jnp.int32),
+        ((2 * half_rows, LANES), BF), ((REST, WIN), jnp.int32),
         ((144, 2 * C), F32),
     ]
     return pl.pallas_call(
@@ -509,13 +489,14 @@
         out_shape=[
             shape((half_rows, LANES), BF),
             shape((half_rows, LANES), BF),
-            shape((12, HALF // 2, LEVELS, 2 * C), BF),
-            shape((12, HALF // 2, LEVELS, 2 * C), BF),
-            shape((LEVELS, HALF, LAT, C), BF),
-            shape((LEVELS, HALF, LAT, C), BF),
+            shape((MTOK, 2 * C), BF),
+            shape((TOK, 3 * C), BF),
+            shape((TOK, C), BF),
+            shape((TOK, C), F32),
+            shape((TOK, 1), F32),
         ],
         in_specs=[pl.BlockSpec(memory_space=pltpu.SMEM)] + [whole] * (len(args) - 1),
-        out_specs=[whole] * 6,
+        out_specs=[whole] * 7,
         scratch_shapes=[pltpu.VMEM(*item) for item in scratch],
         compiler_params=pltpu.CompilerParams(vmem_limit_bytes=24 * 1024 * 1024),
         cost_estimate=pl.CostEstimate(flops=24_000_000_000, bytes_accessed=12_000_000, transcendentals=2_000_000),
@@ -523,8 +504,54 @@
     )(*args)
 
 
+def cells_kernel(
+    merged_ref, triple_ref, grad_attn_ref, unit_ref, scale_ref, qkv_ref, gain_ref,
+    merged_keep_ref, field_keep_ref, home_ref, x_ref,
+):
+    grad_normed = rounded(dot_nt(triple_ref[...], qkv_ref[...]))
+    x_ref[...] = grad_attn_ref[...].astype(F32) + norm_grad(
+        grad_normed, unit_ref[...], scale_ref[...], gain_ref[...]
+    )
+    to_cells = onehot(288, 288, of_col=cell_of_token)
+    for level in range(LEVELS):
+        ordered = jnp.concatenate(
+            [x_ref[WIN * kind + 72 * level : WIN * kind + 72 * level + 72, :] for kind in range(TYPES)], axis=0
+        )
+        cells = dot(to_cells, ordered.astype(BF))
+        home_ref[HALF * level : HALF * (level + 1)] = cells[:144].reshape(HALF, LAT, C).astype(BF)
+        field_keep_ref[level] = cells[144:].reshape(HALF, LAT, C).astype(BF)
+    merged_cells = dot(onehot(144, MTOK, of_col=cell_of_merged), merged_ref[...])
+    for lat in range(12):
+        for lon in range(HALF // 2):
+            row = 72 + (lat * 3 + lon) * 2
+            merged_keep_ref[lat, lon] = merged_cells[row : row + 2].astype(BF)
+    for side in range(2):
+        home_ref[12 + 3 * side : 15 + 3 * side] = (
+            merged_cells[:72, C * side : C * (side + 1)].reshape(3, LAT, C).astype(BF)
+        )
+
+
+def to_grid(*args):
+    shape = jax.ShapeDtypeStruct
+    whole = pl.BlockSpec(memory_space=pltpu.VMEM)
+    return pl.pallas_call(
+        cells_kernel,
+        out_shape=[
+            shape((12, HALF // 2, LEVELS, 2 * C), BF),
+            shape((LEVELS, HALF, LAT, C), BF),
+            shape((LEVELS * HALF + 6, LAT, C), BF),
+        ],
+        in_specs=[whole] * 7,
+        out_specs=[whole] * 3,
+        scratch_shapes=[pltpu.VMEM((TOK, C), F32)],
+        compiler_params=pltpu.CompilerParams(vmem_limit_bytes=12 * 1024 * 1024),
+        cost_estimate=pl.CostEstimate(flops=1_500_000_000, bytes_accessed=3_000_000, transcendentals=0),
+        name="to_grid",
+    )(*args)
+
+
 def finish_kernel(
-    factor, core_ref, held_ref, other_ref, merged_west_ref, merged_keep_ref, field_west_ref, field_keep_ref,
+    factor, core_ref, held_ref, other_ref, east_ref, merged_keep_ref, field_keep_ref,
     merged_ref, field_ref, qkv_ref, proj_ref, up_ref, down_ref, merge_ref, table_ref, grads_ref,
 ):
     core = core_ref[0]
@@ -532,10 +559,16 @@
     grads_ref[pl.ds(pl.multiple_of(core * half, 16), half), :] = held_ref[...]
     grads_ref[pl.ds(pl.multiple_of((1 - core) * half, 16), half), :] = other_ref[...]
 
-    merged_ref[:, : HALF // 2] = merged_west_ref[...]
-    merged_ref[:, HALF // 2 :] = merged_keep_ref[...]
-    field_ref[:, :HALF] = field_west_ref[...]
-    field_ref[:, HALF:] = field_keep_ref[...]
+    for level in range(LEVELS):
+        field_ref[level, HALF:] = east_ref[HALF * level : HALF * (level + 1)]
+    field_ref[:, :HALF] = field_keep_ref[...]
+    sides = [east_ref[12 + 3 * side : 15 + 3 * side].astype(F32).reshape(72, C) for side in range(2)]
+    cells = jnp.concatenate(sides, axis=1)
+    for lat in range(12):
+        for lon in range(HALF // 2):
+            row = (lat * 3 + lon) * 2
+            merged_ref[lat, HALF // 2 + lon] = cells[row : row + 2].astype(BF)
+    merged_ref[:, : HALF // 2] = merged_keep_ref[...]
 
     def part(start, rows):
         return grads_ref[start : start + rows, :].astype(F32) * factor
@@ -579,7 +612,7 @@
             shape((MLP, 2 * C), F32),
             shape((HEADS, TYPES, BPOS), F32),
         ],
-        in_specs=[pl.BlockSpec(memory_space=pltpu.SMEM)] + [whole] * 6,
+        in_specs=[pl.BlockSpec(memory_space=pltpu.SMEM)] + [whole] * 5,
         out_specs=[whole] * 8,
         scratch_shapes=[pltpu.VMEM((2 * held.shape[0], LANES), BF)],
         compiler_params=pltpu.CompilerParams(vmem_limit_bytes=16 * 1024 * 1024),
@@ -643,21 +676,21 @@
     core = (lax.axis_index("lon") % CORES).astype(jnp.int32).reshape(1)
     by_lon = fields.transpose(0, 2, 1, 3)
     by_lat = cotangent.transpose(1, 2, 0, 3)
-    field_head, cotangent_head, table, index, merge_gain = stage(
+    field_last, cotangent_last, table, index, merge_gain = stage(
         by_lon, by_lat, bias_table.transpose(1, 0, 2), bias_index, merge_gain
     )
-    east = passed_along(field_head, "lon", -1)
-    east_cotangent = passed_along(cotangent_head, "lon", -1)
+    west = passed_along(field_last, "lon", 1)
+    west_cotangent = passed_along(cotangent_last, "lon", 1)
     table, core = lax.optimization_barrier((table, core))
     bias, bias_tail = bias_rows(table, index, region_ids)
     half_rows = -(-O_END // (count * 2)) * 2 * count // CORES
-    keep, send, merged_keep, merged_send, field_keep, field_send = block(
+    keep, send, *results = block(
         half_rows,
         core,
         by_lon,
-        east,
+        west,
         by_lat,
-        east_cotangent,
+        west_cotangent,
         norm_gain.reshape(1, C),
         qkv_weight,
         proj_weight,
@@ -670,12 +703,12 @@
         bias_tail,
         index,
     )
-    merged_west = passed_along(merged_send, "lon", 1)
-    field_west = passed_along(field_send, "lon", 1)
+    merged_keep, field_keep, home = to_grid(*results, qkv_weight, norm_gain.reshape(1, C))
+    east = passed_along(home, "lon", -1)
     held, other = summed_over(keep, send, "lon")
     factor = float(LEVELS * LAT * fields.shape[2] * count) ** (-0.5)
     merged, field_grad, qkv_grad, proj_grad, up_grad, down_grad, merge_grad, table_grad = finish(
-        core, held, other, (merged_west, merged_keep, field_west, field_keep), factor
+        core, held, other, (east, merged_keep, field_keep), factor
     )
     return (
         merged.transpose(2, 0, 1, 3),

time: 137 us -> 127 us (0.927)
  the two profiles are of different devices: /device:TPU:168 before, /device:TPU:40 now
where the time goes in v3:
time: 127 us
  blocking collectives  68.6 us (54%)
  waiting for transfers between devices  26.7 us (21%)
  Pallas kernels  24.4 us (19%)
  starting transfers between devices  5.63 us (4%)
    all_to_all x4, blocking collectives, exchanged(): lax.all_to_all(value, axis, 0, 0, axis_index_groups=groups_of(count, apar...  68.6 us
    ppermute x3, waiting for transfers between devices, passed_along(): lax.ppermute(value, axis, [(source, (source + steps) % count) for source...  24.4 us
    pallas_call x1, Pallas kernels, block(): pl.pallas_call(block_kernel, out_shape=[shape((half_rows, LANES), BF), sh...  14.8 us
    ppermute x3, starting transfers between devices, passed_along(): lax.ppermute(value, axis, [(source, (source + steps) % count) for source...  5.49 us
    pallas_call x1, Pallas kernels, bias_rows(): pl.pallas_call(bias_kernel, out_shape=[jax.ShapeDtypeStruct((TH * WIN, LA...  5.16 us
  transfers between devices with their start and end apart: 5, of which 4 were waited for; matrix products, arithmetic and copies ran while one was open for 0% of the time, Pallas kernels for 5%

profile of v3, /device:TPU:40, one launch (start us, length us, event | category | flops | bytes accessed | tf_op | source)
XLA Modules:
  0.0 127.0 jit_solution(11086931766662601139)
XLA Ops:
  0.6 1.2 stage.1
  1.8 0.1 collective-permute-start.1
  1.9 1.7 %collective-permute-start = (bf16[2,6,24,192]{3,2,1,0:T(8,128)(2,1)S(1)}, bf16[2,6,24,192]{3,2,1,0:T(8,128)(2,1)S(1)}, u32[]{:S(2)}, u32[]{:S(2)}) collective-permute-start(bf16[2,6,24,192]{3,2,1,0:T(8,128)(2,1)S(1)} %get-tuple-element.37), channel_id=1, source_target_pairs={{0,1},{1,2},{2,3},{3,4},{4,5},{5,6},{6,7},{7,8},{8,9},{9,10},{10,1... | collective-permute-start | bytes 331784 | tf_op jit(solution)/shard_map/ppermute | solution.py:625
  3.7 0.0 copy-start
  3.7 0.0 copy-start.1
  3.7 0.0 copy-start.2
  3.7 0.0 copy-start.3
  3.7 0.0 copy-start.4
  3.7 0.0 copy-start.5
  3.7 0.0 copy-start.6
  3.7 0.0 copy-start.7
  3.7 0.0 copy-start.8
  3.7 5.2 %bias_rows.1 = (f32[3456,128]{1,0:T(8,128)S(1)}, f32[3456,128]{1,0:T(8,128)S(1)}) custom-call(f32[6,4,3312]{2,1,0:T(4,128)S(1)} %get-tuple-element.40.table_ref, s32[144,144]{1,0:T(8,128)S(1)} %get-tuple-element.41.index_ref, s32[2,24]{1,0:T(2,128)} %regions_ref.1), custom_call_target="tpu_custom_call" | custom-call | flops 14000000000 | bytes 4000000 | tf_op jit(solution)/shard_map/bias_rows/pallas_call | solution.py:250
  8.9 19.4 %collective-permute-done.1.west_cotangent_ref = bf16[12,3,2,384]{3,2,1,0:T(2,128)(2,1)S(1)} collective-permute-done((bf16[12,3,2,384]{3,2,1,0:T(2,128)(2,1)S(1)}, bf16[12,3,2,384]{3,2,1,0:T(2,128)(2,1)S(1)}, u32[]{:S(2)}, u32[]{:S(2)}) %collective-permute-start.1) | collective-permute-done | bytes 55328 | tf_op jit(solution)/shard_map/ppermute | solution.py:625
  28.2 1.6 %collective-permute-done.west_ref = bf16[2,6,24,192]{3,2,1,0:T(8,128)(2,1)S(1)} collective-permute-done((bf16[2,6,24,192]{3,2,1,0:T(8,128)(2,1)S(1)}, bf16[2,6,24,192]{3,2,1,0:T(8,128)(2,1)S(1)}, u32[]{:S(2)}, u32[]{:S(2)}) %collective-permute-start) | collective-permute-done | bytes 110624 | tf_op jit(solution)/shard_map/ppermute | solution.py:625
  29.8 0.0 copy-done
  29.8 0.0 copy-done.1
  29.8 0.0 copy-done.2
  29.8 0.0 copy-done.3
  29.9 0.0 copy-done.4
  29.9 0.0 copy-done.5
  29.9 0.0 copy-done.6
  29.9 0.0 copy-done.7
  29.9 0.0 copy-done.8
  29.9 14.8 %block.1 = (bf16[3200,128]{1,0:T(8,128)(2,1)S(1)}, bf16[3200,128]{1,0:T(8,128)(2,1)S(1)}, bf16[160,384]{1,0:T(8,128)(2,1)S(1)}, bf16[576,576]{1,0:T(8,128)(2,1)S...) custom-call(s32[1]{0:T(128)} %bitcast.3.core_ref.refs_0_, ...), custom_call_target="tpu_custom_call" | custom-call | flops 24000000000 | bytes 12000000 | tf_op jit(solution)/shard_map/block/pallas_call | solution.py:487
  44.7 0.1 collective-permute-start.2
  44.9 2.3 %collective-permute-done.2 = bf16[3200,128]{1,0:T(8,128)(2,1)S(1)} collective-permute-done((bf16[3200,128]{1,0:T(8,128)(2,1)S(1)}, bf16[3200,128]{1,0:T(8,128)(2,1)S(1)}, u32[]{:S(2)}, u32[]{:S(2)}) %collective-permute-start.2) | collective-permute-done | bytes 819232 | tf_op jit(solution)/shard_map/ppermute | solution.py:640
  47.2 0.2 add_convert_fusion
  47.4 15.6 %all_to_all.20 = bf16[4,800,128]{2,1,0:T(8,128)(2,1)S(1)} all-to-all(bf16[4,800,128]{2,1,0:T(8,128)(2,1)S(1)} %bitcast.25), channel_id=1, replica_groups={{0,2,4,6},{1,3,5,7},{8,10,12,14},{9,11,13,15},{16,18,20,22},{17,19,21,2..., dimensions={0} | all-to-all | bytes 1638400 | tf_op jit(solution)/shard_map/all_to_all | solution.py:644
  63.1 0.2 reduce_sum.24
  63.2 20.1 %all_to_all.21 = bf16[16,25,2,128]{3,2,1,0:T(2,128)(2,1)S(1)} all-to-all(bf16[16,25,2,128]{3,2,1,0:T(2,128)(2,1)S(1)} %bitcast.26), channel_id=1, replica_groups={{0,8,16,24,32,40,48,56,64,72,80,88,96,104,112,120},{1,9,17,25,33,41,49,..., dimensions={0} | all-to-all | bytes 409600 | tf_op jit(solution)/shard_map/all_to_all | solution.py:644
  83.3 0.2 reduce_sum.25
  83.5 0.1 broadcast_in_dim.6
  83.6 20.8 %all_to_all.22 = bf16[16,25,2,128]{3,2,1,0:T(2,128)(2,1)S(1)} all-to-all(bf16[16,25,2,128]{3,2,1,0:T(2,128)(2,1)S(1)} %broadcast_in_dim.6), channel_id=1, replica_groups={{0,8,16,24,32,40,48,56,64,72,80,88,96,104,112,120},{1,9,17,25,33,41,49,..., dimensions={0} | all-to-all | bytes 409600 | tf_op jit(solution)/shard_map/all_to_all | solution.py:644
  104.5 0.1 broadcast_in_dim.15
  104.6 12.1 %all_to_all.23 = bf16[4,800,128]{2,1,0:T(8,128)(2,1)S(1)} all-to-all(bf16[4,800,128]{2,1,0:T(8,128)(2,1)S(1)} %broadcast_in_dim.15), channel_id=1, replica_groups={{0,2,4,6},{1,3,5,7},{8,10,12,14},{9,11,13,15},{16,18,20,22},{17,19,21,2..., dimensions={0} | all-to-all | bytes 1638400 | tf_op jit(solution)/shard_map/all_to_all | solution.py:644
  116.6 0.0 collective-permute-start.3
  116.6 1.3 to_grid.1
  117.9 3.6 %collective-permute-start.4 = (bf16[18,24,192]{2,1,0:T(8,128)(2,1)S(1)}, bf16[18,24,192]{2,1,0:T(8,128)(2,1)S(1)}, u32[]{:S(2)}, u32[]{:S(2)}) collective-permute-start(bf16[18,24,192]{2,1,0:T(8,128)(2,1)S(1)} %get-tuple-element.51), channel_id=1, source_target_pairs={{0,127},{1,0},{2,1},{3,2},{4,3},{5,4},{6,5},{7,6},{8,7},{9,8},{10,... | collective-permute-start | bytes 497672 | tf_op jit(solution)/shard_map/ppermute | solution.py:625
  121.6 3.5 %collective-permute-done.4.refs_3_ = bf16[18,24,192]{2,1,0:T(8,128)(2,1)S(1)} collective-permute-done((bf16[18,24,192]{2,1,0:T(8,128)(2,1)S(1)}, bf16[18,24,192]{2,1,0:T(8,128)(2,1)S(1)}, u32[]{:S(2)}, u32[]{:S(2)}) %collective-permute-start.4) | collective-permute-done | bytes 165920 | tf_op jit(solution)/shard_map/ppermute | solution.py:625
  125.0 0.0 collective-permute-done.3.refs_2_
  125.0 2.0 %finish.1 = (bf16[12,6,2,384]{3,2,1,0:T(2,128)(2,1)}, bf16[2,12,24,192]{3,2,1,0:T(8,128)(2,1)}, f32[192,576]{1,0:T(8,128)}, f32[192,192]{1,0:T(8,128)}, f32[192,...) custom-call(s32[1]{0:T(128)} %bitcast.3.core_ref.refs_0_, ...), custom_call_target="tpu_custom_call" | custom-call | tf_op jit(solution)/shard_map/finish/pallas_call | solution.py:603
Async XLA Ops:
  1.8 26.5 %collective-permute-start.1 = (bf16[12,3,2,384]{3,2,1,0:T(2,128)(2,1)S(1)}, bf16[12,3,2,384]{3,2,1,0:T(2,128)(2,1)S(1)}, u32[]{:S(2)}, u32[]{:S(2)}) collective-permute-start(bf16[12,3,2,384]{3,2,1,0:T(2,128)(2,1)S(1)} %get-tuple-element.38), channel_id=1, source_target_pairs={{0,1},{1,2},{2,3},{3,4},{4,5},{5,6},{6,7},{7,8},{8,9},{9,10},{10,1... | collective-permute-start | bytes 165896 | tf_op jit(solution)/shard_map/ppermute | solution.py:625
  1.9 27.9 %collective-permute-start = (bf16[2,6,24,192]{3,2,1,0:T(8,128)(2,1)S(1)}, bf16[2,6,24,192]{3,2,1,0:T(8,128)(2,1)S(1)}, u32[]{:S(2)}, u32[]{:S(2)}) collective-permute-start(bf16[2,6,24,192]{3,2,1,0:T(8,128)(2,1)S(1)} %get-tuple-element.37), channel_id=1, source_target_pairs={{0,1},{1,2},{2,3},{3,4},{4,5},{5,6},{6,7},{7,8},{8,9},{9,10},{10,1... | collective-permute-start | bytes 331784 | tf_op jit(solution)/shard_map/ppermute | solution.py:625
  3.7 26.2 %copy-start = (bf16[2,24,12,192]{3,1,2,0:T(8,128)(2,1)S(1)}, bf16[2,24,12,192]{3,1,2,0:T(8,128)(2,1)}, u32[]{:S(2)}) copy-start(bf16[2,24,12,192]{3,1,2,0:T(8,128)(2,1)} %param.13) | copy-start | bytes 663556
  3.7 26.2 %copy-start.1 = (bf16[2,12,6,384]{3,0,2,1:T(2,128)(2,1)S(1)}, bf16[2,12,6,384]{3,0,2,1:T(2,128)(2,1)}, u32[]{:S(2)}) copy-start(bf16[2,12,6,384]{3,0,2,1:T(2,128)(2,1)} %param.25) | copy-start | bytes 331780
  3.7 26.2 %copy-start.2 = (bf16[768,384]{1,0:T(8,128)(2,1)S(1)}, bf16[768,384]{1,0:T(8,128)(2,1)}, u32[]{:S(2)}) copy-start(bf16[768,384]{1,0:T(8,128)(2,1)} %merge_ref.1) | copy-start | bytes 1769476
  3.7 26.2 %copy-start.3 = (bf16[192,768]{1,0:T(8,128)(2,1)S(1)}, bf16[192,768]{1,0:T(8,128)(2,1)}, u32[]{:S(2)}) copy-start(bf16[192,768]{1,0:T(8,128)(2,1)} %up_ref.1) | copy-start | bytes 884740
  3.7 26.2 %copy-start.4 = (bf16[768,192]{0,1:T(8,128)(2,1)S(1)}, bf16[768,192]{0,1:T(8,128)(2,1)}, u32[]{:S(2)}) copy-start(bf16[768,192]{0,1:T(8,128)(2,1)} %param.22) | copy-start | bytes 884740
  3.7 26.2 %copy-start.5 = (bf16[192,576]{1,0:T(8,128)(2,1)S(1)}, bf16[192,576]{1,0:T(8,128)(2,1)}, u32[]{:S(2)}) copy-start(bf16[192,576]{1,0:T(8,128)(2,1)} %qkv_ref.3) | copy-start | bytes 663556
  3.7 26.2 %copy-start.6 = (bf16[192,192]{1,0:T(8,128)(2,1)S(1)}, bf16[192,192]{1,0:T(8,128)(2,1)}, u32[]{:S(2)}) copy-start(bf16[192,192]{1,0:T(8,128)(2,1)} %proj_ref.1) | copy-start | bytes 221188
  3.7 26.2 %copy-start.7 = (f32[192]{0:T(256)S(1)}, f32[192]{0:T(256)}, u32[]{:S(2)}) copy-start(f32[192]{0:T(256)} %param.20) | copy-start | bytes 2308
  3.7 26.2 %copy-start.8 = (f32[192]{0:T(256)S(1)}, f32[192]{0:T(256)}, u32[]{:S(2)}) copy-start(f32[192]{0:T(256)} %param.14) | copy-start | bytes 2308
  44.7 2.5 %collective-permute-start.2 = (bf16[3200,128]{1,0:T(8,128)(2,1)S(1)}, bf16[3200,128]{1,0:T(8,128)(2,1)S(1)}, u32[]{:S(2)}, u32[]{:S(2)}) collective-permute-start(bf16[3200,128]{1,0:T(8,128)(2,1)S(1)} %get-tuple-element.45), channel_id=1, source_target_pairs={{0,1},{1,0},{2,3},{3,2},{4,5},{5,4},{6,7},{7,6},{8,9},{9,8},{10,11... | collective-permute-start | bytes 2457608 | tf_op jit(solution)/shard_map/ppermute | solution.py:640
  116.6 8.4 %collective-permute-start.3 = (bf16[3200,128]{1,0:T(8,128)(2,1)S(1)}, bf16[3200,128]{1,0:T(8,128)(2,1)S(1)}, u32[]{:S(2)}, u32[]{:S(2)}) collective-permute-start(bf16[3200,128]{1,0:T(8,128)(2,1)S(1)} %bitcast.15), channel_id=1, source_target_pairs={{0,1},{1,0},{2,3},{3,2},{4,5},{5,4},{6,7},{7,6},{8,9},{9,8},{10,11... | collective-permute-start | bytes 2457608 | tf_op jit(solution)/shard_map/ppermute | solution.py:657
  117.9 7.1 %collective-permute-start.4 = (bf16[18,24,192]{2,1,0:T(8,128)(2,1)S(1)}, bf16[18,24,192]{2,1,0:T(8,128)(2,1)S(1)}, u32[]{:S(2)}, u32[]{:S(2)}) collective-permute-start(bf16[18,24,192]{2,1,0:T(8,128)(2,1)S(1)} %get-tuple-element.51), channel_id=1, source_target_pairs={{0,127},{1,0},{2,1},{3,2},{4,3},{5,4},{6,5},{7,6},{8,7},{9,8},{10,... | collective-permute-start | bytes 497672 | tf_op jit(solution)/shard_map/ppermute | solution.py:625

commit v4 on v3

--- a/solution.py
+++ b/solution.py
@@ -31,15 +31,18 @@
 ACROSS = 4
 
 TROWS = 320
+TLAST = (HIGH - 1) * TH
+LAST = (HIGH - 1) * LOW + LANES
 O_UP = 0
-O_MERGE = O_UP + 6 * C
-O_DOWN = O_MERGE + 3 * MLP
+O_DOWN = O_UP + 6 * C
 O_QKV = O_DOWN + 6 * C
 O_QKV_TAIL = O_QKV + 4 * C
-O_PROJ = O_QKV_TAIL + C // 2
+O_LAST = O_QKV_TAIL + C // 2
+O_MERGE = O_LAST + TROWS - TLAST
+O_PROJ = O_MERGE + 3 * MLP
 O_PROJ_TAIL = O_PROJ + C
 O_TABLE = O_PROJ_TAIL + C // 2
-O_END = O_TABLE + 2 * TROWS
+O_END = O_TABLE + TROWS + TLAST
 
 
 def dot(a, b):
@@ -270,11 +273,11 @@
     core_ref, own_ref, west_ref, own_cotangent_ref, west_cotangent_ref,
     norm_gain_ref, qkv_ref, proj_ref, mlp_gain_ref, up_ref, down_ref, merge_gain_ref, merge_ref,
     bias_ref, bias_tail_ref, index_ref,
-    keep_ref, send_ref, merged_ref, triple_ref, grad_attn_ref, unit_ref, scale_ref,
+    keep_ref, send_ref, normed_merge_ref, triple_ref, grad_attn_ref, unit_ref, scale_ref,
     x_ref, tokens_ref, q_ref, k_ref, v_ref, p_ref, mixed_ref,
     unit_mlp_ref, scale_mlp_ref, normed_mlp_ref, hidden_ref, slope_ref, after_mlp_ref,
-    group_ref, normed_merge_ref, grad_after_ref, grad_up_ref, grad_mixed_ref,
-    ds_ref, ds_tail_ref, ds_corner_ref, grads_ref, turned_ref, cells_ref,
+    group_ref, grad_after_ref, grad_up_ref, grad_mixed_ref,
+    ds_ref, ds_tail_ref, ds_corner_ref, grads_ref, turned_ref, cells_ref, grad_merged_ref, scaled_ref,
 ):
     to_tokens = onehot(288, 288, of_row=cell_of_token)
     for level in range(LEVELS):
@@ -296,6 +299,15 @@
     q_ref[...] = dot(tokens, qkv_ref[:, 0:C]).astype(BF)
     k_ref[...] = dot(tokens, qkv_ref[:, C : 2 * C]).astype(BF)
     v_ref[...] = dot(tokens, qkv_ref[:, 2 * C :]).astype(BF)
+    for lat in range(12):
+        for lon in range(HALF // 2):
+            row = (lat * 3 + lon) * 2
+            cells_ref[row : row + 2, :] = west_cotangent_ref[lat, lon].astype(F32)
+            cells_ref[72 + row : 74 + row, :] = own_cotangent_ref[lat, lon].astype(F32)
+    grad_merged_ref[...] = dot(onehot(MTOK, 144, of_row=cell_of_merged), cells_ref[...].astype(BF)).astype(BF)
+    for n in range(4):
+        value = rounded(dot_nt(grad_merged_ref[...], merge_ref[C * n : C * (n + 1), :]))
+        scaled_ref[n] = value * merge_gain_ref[:, C * n : C * (n + 1)]
     lane = lax.broadcasted_iota(jnp.int32, (1, C), 1)
     of_head = [
         jnp.where((lane >= HEAD * h) & (lane < HEAD * (h + 1)), 1.0, 0.0).astype(BF) for h in range(HEADS)
@@ -345,28 +357,14 @@
     centred = [v - mean for v in quarters]
     variance = sum(jnp.sum(v * v, axis=-1, keepdims=True) for v in centred) * (1.0 / MLP)
     scale_merge = lax.rsqrt(variance + EPS)
-    merged = jnp.zeros((MTOK, 2 * C), F32)
     for n in range(4):
         unit = centred[n] * scale_merge
         group_ref[n] = unit
         normed_merge = (unit * merge_gain_ref[:, C * n : C * (n + 1)]).astype(BF)
         normed_merge_ref[n] = normed_merge
-        merged = merged + dot(normed_merge, merge_ref[C * n : C * (n + 1), :])
-    merged_ref[...] = merged.astype(BF)
-    for lat in range(12):
-        for lon in range(HALF // 2):
-            row = (lat * 3 + lon) * 2
-            cells_ref[row : row + 2, :] = west_cotangent_ref[lat, lon].astype(F32)
-            cells_ref[72 + row : 74 + row, :] = own_cotangent_ref[lat, lon].astype(F32)
-    grad_merged = dot(onehot(MTOK, 144, of_row=cell_of_merged), cells_ref[...].astype(BF)).astype(BF)
-
     scaled, total, along = [], 0.0, 0.0
     for n in range(4):
-        grad = dot_tn(normed_merge_ref[n], grad_merged).astype(BF)
-        for b in range(3):
-            start = O_MERGE + MLP * b + C * n
-            grads_ref[start : start + C, :] = grad[:, 128 * b : 128 * b + 128]
-        value = rounded(dot_nt(grad_merged, merge_ref[C * n : C * (n + 1), :])) * merge_gain_ref[:, C * n : C * (n + 1)]
+        value = scaled_ref[n]
         total = total + jnp.sum(value, axis=-1, keepdims=True)
         along = along + jnp.sum(value * group_ref[n], axis=-1, keepdims=True)
         scaled.append(value)
@@ -383,11 +381,6 @@
     for part in range(3):
         cols = slice(256 * part, 256 * part + 256)
         grad_up_ref[:, cols] = (rounded(dot(grad_after, down_ref[:, cols])) * slope_ref[:, cols]).astype(BF)
-    grad_down = dot_tn(grad_after, hidden_ref[...]).astype(BF)
-    grad_up = dot_tn(normed_mlp_ref[...], grad_up_ref[...]).astype(BF)
-    for b in range(6):
-        grads_ref[O_DOWN + C * b : O_DOWN + C * (b + 1), :] = grad_down[:, 128 * b : 128 * b + 128]
-        grads_ref[O_UP + C * b : O_UP + C * (b + 1), :] = grad_up[:, 128 * b : 128 * b + 128]
     grad_normed = rounded(dot_nt(grad_up_ref[...], up_ref[...]))
     grad_attn = (
         grad_after.astype(F32)
@@ -395,18 +388,36 @@
     ).astype(BF)
     grad_attn_ref[...] = grad_attn
 
-    grad_proj = dot_tn(mixed_ref[...], grad_attn).astype(BF)
-    grads_ref[O_PROJ : O_PROJ + C, :] = grad_proj[:, :128]
-    grads_ref[O_PROJ_TAIL : O_PROJ_TAIL + C // 2, :] = jnp.concatenate(
-        [grad_proj[: C // 2, 128:], grad_proj[C // 2 :, 128:]], axis=1
-    )
     grad_mixed_ref[...] = dot_nt(grad_attn, proj_ref[...]).astype(BF)
-    ds_corner_ref[...] = jnp.zeros(ds_corner_ref.shape, F32)
+
+    def down_terms():
+        grad = dot_tn(grad_after_ref[...], hidden_ref[...]).astype(BF)
+        for b in range(6):
+            grads_ref[O_DOWN + C * b : O_DOWN + C * (b + 1), :] = grad[:, 128 * b : 128 * b + 128]
+
+    def up_terms():
+        grad = dot_tn(normed_mlp_ref[...], grad_up_ref[...]).astype(BF)
+        for b in range(6):
+            grads_ref[O_UP + C * b : O_UP + C * (b + 1), :] = grad[:, 128 * b : 128 * b + 128]
+
+    def merge_terms():
+        for n in range(4):
+            grad = dot_tn(normed_merge_ref[n], grad_merged_ref[...]).astype(BF)
+            for b in range(3):
+                start = O_MERGE + MLP * b + C * n
+                grads_ref[start : start + C, :] = grad[:, 128 * b : 128 * b + 128]
+
+    def proj_terms():
+        grad_proj = dot_tn(mixed_ref[...], grad_attn_ref[...]).astype(BF)
+        grads_ref[O_PROJ : O_PROJ + C, :] = grad_proj[:, :128]
+        grads_ref[O_PROJ_TAIL : O_PROJ_TAIL + C // 2, :] = jnp.concatenate(
+            [grad_proj[: C // 2, 128:], grad_proj[C // 2 :, 128:]], axis=1
+        )
 
     last_keys = onehot(REST, WIN, of_row=lambda n: n + MAIN)
 
     def attend_back(kind, carry):
-        rows = pl.ds(pl.multiple_of(kind * WIN, 16), WIN)
+        rows = pl.ds(kind * WIN, WIN)
         v, grad = v_ref[rows, :], grad_mixed_ref[rows, :]
         q_turned, k_turned, grad_turned = (jnp.transpose(a) for a in (q_ref[rows, :], k_ref[rows, :], grad))
         products = dot_nt(jnp.concatenate([grad * of_head[h] for h in range(HEADS)], axis=0), v)
@@ -417,10 +428,10 @@
             p = p_ref[th]
             weighted = p * products[WIN * h : WIN * (h + 1)]
             ds = weighted - p * jnp.sum(weighted, axis=-1, keepdims=True)
-            ds_ref[pl.ds(pl.multiple_of(th * WIN, 16), WIN), :] = ds[:, :MAIN]
+            ds_ref[pl.ds(th * WIN, WIN), :] = ds[:, :MAIN]
             ds = ds.astype(BF)
             turned = dot_nt(jnp.concatenate([k_turned[lanes], last_keys], axis=0), ds)
-            at = pl.ds(pl.multiple_of(th * REST, 16), REST)
+            at = pl.ds(th * REST, REST)
             ds_tail_ref[at, :] = turned[HEAD:, :MAIN]
             ds_corner_ref[at, :REST] = turned[HEAD:, MAIN:]
             dq.append(turned[:HEAD])
@@ -430,7 +441,9 @@
         triple_ref[rows, :] = jnp.transpose(triple)
         return carry
 
-    lax.fori_loop(0, TYPES, attend_back, 0, unroll=True)
+    for kind, terms in enumerate((down_terms, up_terms, merge_terms, proj_terms)):
+        attend_back(kind, 0)
+        terms()
     grad_triple = triple_ref[...]
     grad_qkv = dot_tn(tokens_ref[...], grad_triple).astype(BF)
     for b in range(4):
@@ -454,16 +467,16 @@
         return carry + table_terms(index, slab)
 
     table = lax.fori_loop(0, WIN // 8, row_block, jnp.zeros((TROWS, LOW), F32), unroll=9)
-    blank = jnp.zeros((1, LOW - WIN), jnp.int32)
-    for key in range(0, REST, 4):
-        index, slab = [], []
-        for n in range(key, key + 4):
-            index += [turned_ref[n : n + 1, :], blank]
-            slab += [ds_tail_ref[pl.ds(n, TH, stride=REST), :], ds_corner_ref[pl.ds(n, TH, stride=REST), :]]
-        table = table + table_terms(jnp.concatenate(index, axis=1), jnp.concatenate(slab, axis=1))
+    index = jnp.concatenate([turned_ref[n : n + 1, :MAIN] for n in range(REST)], axis=1)
+    slab = jnp.concatenate([ds_tail_ref[pl.ds(n, TH, stride=REST), :] for n in range(REST)], axis=1)
+    table = table + table_terms(index, slab)
+    index = jnp.concatenate([turned_ref[n : n + 1, MAIN:] for n in range(REST)], axis=1)
+    slab = jnp.concatenate([ds_corner_ref[pl.ds(n, TH, stride=REST), :][:, :REST] for n in range(REST)], axis=1)
+    table = table + table_terms(index, slab)
     table = table.astype(BF)
     grads_ref[O_TABLE : O_TABLE + TROWS, :] = table[:, :LANES]
-    grads_ref[O_TABLE + TROWS : O_END, :] = table[:, LANES:]
+    grads_ref[O_TABLE + TROWS : O_END, :] = table[:TLAST, LANES:]
+    grads_ref[O_LAST : O_LAST + TROWS - TLAST, :] = table[TLAST:, LANES:]
     half = keep_ref.shape[0]
     if 2 * half > O_END:
         grads_ref[O_END:, :] = jnp.zeros((2 * half - O_END, LANES), BF)
@@ -479,17 +492,17 @@
         ((TOK, C), F32), ((TOK, C), BF), ((TOK, C), BF), ((TOK, C), BF),
         ((TOK, C), BF), ((TH, WIN, WIN), F32), ((TOK, C), BF),
         ((TOK, C), F32), ((TOK, 1), F32), ((TOK, C), BF), ((TOK, MLP), BF), ((TOK, MLP), F32), ((TOK, C), BF),
-        ((4, MTOK, C), F32), ((4, MTOK, C), BF), ((TOK, C), BF), ((TOK, MLP), BF), ((TOK, C), BF),
+        ((4, MTOK, C), F32), ((TOK, C), BF), ((TOK, MLP), BF), ((TOK, C), BF),
         ((TH * WIN, LANES), F32), ((TH * REST, LANES), F32), ((TH * REST, LANES), F32),
         ((2 * half_rows, LANES), BF), ((REST, WIN), jnp.int32),
-        ((144, 2 * C), F32),
+        ((144, 2 * C), F32), ((MTOK, 2 * C), BF), ((4, MTOK, C), F32),
     ]
     return pl.pallas_call(
         block_kernel,
         out_shape=[
             shape((half_rows, LANES), BF),
             shape((half_rows, LANES), BF),
-            shape((MTOK, 2 * C), BF),
+            shape((4, MTOK, C), BF),
             shape((TOK, 3 * C), BF),
             shape((TOK, C), BF),
             shape((TOK, C), F32),
@@ -505,7 +518,7 @@
 
 
 def cells_kernel(
-    merged_ref, triple_ref, grad_attn_ref, unit_ref, scale_ref, qkv_ref, gain_ref,
+    normed_merge_ref, triple_ref, grad_attn_ref, unit_ref, scale_ref, qkv_ref, gain_ref, merge_ref,
     merged_keep_ref, field_keep_ref, home_ref, x_ref,
 ):
     grad_normed = rounded(dot_nt(triple_ref[...], qkv_ref[...]))
@@ -513,22 +526,22 @@
         grad_normed, unit_ref[...], scale_ref[...], gain_ref[...]
     )
     to_cells = onehot(288, 288, of_col=cell_of_token)
+    leaving = []
     for level in range(LEVELS):
         ordered = jnp.concatenate(
             [x_ref[WIN * kind + 72 * level : WIN * kind + 72 * level + 72, :] for kind in range(TYPES)], axis=0
         )
         cells = dot(to_cells, ordered.astype(BF))
-        home_ref[HALF * level : HALF * (level + 1)] = cells[:144].reshape(HALF, LAT, C).astype(BF)
+        leaving.append(cells[:144])
         field_keep_ref[level] = cells[144:].reshape(HALF, LAT, C).astype(BF)
-    merged_cells = dot(onehot(144, MTOK, of_col=cell_of_merged), merged_ref[...])
+    home_ref[:HALF] = jnp.concatenate(leaving, axis=1).reshape(HALF, LAT, 2 * C).astype(BF)
+    merged = sum(dot(normed_merge_ref[n], merge_ref[C * n : C * (n + 1), :]) for n in range(4))
+    merged_cells = dot(onehot(144, MTOK, of_col=cell_of_merged), merged.astype(BF))
     for lat in range(12):
         for lon in range(HALF // 2):
             row = 72 + (lat * 3 + lon) * 2
             merged_keep_ref[lat, lon] = merged_cells[row : row + 2].astype(BF)
-    for side in range(2):
-        home_ref[12 + 3 * side : 15 + 3 * side] = (
-            merged_cells[:72, C * side : C * (side + 1)].reshape(3, LAT, C).astype(BF)
-        )
+    home_ref[HALF:] = merged_cells[:72].reshape(3, LAT, 2 * C).astype(BF)
 
 
 def to_grid(*args):
@@ -539,9 +552,9 @@
         out_shape=[
             shape((12, HALF // 2, LEVELS, 2 * C), BF),
             shape((LEVELS, HALF, LAT, C), BF),
-            shape((LEVELS * HALF + 6, LAT, C), BF),
+            shape((HALF + 3, LAT, 2 * C), BF),
         ],
-        in_specs=[whole] * 7,
+        in_specs=[whole] * 8,
         out_specs=[whole] * 3,
         scratch_shapes=[pltpu.VMEM((TOK, C), F32)],
         compiler_params=pltpu.CompilerParams(vmem_limit_bytes=12 * 1024 * 1024),
@@ -550,74 +563,143 @@
     )(*args)
 
 
-def finish_kernel(
-    factor, core_ref, held_ref, other_ref, east_ref, merged_keep_ref, field_keep_ref,
-    merged_ref, field_ref, qkv_ref, proj_ref, up_ref, down_ref, merge_ref, table_ref, grads_ref,
-):
-    core = core_ref[0]
-    half = held_ref.shape[0]
-    grads_ref[pl.ds(pl.multiple_of(core * half, 16), half), :] = held_ref[...]
-    grads_ref[pl.ds(pl.multiple_of((1 - core) * half, 16), half), :] = other_ref[...]
-
-    for level in range(LEVELS):
-        field_ref[level, HALF:] = east_ref[HALF * level : HALF * (level + 1)]
-    field_ref[:, :HALF] = field_keep_ref[...]
-    sides = [east_ref[12 + 3 * side : 15 + 3 * side].astype(F32).reshape(72, C) for side in range(2)]
-    cells = jnp.concatenate(sides, axis=1)
-    for lat in range(12):
-        for lon in range(HALF // 2):
-            row = (lat * 3 + lon) * 2
-            merged_ref[lat, HALF // 2 + lon] = cells[row : row + 2].astype(BF)
-    merged_ref[:, : HALF // 2] = merged_keep_ref[...]
-
-    def part(start, rows):
-        return grads_ref[start : start + rows, :].astype(F32) * factor
+def first_half(part, refs, staged, sems):
+    _, _, up_ref, down_ref, qkv_ref, _, _, table_ref = refs
+    up, down, qkv, _, _, table = staged
+    copies = []
+
+    def leaves(source, target):
+        copies.append(pltpu.make_async_copy(source, target, sems.at[len(copies)]))
+        copies[-1].start()
 
     for b in range(6):
-        up_ref[:, 128 * b : 128 * b + 128] = part(O_UP + C * b, C)
-        down_ref[:, 128 * b : 128 * b + 128] = part(O_DOWN + C * b, C)
+        up[:, 128 * b : 128 * b + 128] = part(O_UP + C * b, C)
+    leaves(up, up_ref)
+    for b in range(6):
+        down[:, 128 * b : 128 * b + 128] = part(O_DOWN + C * b, C)
+    leaves(down, down_ref)
+    for b in range(4):
+        qkv[:, 128 * b : 128 * b + 128] = part(O_QKV + C * b, C)
+    tail = part(O_QKV_TAIL, C // 2)
+    qkv[: C // 2, 512:] = tail[:, :64]
+    qkv[C // 2 :, 512:] = tail[:, 64:]
+    leaves(qkv, qkv_ref)
+    last = part(O_LAST, TROWS - TLAST)
+    width = BPOS - LAST
+    for head in range(HEADS):
+        table[head, :, LAST:] = last[head * TYPES : (head + 1) * TYPES, :width]
+    leaves(table.at[:, :, LAST:], table_ref.at[:, :, LAST:])
+    for copy in copies:
+        copy.wait()
+
+
+def second_half(part, refs, staged, sems):
+    _, _, _, _, _, merge_ref, proj_ref, table_ref = refs
+    _, _, _, merge, proj, table = staged
+    copies = []
+
+    def leaves(source, target):
+        copies.append(pltpu.make_async_copy(source, target, sems.at[len(copies)]))
+        copies[-1].start()
+
     for b in range(3):
-        merge_ref[:, 128 * b : 128 * b + 128] = part(O_MERGE + MLP * b, MLP)
-    for b in range(4):
-        qkv_ref[:, 128 * b : 128 * b + 128] = part(O_QKV + C * b, C)
-    tail = part(O_QKV_TAIL, C // 2)
-    qkv_ref[: C // 2, 512:] = tail[:, :64]
-    qkv_ref[C // 2 :, 512:] = tail[:, 64:]
-    proj_ref[:, :128] = part(O_PROJ, C)
+        merge[:, 128 * b : 128 * b + 128] = part(O_MERGE + MLP * b, MLP)
+    leaves(merge, merge_ref)
+    proj[:, :128] = part(O_PROJ, C)
     tail = part(O_PROJ_TAIL, C // 2)
-    proj_ref[: C // 2, 128:] = tail[:, :64]
-    proj_ref[C // 2 :, 128:] = tail[:, 64:]
+    proj[: C // 2, 128:] = tail[:, :64]
+    proj[C // 2 :, 128:] = tail[:, 64:]
+    leaves(proj, proj_ref)
     for side in range(2):
-        table = part(O_TABLE + TROWS * side, TROWS)
-        for high in range(HIGH):
+        terms = part(O_TABLE + TROWS * side, TLAST if side else TROWS)
+        for high in range(HIGH - side):
             start = high * LOW + side * LANES
-            width = min(LANES, BPOS - start)
             for head in range(HEADS):
                 row = high * TH + head * TYPES
-                table_ref[head, :, start : start + width] = table[row : row + TYPES, :width]
+                table[head, :, start : start + LANES] = terms[row : row + TYPES]
+    leaves(table.at[:, :, :LAST], table_ref.at[:, :, :LAST])
+    for copy in copies:
+        copy.wait()
+
+
+def half_kernel(factor, own, core_ref, sums_ref, *refs):
+    if own:
+        outs, scratch = (None, None, *refs[:6]), refs[6:]
+    else:
+        partner_ref, forwarded_ref, merged_keep_ref, field_keep_ref = refs[:4]
+        outs, scratch = refs[10:18], refs[18:]
+    staged, sems = scratch[:6], scratch[6]
+    core = core_ref[0]
+    half = core if own else 1 - core
+    copies = []
+    if not own:
+        merged, field = scratch[7:9]
+        east = jnp.where(core == 0, partner_ref[...].astype(F32), forwarded_ref[...].astype(F32))
+        for level in range(LEVELS):
+            field[level, HALF:] = east[:HALF, :, C * level : C * (level + 1)].astype(BF)
+        field[:, :HALF] = field_keep_ref[...]
+        copies.append(pltpu.make_async_copy(field, outs[1], sems.at[4]))
+        copies[-1].start()
+        cells = east[HALF:].reshape(72, 2 * C)
+        for lat in range(12):
+            for lon in range(HALF // 2):
+                row = (lat * 3 + lon) * 2
+                merged[lat, HALF // 2 + lon] = cells[row : row + 2].astype(BF)
+        merged[:, : HALF // 2] = merged_keep_ref[...]
+        copies.append(pltpu.make_async_copy(merged, outs[0], sems.at[5]))
+        copies[-1].start()
+
+    def part_of(base):
+        return lambda start, rows: sums_ref[start - base : start - base + rows, :].astype(F32) * factor
+
+    @pl.when(half == 0)
+    def _():
+        first_half(part_of(0), outs, staged, sems)
+
+    @pl.when(half == 1)
+    def _():
+        second_half(part_of(O_MERGE), outs, staged, sems)
+
+    for copy in copies:
+        copy.wait()
 
 
 def finish(core, held, other, cells, factor):
     shape = jax.ShapeDtypeStruct
     whole = pl.BlockSpec(memory_space=pltpu.VMEM)
+    scalar = pl.BlockSpec(memory_space=pltpu.SMEM)
+    place = pl.BlockSpec(memory_space=pl.ANY)
+    sums = [
+        shape((C, MLP), F32),
+        shape((C, MLP), F32),
+        shape((C, 3 * C), F32),
+        shape((MLP, 2 * C), F32),
+        shape((C, C), F32),
+        shape((HEADS, TYPES, BPOS), F32),
+    ]
+    scratch = [pltpu.VMEM(item.shape, F32) for item in sums] + [pltpu.SemaphoreType.DMA((6,))]
+    grid = [shape((12, HALF, LEVELS, 2 * C), BF), shape((LEVELS, 2 * HALF, LAT, C), BF)]
+    params = pltpu.CompilerParams(vmem_limit_bytes=16 * 1024 * 1024)
+    begun = pl.pallas_call(
+        lambda *refs: half_kernel(factor, True, *refs),
+        out_shape=sums,
+        in_specs=[scalar, whole],
+        out_specs=[place] * 6,
+        scratch_shapes=scratch,
+        compiler_params=params,
+        cost_estimate=pl.CostEstimate(flops=400_000, bytes_accessed=2_500_000, transcendentals=0),
+        name="finish_own",
+    )(core, held)
     return pl.pallas_call(
-        lambda *refs: finish_kernel(factor, *refs),
-        out_shape=[
-            shape((12, HALF, LEVELS, 2 * C), BF),
-            shape((LEVELS, 2 * HALF, LAT, C), BF),
-            shape((C, 3 * C), F32),
-            shape((C, C), F32),
-            shape((C, MLP), F32),
-            shape((C, MLP), F32),
-            shape((MLP, 2 * C), F32),
-            shape((HEADS, TYPES, BPOS), F32),
-        ],
-        in_specs=[pl.BlockSpec(memory_space=pltpu.SMEM)] + [whole] * 5,
-        out_specs=[whole] * 8,
-        scratch_shapes=[pltpu.VMEM((2 * held.shape[0], LANES), BF)],
-        compiler_params=pltpu.CompilerParams(vmem_limit_bytes=16 * 1024 * 1024),
-        name="finish",
-    )(core, held, other, *cells)
+        lambda *refs: half_kernel(factor, False, *refs),
+        out_shape=[*grid, *sums],
+        in_specs=[scalar] + [whole] * 5 + [place] * 6,
+        out_specs=[place] * 8,
+        scratch_shapes=scratch + [pltpu.VMEM(item.shape, BF) for item in grid],
+        input_output_aliases={6 + n: 2 + n for n in range(6)},
+        compiler_params=params,
+        name="finish_other",
+    )(core, other, *cells, *begun)
 
 
 def passed_along(value, axis, steps):
@@ -633,7 +715,7 @@
     ]
 
 
-def summed_over(keep, send, axis):
+def summed_over(keep, send, axis, partner, forward):
     count = lax.axis_size(axis)
     along = count // (CORES * ACROSS)
     pairs = [(i, i ^ 1) for i in range(count)]
@@ -651,10 +733,12 @@
         return exchanged(jnp.broadcast_to(value[None], (size, *value.shape)), apart, size).reshape(-1, *value.shape[1:])
 
     held = reduced(held, CORES, ACROSS)
+    held, partner = lax.optimization_barrier((held, partner))
     held = reduced(held.reshape(-1, 2, LANES), CORES * ACROSS, along)
     held = gathered(held, CORES * ACROSS, along).reshape(-1, LANES)
     held = gathered(held, CORES, ACROSS)
-    return held, lax.ppermute(held, axis, pairs)
+    held, forwarded = forward(held, partner)
+    return held, lax.ppermute(held, axis, pairs), partner, forwarded
 
 
 def local(
@@ -703,12 +787,17 @@
         bias_tail,
         index,
     )
-    merged_keep, field_keep, home = to_grid(*results, qkv_weight, norm_gain.reshape(1, C))
-    east = passed_along(home, "lon", -1)
-    held, other = summed_over(keep, send, "lon")
+    merged_keep, field_keep, home = to_grid(*results, qkv_weight, norm_gain.reshape(1, C), merge_weight)
+    partner = lax.ppermute(home, "lon", [(i, i ^ 1) for i in range(count)])
+
+    def forward(held, leaving):
+        held, leaving = lax.optimization_barrier((held, leaving))
+        return held, lax.ppermute(leaving, "lon", [(i, (i - CORES) % count) for i in range(1, count, CORES)])
+
+    held, other, partner, forwarded = summed_over(keep, send, "lon", partner, forward)
     factor = float(LEVELS * LAT * fields.shape[2] * count) ** (-0.5)
-    merged, field_grad, qkv_grad, proj_grad, up_grad, down_grad, merge_grad, table_grad = finish(
-        core, held, other, (east, merged_keep, field_keep), factor
+    merged, field_grad, up_grad, down_grad, qkv_grad, merge_grad, proj_grad, table_grad = finish(
+        core, held, other, (partner, forwarded, merged_keep, field_keep), factor
     )
     return (
         merged.transpose(2, 0, 1, 3),

time: 127 us -> 129 us (1.016)
  the two profiles are of different devices: /device:TPU:40 before, /device:TPU:33 now
where the time goes in v4:
time: 129 us; the launch traced here: 128 us
  blocking collectives  46.4 us (36%)
  starting transfers between devices  26.9 us (21%)
  waiting for transfers between devices  25.5 us (20%)
  Pallas kernels  24.7 us (19%)
  other arithmetic  2.6 us (2%)
    all_to_all x3, blocking collectives, exchanged(): lax.all_to_all(value, axis, 0, 0, axis_index_groups=groups_of(count, apar...  46.4 us
    pallas_call x1, Pallas kernels, block(): pl.pallas_call(block_kernel, out_shape=[shape((half_rows, LANES), BF), sh...  14 us
    ppermute x2, waiting for transfers between devices, passed_along(): lax.ppermute(value, axis, [(source, (source + steps) % count) for source...  13.4 us
    all_to_all x1, waiting for transfers between devices, exchanged(): lax.all_to_all(value, axis, 0, 0, axis_index_groups=groups_of(count, apar...  9.24 us
    ppermute x1, starting transfers between devices, summed_over(): arrived = lax.ppermute(send, axis, pairs)  8.02 us
    ppermute x1, starting transfers between devices, summed_over(): return (held, lax.ppermute(held, axis, pairs), partner, forwarded)  6.84 us
    pallas_call x1, Pallas kernels, bias_rows(): pl.pallas_call(bias_kernel, out_shape=[jax.ShapeDtypeStruct((TH * WIN, LA...  5.14 us
    all_to_all x1, starting transfers between devices, exchanged(): lax.all_to_all(value, axis, 0, 0, axis_index_groups=groups_of(count, apar...  4.42 us
  transfers between devices with their start and end apart: 7, of which 5 were waited for; matrix products, arithmetic and copies ran while one was open for 1% of the time, Pallas kernels for 6%

profile of v4, /device:TPU:33, one launch (start us, length us, event | category | flops | bytes accessed | tf_op | source)
XLA Modules:
  0.0 128.4 jit_solution(11007432739759328260)
XLA Ops:
  0.6 1.2 stage.1
  1.8 2.8 %collective-permute-start.1 = (bf16[12,3,2,384]{3,2,1,0:T(2,128)(2,1)S(1)}, bf16[12,3,2,384]{3,2,1,0:T(2,128)(2,1)S(1)}, u32[]{:S(2)}, u32[]{:S(2)}) collective-permute-start(bf16[12,3,2,384]{3,2,1,0:T(2,128)(2,1)S(1)} %get-tuple-element.48), channel_id=1, source_target_pairs={{0,1},{1,2},{2,3},{3,4},{4,5},{5,6},{6,7},{7,8},{8,9},{9,10},{10,1... | collective-permute-start | bytes 165896 | tf_op jit(solution)/shard_map/ppermute | solution.py:707
  4.6 0.1 collective-permute-start
  4.7 0.0 copy-start
  4.7 0.0 copy-start.1
  4.7 0.0 copy-start.2
  4.7 0.0 copy-start.3
  4.7 0.0 copy-start.4
  4.7 0.0 copy-start.5
  4.7 0.0 copy-start.6
  4.8 0.0 copy-start.7
  4.8 0.0 copy-start.8
  4.8 5.1 %bias_rows.1 = (f32[3456,128]{1,0:T(8,128)S(1)}, f32[3456,128]{1,0:T(8,128)S(1)}) custom-call(f32[6,4,3312]{2,1,0:T(4,128)S(1)} %get-tuple-element.50.table_ref, s32[144,144]{1,0:T(8,128)S(1)} %get-tuple-element.51.index_ref, s32[2,24]{1,0:T(2,128)} %regions_ref.1), custom_call_target="tpu_custom_call" | custom-call | flops 14000000000 | bytes 4000000 | tf_op jit(solution)/shard_map/bias_rows/pallas_call | solution.py:253
  9.9 13.1 %collective-permute-done.1.west_cotangent_ref = bf16[12,3,2,384]{3,2,1,0:T(2,128)(2,1)S(1)} collective-permute-done((bf16[12,3,2,384]{3,2,1,0:T(2,128)(2,1)S(1)}, bf16[12,3,2,384]{3,2,1,0:T(2,128)(2,1)S(1)}, u32[]{:S(2)}, u32[]{:S(2)}) %collective-permute-start.1) | collective-permute-done | bytes 55328 | tf_op jit(solution)/shard_map/ppermute | solution.py:707
  23.1 0.3 collective-permute-done.west_ref
  23.3 0.0 copy-done
  23.3 0.0 copy-done.1
  23.3 0.0 copy-done.2
  23.4 0.0 copy-done.3
  23.4 0.0 copy-done.4
  23.4 0.0 copy-done.5
  23.4 0.0 copy-done.6
  23.4 0.0 copy-done.7
  23.4 0.0 copy-done.8
  23.4 14.0 %block.1 = (bf16[3200,128]{1,0:T(8,128)(2,1)S(1)}, bf16[3200,128]{1,0:T(8,128)(2,1)S(1)}, bf16[4,160,192]{2,1,0:T(8,128)(2,1)S(1)}, bf16[576,576]{1,0:T(8,128)(2...) custom-call(s32[1]{0:T(128)} %bitcast.3.core_ref.refs_0_, ...), custom_call_target="tpu_custom_call" | custom-call | flops 24000000000 | bytes 12000000 | tf_op jit(solution)/shard_map/block/pallas_call | solution.py:500
  37.4 0.0 copy-start.9
  37.4 0.0 copy-start.11
  37.5 8.0 %collective-permute-start.2 = (bf16[3200,128]{1,0:T(8,128)(2,1)S(1)}, bf16[3200,128]{1,0:T(8,128)(2,1)S(1)}, u32[]{:S(2)}, u32[]{:S(2)}) collective-permute-start(bf16[3200,128]{1,0:T(8,128)(2,1)S(1)} %get-tuple-element.55), channel_id=1, source_target_pairs={{0,1},{1,0},{2,3},{3,2},{4,5},{5,4},{6,7},{7,6},{8,9},{9,8},{10,11... | collective-permute-start | bytes 2457608 | tf_op jit(solution)/shard_map/ppermute | solution.py:722
  45.5 2.0 %collective-permute-done.2 = bf16[3200,128]{1,0:T(8,128)(2,1)S(1)} collective-permute-done((bf16[3200,128]{1,0:T(8,128)(2,1)S(1)}, bf16[3200,128]{1,0:T(8,128)(2,1)S(1)}, u32[]{:S(2)}, u32[]{:S(2)}) %collective-permute-start.2) | collective-permute-done | bytes 819232 | tf_op jit(solution)/shard_map/ppermute | solution.py:722
  47.4 1.1 add_convert_fusion
  48.5 0.0 copy-done.9
  48.5 0.0 copy-done.11
  48.5 0.0 copy-start.10
  48.5 4.4 %all-to-all-start = ((bf16[4,800,128]{2,1,0:T(8,128)(2,1)}), bf16[4,800,128]{2,1,0:T(8,128)(2,1)}, u32[]{:S(2)}, u32[]{:S(2)}) async-start(bf16[4,800,128]{2,1,0:T(8,128)(2,1)} %bitcast.25), calls=%async_computation | async-start | bytes 1638400 | tf_op jit(solution)/shard_map/all_to_all | solution.py:726
  53.0 0.0 copy-done.10
  53.0 0.0 copy-start.12
  53.0 1.0 copy-done.12
  53.9 1.6 %to_grid.1 = (bf16[12,3,2,384]{3,2,1,0:T(2,128)(2,1)S(1)}, bf16[2,6,24,192]{3,2,1,0:T(8,128)(2,1)S(1)}, bf16[9,24,384]{2,1,0:T(8,128)(2,1)S(1)}) custom-call(bf16[4,160,192]{2,1,0:T(8,128)(2,1)S(1)} %get-tuple-element.56.normed_merge_ref, bf16[576,576]{1,0:T(8,128)(2,1)S(1)} %get-tuple-element.57.triple_ref, bf16[576,192]{1,0:T(8,128)(2,1)S(1)} %copy-done.10, ...), custom_call_target="tpu_custom_call" | custom-call | flops 1500000000 | bytes 3000000 | tf_op jit(solution)/shard_map/to_grid/pallas_call | solution.py:550
  55.6 0.5 collective-permute-start.3
  56.1 9.2 %all-to-all-done = bf16[4,800,128]{2,1,0:T(8,128)(2,1)} async-done(((bf16[4,800,128]{2,1,0:T(8,128)(2,1)}), bf16[4,800,128]{2,1,0:T(8,128)(2,1)}, u32[]{:S(2)}, u32[]{:S(2)}) %all-to-all-start) | async-done | bytes 819232 | tf_op jit(solution)/shard_map/all_to_all | solution.py:726
  65.3 1.3 %reduce_sum.24 = bf16[800,128]{1,0:T(8,128)(2,1)S(1)} reduce(bf16[4,800,128]{2,1,0:T(8,128)(2,1)} %all-to-all-done, bf16[]{:T(256)} %constant.20.clone.1), dimensions={0}, to_apply=%region_0.1 | reduce | flops 307200 | bytes 1024002 | tf_op jit(solution)/shard_map/reduce_sum | solution.py:730
  66.7 0.0 collective-permute-done.3.refs_2_
  66.7 15.1 %all_to_all.20 = bf16[16,25,2,128]{3,2,1,0:T(2,128)(2,1)S(1)} all-to-all(bf16[16,25,2,128]{3,2,1,0:T(2,128)(2,1)S(1)} %bitcast.26), channel_id=1, replica_groups={{0,8,16,24,32,40,48,56,64,72,80,88,96,104,112,120},{1,9,17,25,33,41,49,..., dimensions={0} | all-to-all | bytes 409600 | tf_op jit(solution)/shard_map/all_to_all | solution.py:726
  81.8 0.2 reduce_sum.25
  82.0 0.1 broadcast_in_dim.6
  82.1 20.4 %all_to_all.21 = bf16[16,25,2,128]{3,2,1,0:T(2,128)(2,1)S(1)} all-to-all(bf16[16,25,2,128]{3,2,1,0:T(2,128)(2,1)S(1)} %broadcast_in_dim.6), channel_id=1, replica_groups={{0,8,16,24,32,40,48,56,64,72,80,88,96,104,112,120},{1,9,17,25,33,41,49,..., dimensions={0} | all-to-all | bytes 409600 | tf_op jit(solution)/shard_map/all_to_all | solution.py:726
  102.5 0.1 broadcast_in_dim.15
  102.6 10.9 %all_to_all.22 = bf16[4,800,128]{2,1,0:T(8,128)(2,1)S(1)} all-to-all(bf16[4,800,128]{2,1,0:T(8,128)(2,1)S(1)} %broadcast_in_dim.15), channel_id=1, replica_groups={{0,2,4,6},{1,3,5,7},{8,10,12,14},{9,11,13,15},{16,18,20,22},{17,19,21,2..., dimensions={0} | all-to-all | bytes 1638400 | tf_op jit(solution)/shard_map/all_to_all | solution.py:726
  113.5 6.8 %collective-permute-start.4 = (bf16[3200,128]{1,0:T(8,128)(2,1)S(1)}, bf16[3200,128]{1,0:T(8,128)(2,1)S(1)}, u32[]{:S(2)}, u32[]{:S(2)}) collective-permute-start(bf16[3200,128]{1,0:T(8,128)(2,1)S(1)} %bitcast.15), channel_id=1, source_target_pairs={{0,1},{1,0},{2,3},{3,2},{4,5},{5,4},{6,7},{7,6},{8,9},{9,8},{10,11... | collective-permute-start | bytes 2457608 | tf_op jit(solution)/shard_map/ppermute | solution.py:741
  120.4 4.2 %collective-permute-start.5 = (bf16[9,24,384]{2,1,0:T(8,128)(2,1)S(1)}, bf16[9,24,384]{2,1,0:T(8,128)(2,1)S(1)}, u32[]{:S(2)}, u32[]{:S(2)}) collective-permute-start(bf16[9,24,384]{2,1,0:T(8,128)(2,1)S(1)} %collective-permute-done.3.refs_2_), channel_id=1, source_target_pairs={{1,127},{3,1},{5,3},{7,5},{9,7},{11,9},{13,11},{15,13},{17,15},{19... | collective-permute-start | bytes 497672 | tf_op jit(solution)/shard_map/ppermute | solution.py:795
  124.5 1.3 %finish_own.1 = (f32[192,768]{1,0:T(8,128)}, f32[192,768]{1,0:T(8,128)}, f32[192,576]{1,0:T(8,128)}, f32[768,384]{1,0:T(8,128)}, f32[192,192]{1,0:T(8,128)}, /*index=5*/f32[6,4,3312]{2,1,0:T(4,128)}) custom-call(s32[1]{0:T(128)} %bitcast.3.core_ref.refs_0_, bf16[3200,128]{1,0:T(8,128)(2,1)S(1)} %bitcast.16), custom_call_target="tpu_custom_call" | custom-call | flops 400000 | bytes 2500000 | tf_op jit(solution)/shard_map/finish_own/pallas_call | solution.py:683
  125.9 0.9 collective-permute-done.5.refs_3_
  126.8 0.0 collective-permute-done.4.refs_1_
  126.8 1.5 %finish_other.1 = (bf16[12,6,2,384]{3,2,1,0:T(2,128)(2,1)}, bf16[2,12,24,192]{3,2,1,0:T(8,128)(2,1)}, f32[192,768]{1,0:T(8,128)}, f32[192,768]{1,0:T(8,128)}, f3...) custom-call(s32[1]{0:T(128)} %bitcast.3.core_ref.refs_0_, ...), custom_call_target="tpu_custom_call", output_to_operand_aliasing={{2}: (6, {}), {3}: (7, {}), {4}: (8, {}), {5}: (9, {}), {6}... | custom-call | tf_op jit(solution)/shard_map/finish_other/pallas_call | solution.py:693
Async XLA Ops:
  1.8 21.3 %collective-permute-start.1 = (bf16[12,3,2,384]{3,2,1,0:T(2,128)(2,1)S(1)}, bf16[12,3,2,384]{3,2,1,0:T(2,128)(2,1)S(1)}, u32[]{:S(2)}, u32[]{:S(2)}) collective-permute-start(bf16[12,3,2,384]{3,2,1,0:T(2,128)(2,1)S(1)} %get-tuple-element.48), channel_id=1, source_target_pairs={{0,1},{1,2},{2,3},{3,4},{4,5},{5,6},{6,7},{7,8},{8,9},{9,10},{10,1... | collective-permute-start | bytes 165896 | tf_op jit(solution)/shard_map/ppermute | solution.py:707
  4.6 18.8 %collective-permute-start = (bf16[2,6,24,192]{3,2,1,0:T(8,128)(2,1)S(1)}, bf16[2,6,24,192]{3,2,1,0:T(8,128)(2,1)S(1)}, u32[]{:S(2)}, u32[]{:S(2)}) collective-permute-start(bf16[2,6,24,192]{3,2,1,0:T(8,128)(2,1)S(1)} %get-tuple-element.47), channel_id=1, source_target_pairs={{0,1},{1,2},{2,3},{3,4},{4,5},{5,6},{6,7},{7,8},{8,9},{9,10},{10,1... | collective-permute-start | bytes 331784 | tf_op jit(solution)/shard_map/ppermute | solution.py:707
  4.7 18.6 %copy-start = (bf16[2,24,12,192]{3,1,2,0:T(8,128)(2,1)S(1)}, bf16[2,24,12,192]{3,1,2,0:T(8,128)(2,1)}, u32[]{:S(2)}) copy-start(bf16[2,24,12,192]{3,1,2,0:T(8,128)(2,1)} %param.13) | copy-start | bytes 663556
  4.7 18.6 %copy-start.1 = (bf16[2,12,6,384]{3,0,2,1:T(2,128)(2,1)S(1)}, bf16[2,12,6,384]{3,0,2,1:T(2,128)(2,1)}, u32[]{:S(2)}) copy-start(bf16[2,12,6,384]{3,0,2,1:T(2,128)(2,1)} %param.25) | copy-start | bytes 331780
  4.7 18.6 %copy-start.2 = (bf16[768,384]{1,0:T(8,128)(2,1)S(1)}, bf16[768,384]{1,0:T(8,128)(2,1)}, u32[]{:S(2)}) copy-start(bf16[768,384]{1,0:T(8,128)(2,1)} %merge_ref.3) | copy-start | bytes 1769476
  4.7 18.6 %copy-start.3 = (bf16[192,768]{1,0:T(8,128)(2,1)S(1)}, bf16[192,768]{1,0:T(8,128)(2,1)}, u32[]{:S(2)}) copy-start(bf16[192,768]{1,0:T(8,128)(2,1)} %up_ref.1) | copy-start | bytes 884740
  4.7 18.6 %copy-start.4 = (bf16[768,192]{0,1:T(8,128)(2,1)S(1)}, bf16[768,192]{0,1:T(8,128)(2,1)}, u32[]{:S(2)}) copy-start(bf16[768,192]{0,1:T(8,128)(2,1)} %param.22) | copy-start | bytes 884740
  4.7 18.6 %copy-start.5 = (bf16[192,576]{1,0:T(8,128)(2,1)S(1)}, bf16[192,576]{1,0:T(8,128)(2,1)}, u32[]{:S(2)}) copy-start(bf16[192,576]{1,0:T(8,128)(2,1)} %qkv_ref.3) | copy-start | bytes 663556
  4.7 18.6 %copy-start.6 = (bf16[192,192]{1,0:T(8,128)(2,1)S(1)}, bf16[192,192]{1,0:T(8,128)(2,1)}, u32[]{:S(2)}) copy-start(bf16[192,192]{1,0:T(8,128)(2,1)} %proj_ref.1) | copy-start | bytes 221188
  4.8 18.6 %copy-start.7 = (f32[192]{0:T(256)S(1)}, f32[192]{0:T(256)}, u32[]{:S(2)}) copy-start(f32[192]{0:T(256)} %param.20) | copy-start | bytes 2308
  4.8 18.6 %copy-start.8 = (f32[192]{0:T(256)S(1)}, f32[192]{0:T(256)}, u32[]{:S(2)}) copy-start(f32[192]{0:T(256)} %param.14) | copy-start | bytes 2308
  37.4 11.1 %copy-start.9 = (bf16[576,192]{1,0:T(8,128)(2,1)}, bf16[576,192]{1,0:T(8,128)(2,1)S(1)}, u32[]{:S(2)}) copy-start(bf16[576,192]{1,0:T(8,128)(2,1)S(1)} %get-tuple-element.58.grad_attn_ref) | copy-start | bytes 663556
  37.4 11.1 %copy-start.11 = (f32[576,1]{1,0:T(8,128)}, f32[576,1]{1,0:T(8,128)S(1)}, u32[]{:S(2)}) copy-start(f32[576,1]{1,0:T(8,128)S(1)} %get-tuple-element.60.scale_ref) | copy-start | bytes 6916
  37.5 10.0 %collective-permute-start.2 = (bf16[3200,128]{1,0:T(8,128)(2,1)S(1)}, bf16[3200,128]{1,0:T(8,128)(2,1)S(1)}, u32[]{:S(2)}, u32[]{:S(2)}) collective-permute-start(bf16[3200,128]{1,0:T(8,128)(2,1)S(1)} %get-tuple-element.55), channel_id=1, source_target_pairs={{0,1},{1,0},{2,3},{3,2},{4,5},{5,4},{6,7},{7,6},{8,9},{9,8},{10,11... | collective-permute-start | bytes 2457608 | tf_op jit(solution)/shard_map/ppermute | solution.py:722
  48.5 4.4 %copy-start.10 = (bf16[576,192]{1,0:T(8,128)(2,1)S(1)}, bf16[576,192]{1,0:T(8,128)(2,1)}, u32[]{:S(2)}) copy-start(bf16[576,192]{1,0:T(8,128)(2,1)} %copy-done.9) | copy-start | bytes 663556
  48.5 16.8 %all-to-all-start = ((bf16[4,800,128]{2,1,0:T(8,128)(2,1)}), bf16[4,800,128]{2,1,0:T(8,128)(2,1)}, u32[]{:S(2)}, u32[]{:S(2)}) async-start(bf16[4,800,128]{2,1,0:T(8,128)(2,1)} %bitcast.25), calls=%async_computation | async-start | bytes 1638400 | tf_op jit(solution)/shard_map/all_to_all | solution.py:726
  53.0 1.0 copy-start.12
  55.6 11.1 %collective-permute-start.3 = (bf16[9,24,384]{2,1,0:T(8,128)(2,1)S(1)}, bf16[9,24,384]{2,1,0:T(8,128)(2,1)S(1)}, u32[]{:S(2)}, u32[]{:S(2)}) collective-permute-start(bf16[9,24,384]{2,1,0:T(8,128)(2,1)S(1)} %get-tuple-element.61), channel_id=1, source_target_pairs={{0,1},{1,0},{2,3},{3,2},{4,5},{5,4},{6,7},{7,6},{8,9},{9,8},{10,11... | collective-permute-start | bytes 497672 | tf_op jit(solution)/shard_map/ppermute | solution.py:791
  113.5 13.3 %collective-permute-start.4 = (bf16[3200,128]{1,0:T(8,128)(2,1)S(1)}, bf16[3200,128]{1,0:T(8,128)(2,1)S(1)}, u32[]{:S(2)}, u32[]{:S(2)}) collective-permute-start(bf16[3200,128]{1,0:T(8,128)(2,1)S(1)} %bitcast.15), channel_id=1, source_target_pairs={{0,1},{1,0},{2,3},{3,2},{4,5},{5,4},{6,7},{7,6},{8,9},{9,8},{10,11... | collective-permute-start | bytes 2457608 | tf_op jit(solution)/shard_map/ppermute | solution.py:741
  120.4 6.5 %collective-permute-start.5 = (bf16[9,24,384]{2,1,0:T(8,128)(2,1)S(1)}, bf16[9,24,384]{2,1,0:T(8,128)(2,1)S(1)}, u32[]{:S(2)}, u32[]{:S(2)}) collective-permute-start(bf16[9,24,384]{2,1,0:T(8,128)(2,1)S(1)} %collective-permute-done.3.refs_2_), channel_id=1, source_target_pairs={{1,127},{3,1},{5,3},{7,5},{9,7},{11,9},{13,11},{15,13},{17,15},{19... | collective-permute-start | bytes 497672 | tf_op jit(solution)/shard_map/ppermute | solution.py:795

commit v5 on v4

--- a/solution.py
+++ b/solution.py
@@ -31,18 +31,21 @@
 ACROSS = 4
 
 TROWS = 320
-TLAST = (HIGH - 1) * TH
-LAST = (HIGH - 1) * LOW + LANES
+MSPLIT = 512
 O_UP = 0
-O_DOWN = O_UP + 6 * C
-O_QKV = O_DOWN + 6 * C
+O_QKV = O_UP + 6 * C
 O_QKV_TAIL = O_QKV + 4 * C
-O_LAST = O_QKV_TAIL + C // 2
-O_MERGE = O_LAST + TROWS - TLAST
-O_PROJ = O_MERGE + 3 * MLP
+O_PROJ = O_QKV_TAIL + C // 2
 O_PROJ_TAIL = O_PROJ + C
 O_TABLE = O_PROJ_TAIL + C // 2
-O_END = O_TABLE + TROWS + TLAST
+O_MERGE_LAST = O_TABLE + 2 * TROWS
+O_MERGE = O_MERGE_LAST + MLP - MSPLIT
+O_DOWN = O_MERGE + 2 * MLP + MSPLIT
+O_END = O_DOWN + 6 * C
+
+DS_TAIL = TH * WIN
+DS_CORNER = DS_TAIL + TH * REST
+DS_END = DS_CORNER + TH * REST
 
 
 def dot(a, b):
@@ -270,14 +273,14 @@
 
 
 def block_kernel(
-    core_ref, own_ref, west_ref, own_cotangent_ref, west_cotangent_ref,
+    own_ref, west_ref, own_cotangent_ref, west_cotangent_ref,
     norm_gain_ref, qkv_ref, proj_ref, mlp_gain_ref, up_ref, down_ref, merge_gain_ref, merge_ref,
-    bias_ref, bias_tail_ref, index_ref,
-    keep_ref, send_ref, normed_merge_ref, triple_ref, grad_attn_ref, unit_ref, scale_ref,
-    x_ref, tokens_ref, q_ref, k_ref, v_ref, p_ref, mixed_ref,
+    bias_ref, bias_tail_ref,
+    grads_ref, tokens_ref, ds_ref, normed_merge_ref, triple_ref, grad_attn_ref, unit_ref, scale_ref,
+    x_ref, q_ref, k_ref, v_ref, p_ref, mixed_ref,
     unit_mlp_ref, scale_mlp_ref, normed_mlp_ref, hidden_ref, slope_ref, after_mlp_ref,
     group_ref, grad_after_ref, grad_up_ref, grad_mixed_ref,
-    ds_ref, ds_tail_ref, ds_corner_ref, grads_ref, turned_ref, cells_ref, grad_merged_ref, scaled_ref,
+    cells_ref, grad_merged_ref, scaled_ref,
 ):
     to_tokens = onehot(288, 288, of_row=cell_of_token)
     for level in range(LEVELS):
@@ -403,9 +406,16 @@
     def merge_terms():
         for n in range(4):
             grad = dot_tn(normed_merge_ref[n], grad_merged_ref[...]).astype(BF)
-            for b in range(3):
+            for b in range(2):
                 start = O_MERGE + MLP * b + C * n
                 grads_ref[start : start + C, :] = grad[:, 128 * b : 128 * b + 128]
+            kept = max(0, min(C, MSPLIT - C * n))
+            if kept:
+                start = O_MERGE + 2 * MLP + C * n
+                grads_ref[start : start + kept, :] = grad[:kept, 256:]
+            if kept < C:
+                start = O_MERGE_LAST + C * n + kept - MSPLIT
+                grads_ref[start : start + C - kept, :] = grad[kept:, 256:]
 
     def proj_terms():
         grad_proj = dot_tn(mixed_ref[...], grad_attn_ref[...]).astype(BF)
@@ -415,6 +425,9 @@
         )
 
     last_keys = onehot(REST, WIN, of_row=lambda n: n + MAIN)
+    ds_ref[DS_CORNER:, :] = jnp.zeros((TH * REST, LANES), BF)
+    grads_ref[O_QKV:O_PROJ, :] = jnp.zeros((O_PROJ - O_QKV, LANES), BF)
+    grads_ref[O_TABLE:O_MERGE_LAST, :] = jnp.zeros((O_MERGE_LAST - O_TABLE, LANES), BF)
 
     def attend_back(kind, carry):
         rows = pl.ds(kind * WIN, WIN)
@@ -428,12 +441,12 @@
             p = p_ref[th]
             weighted = p * products[WIN * h : WIN * (h + 1)]
             ds = weighted - p * jnp.sum(weighted, axis=-1, keepdims=True)
+            ds = ds.astype(BF)
             ds_ref[pl.ds(th * WIN, WIN), :] = ds[:, :MAIN]
-            ds = ds.astype(BF)
             turned = dot_nt(jnp.concatenate([k_turned[lanes], last_keys], axis=0), ds)
-            at = pl.ds(th * REST, REST)
-            ds_tail_ref[at, :] = turned[HEAD:, :MAIN]
-            ds_corner_ref[at, :REST] = turned[HEAD:, MAIN:]
+            tail = turned[HEAD:].astype(BF)
+            ds_ref[pl.ds(DS_TAIL + th * REST, REST), :] = tail[:, :MAIN]
+            ds_ref[pl.ds(DS_CORNER + th * REST, REST), :REST] = tail[:, MAIN:]
             dq.append(turned[:HEAD])
             dk.append(dot(q_turned[lanes], ds))
             dv.append(dot(grad_turned[lanes], p.astype(BF)))
@@ -444,15 +457,70 @@
     for kind, terms in enumerate((down_terms, up_terms, merge_terms, proj_terms)):
         attend_back(kind, 0)
         terms()
-    grad_triple = triple_ref[...]
-    grad_qkv = dot_tn(tokens_ref[...], grad_triple).astype(BF)
-    for b in range(4):
-        grads_ref[O_QKV + C * b : O_QKV + C * (b + 1), :] = grad_qkv[:, 128 * b : 128 * b + 128]
-    grads_ref[O_QKV_TAIL : O_QKV_TAIL + C // 2, :] = jnp.concatenate(
-        [grad_qkv[: C // 2, 512:], grad_qkv[C // 2 :, 512:]], axis=1
-    )
-    turned_ref[...] = jnp.transpose(index_ref[:, MAIN:])
-
+
+
+def block(half_rows, *args):
+    shape = jax.ShapeDtypeStruct
+    whole = pl.BlockSpec(memory_space=pltpu.VMEM)
+    scratch = [
+        ((TOK, C), F32), ((TOK, C), BF), ((TOK, C), BF),
+        ((TOK, C), BF), ((TH, WIN, WIN), F32), ((TOK, C), BF),
+        ((TOK, C), F32), ((TOK, 1), F32), ((TOK, C), BF), ((TOK, MLP), BF), ((TOK, MLP), F32), ((TOK, C), BF),
+        ((4, MTOK, C), F32), ((TOK, C), BF), ((TOK, MLP), BF), ((TOK, C), BF),
+        ((144, 2 * C), F32), ((MTOK, 2 * C), BF), ((4, MTOK, C), F32),
+    ]
+    return pl.pallas_call(
+        block_kernel,
+        out_shape=[
+            shape((2 * half_rows, LANES), BF),
+            shape((TOK, C), BF),
+            shape((DS_END, LANES), BF),
+            shape((4, MTOK, C), BF),
+            shape((TOK, 3 * C), BF),
+            shape((TOK, C), BF),
+            shape((TOK, C), F32),
+            shape((TOK, 1), F32),
+        ],
+        in_specs=[whole] * len(args),
+        out_specs=[whole] * 8,
+        scratch_shapes=[pltpu.VMEM(*item) for item in scratch],
+        compiler_params=pltpu.CompilerParams(vmem_limit_bytes=24 * 1024 * 1024),
+        cost_estimate=pl.CostEstimate(flops=24_000_000_000, bytes_accessed=12_000_000, transcendentals=2_000_000),
+        name="block",
+    )(*args)
+
+
+def pack_kernel(core_ref, grads_ref, tokens_ref, triple_ref, keep_ref, send_ref):
+    half = keep_ref.shape[0]
+    core = core_ref[0]
+    grad_qkv = dot_tn(tokens_ref[...], triple_ref[...]).astype(BF)
+    tail = jnp.concatenate([grad_qkv[: C // 2, 512:], grad_qkv[C // 2 :, 512:]], axis=1)
+    keep_ref[...] = grads_ref[pl.ds(pl.multiple_of(core * half, 16), half), :]
+    send_ref[...] = grads_ref[pl.ds(pl.multiple_of((1 - core) * half, 16), half), :]
+    for owner, target_ref in ((0, keep_ref), (1, send_ref)):
+
+        @pl.when(core == owner)
+        def _():
+            for b in range(4):
+                target_ref[O_QKV + C * b : O_QKV + C * (b + 1), :] = grad_qkv[:, 128 * b : 128 * b + 128]
+            target_ref[O_QKV_TAIL : O_QKV_TAIL + C // 2, :] = tail
+
+
+def pack(core, grads, tokens, triple):
+    half = jax.ShapeDtypeStruct((grads.shape[0] // 2, LANES), BF)
+    whole = pl.BlockSpec(memory_space=pltpu.VMEM)
+    return pl.pallas_call(
+        pack_kernel,
+        out_shape=[half, half],
+        in_specs=[pl.BlockSpec(memory_space=pltpu.SMEM)] + [whole] * 3,
+        out_specs=[whole] * 2,
+        compiler_params=pltpu.CompilerParams(vmem_limit_bytes=12 * 1024 * 1024),
+        cost_estimate=pl.CostEstimate(flops=600_000_000, bytes_accessed=4_000_000, transcendentals=0),
+        name="pack",
+    )(core, grads, tokens, triple)
+
+
+def table_kernel(core_ref, own_ref, partner_ref, index_ref, table_ref, ds_ref, turned_ref):
     def table_terms(index, slab):
         high_row = index >> 8
         spread = [jnp.where(high_row == n, slab, 0.0) for n in range(HIGH)]
@@ -466,55 +534,60 @@
         slab = jnp.concatenate([ds_ref[pl.ds(base + n, TH, stride=WIN), :] for n in range(8)], axis=1)
         return carry + table_terms(index, slab)
 
-    table = lax.fori_loop(0, WIN // 8, row_block, jnp.zeros((TROWS, LOW), F32), unroll=9)
-    index = jnp.concatenate([turned_ref[n : n + 1, :MAIN] for n in range(REST)], axis=1)
-    slab = jnp.concatenate([ds_tail_ref[pl.ds(n, TH, stride=REST), :] for n in range(REST)], axis=1)
-    table = table + table_terms(index, slab)
-    index = jnp.concatenate([turned_ref[n : n + 1, MAIN:] for n in range(REST)], axis=1)
-    slab = jnp.concatenate([ds_corner_ref[pl.ds(n, TH, stride=REST), :][:, :REST] for n in range(REST)], axis=1)
-    table = table + table_terms(index, slab)
-    table = table.astype(BF)
-    grads_ref[O_TABLE : O_TABLE + TROWS, :] = table[:, :LANES]
-    grads_ref[O_TABLE + TROWS : O_END, :] = table[:TLAST, LANES:]
-    grads_ref[O_LAST : O_LAST + TROWS - TLAST, :] = table[TLAST:, LANES:]
-    half = keep_ref.shape[0]
-    if 2 * half > O_END:
-        grads_ref[O_END:, :] = jnp.zeros((2 * half - O_END, LANES), BF)
-    core = core_ref[0]
-    keep_ref[...] = grads_ref[pl.ds(pl.multiple_of(core * half, 16), half), :]
-    send_ref[...] = grads_ref[pl.ds(pl.multiple_of((1 - core) * half, 16), half), :]
-
-
-def block(half_rows, *args):
-    shape = jax.ShapeDtypeStruct
+    @pl.when(core_ref[0] == 0)
+    def _():
+        ds_ref[...] = own_ref[...].astype(F32) + partner_ref[...].astype(F32)
+        turned_ref[...] = jnp.transpose(index_ref[:, MAIN:])
+        table = lax.fori_loop(0, WIN // 8, row_block, jnp.zeros((TROWS, LOW), F32), unroll=9)
+        index = jnp.concatenate([turned_ref[n : n + 1, :MAIN] for n in range(REST)], axis=1)
+        slab = jnp.concatenate([ds_ref[pl.ds(DS_TAIL + n, TH, stride=REST), :] for n in range(REST)], axis=1)
+        table = table + table_terms(index, slab)
+        index = jnp.concatenate([turned_ref[n : n + 1, MAIN:] for n in range(REST)], axis=1)
+        slab = jnp.concatenate(
+            [ds_ref[pl.ds(DS_CORNER + n, TH, stride=REST), :][:, :REST] for n in range(REST)], axis=1
+        )
+        table = (table + table_terms(index, slab)).astype(BF)
+        table_ref[:TROWS, :] = table[:, :LANES]
+        table_ref[TROWS:, :] = table[:, LANES:]
+
+    @pl.when(core_ref[0] == 1)
+    def _():
+        table_ref[...] = jnp.zeros(table_ref.shape, BF)
+
+
+def table_sum(core, own, partner, index):
     whole = pl.BlockSpec(memory_space=pltpu.VMEM)
-    scratch = [
-        ((TOK, C), F32), ((TOK, C), BF), ((TOK, C), BF), ((TOK, C), BF),
-        ((TOK, C), BF), ((TH, WIN, WIN), F32), ((TOK, C), BF),
-        ((TOK, C), F32), ((TOK, 1), F32), ((TOK, C), BF), ((TOK, MLP), BF), ((TOK, MLP), F32), ((TOK, C), BF),
-        ((4, MTOK, C), F32), ((TOK, C), BF), ((TOK, MLP), BF), ((TOK, C), BF),
-        ((TH * WIN, LANES), F32), ((TH * REST, LANES), F32), ((TH * REST, LANES), F32),
-        ((2 * half_rows, LANES), BF), ((REST, WIN), jnp.int32),
-        ((144, 2 * C), F32), ((MTOK, 2 * C), BF), ((4, MTOK, C), F32),
-    ]
     return pl.pallas_call(
-        block_kernel,
-        out_shape=[
-            shape((half_rows, LANES), BF),
-            shape((half_rows, LANES), BF),
-            shape((4, MTOK, C), BF),
-            shape((TOK, 3 * C), BF),
-            shape((TOK, C), BF),
-            shape((TOK, C), F32),
-            shape((TOK, 1), F32),
-        ],
-        in_specs=[pl.BlockSpec(memory_space=pltpu.SMEM)] + [whole] * (len(args) - 1),
-        out_specs=[whole] * 7,
-        scratch_shapes=[pltpu.VMEM(*item) for item in scratch],
-        compiler_params=pltpu.CompilerParams(vmem_limit_bytes=24 * 1024 * 1024),
-        cost_estimate=pl.CostEstimate(flops=24_000_000_000, bytes_accessed=12_000_000, transcendentals=2_000_000),
-        name="block",
-    )(*args)
+        table_kernel,
+        out_shape=jax.ShapeDtypeStruct((2 * TROWS, LANES), BF),
+        in_specs=[pl.BlockSpec(memory_space=pltpu.SMEM)] + [whole] * 3,
+        out_specs=whole,
+        scratch_shapes=[pltpu.VMEM((DS_END, LANES), F32), pltpu.VMEM((REST, WIN), jnp.int32)],
+        compiler_params=pltpu.CompilerParams(vmem_limit_bytes=12 * 1024 * 1024),
+        cost_estimate=pl.CostEstimate(flops=4_000_000_000, bytes_accessed=3_000_000, transcendentals=0),
+        name="table_sum",
+    )(core, own, partner, index)
+
+
+def join_kernel(core_ref, keep_ref, arrived_ref, table_ref, held_ref):
+    held_ref[...] = (keep_ref[...].astype(F32) + arrived_ref[...].astype(F32)).astype(BF)
+
+    @pl.when(core_ref[0] == 0)
+    def _():
+        held_ref[O_TABLE : O_TABLE + 2 * TROWS, :] = table_ref[...]
+
+
+def join(core, keep, arrived, table):
+    whole = pl.BlockSpec(memory_space=pltpu.VMEM)
+    return pl.pallas_call(
+        join_kernel,
+        out_shape=jax.ShapeDtypeStruct(keep.shape, BF),
+        in_specs=[pl.BlockSpec(memory_space=pltpu.SMEM)] + [whole] * 3,
+        out_specs=whole,
+        compiler_params=pltpu.CompilerParams(vmem_limit_bytes=8 * 1024 * 1024),
+        cost_estimate=pl.CostEstimate(flops=400_000, bytes_accessed=2_500_000, transcendentals=0),
+        name="join",
+    )(core, keep, arrived, table)
 
 
 def cells_kernel(
@@ -563,63 +636,47 @@
     )(*args)
 
 
-def first_half(part, refs, staged, sems):
-    _, _, up_ref, down_ref, qkv_ref, _, _, table_ref = refs
-    up, down, qkv, _, _, table = staged
-    copies = []
-
-    def leaves(source, target):
-        copies.append(pltpu.make_async_copy(source, target, sems.at[len(copies)]))
-        copies[-1].start()
-
+def first_half(part, refs, staged, leaves):
+    _, _, up_ref, _, qkv_ref, merge_ref, proj_ref, table_ref = refs
+    up, _, qkv, merge, proj, table = staged
     for b in range(6):
         up[:, 128 * b : 128 * b + 128] = part(O_UP + C * b, C)
     leaves(up, up_ref)
-    for b in range(6):
-        down[:, 128 * b : 128 * b + 128] = part(O_DOWN + C * b, C)
-    leaves(down, down_ref)
     for b in range(4):
         qkv[:, 128 * b : 128 * b + 128] = part(O_QKV + C * b, C)
     tail = part(O_QKV_TAIL, C // 2)
     qkv[: C // 2, 512:] = tail[:, :64]
     qkv[C // 2 :, 512:] = tail[:, 64:]
     leaves(qkv, qkv_ref)
-    last = part(O_LAST, TROWS - TLAST)
-    width = BPOS - LAST
-    for head in range(HEADS):
-        table[head, :, LAST:] = last[head * TYPES : (head + 1) * TYPES, :width]
-    leaves(table.at[:, :, LAST:], table_ref.at[:, :, LAST:])
-    for copy in copies:
-        copy.wait()
-
-
-def second_half(part, refs, staged, sems):
-    _, _, _, _, _, merge_ref, proj_ref, table_ref = refs
-    _, _, _, merge, proj, table = staged
-    copies = []
-
-    def leaves(source, target):
-        copies.append(pltpu.make_async_copy(source, target, sems.at[len(copies)]))
-        copies[-1].start()
-
-    for b in range(3):
-        merge[:, 128 * b : 128 * b + 128] = part(O_MERGE + MLP * b, MLP)
-    leaves(merge, merge_ref)
+    for side in range(2):
+        terms = part(O_TABLE + TROWS * side, TROWS)
+        for high in range(HIGH):
+            start = high * LOW + side * LANES
+            width = min(LANES, BPOS - start)
+            for head in range(HEADS):
+                row = high * TH + head * TYPES
+                table[head, :, start : start + width] = terms[row : row + TYPES, :width]
+    leaves(table, table_ref)
     proj[:, :128] = part(O_PROJ, C)
     tail = part(O_PROJ_TAIL, C // 2)
     proj[: C // 2, 128:] = tail[:, :64]
     proj[C // 2 :, 128:] = tail[:, 64:]
     leaves(proj, proj_ref)
-    for side in range(2):
-        terms = part(O_TABLE + TROWS * side, TLAST if side else TROWS)
-        for high in range(HIGH - side):
-            start = high * LOW + side * LANES
-            for head in range(HEADS):
-                row = high * TH + head * TYPES
-                table[head, :, start : start + LANES] = terms[row : row + TYPES]
-    leaves(table.at[:, :, :LAST], table_ref.at[:, :, :LAST])
-    for copy in copies:
-        copy.wait()
+    merge[MSPLIT:, 256:] = part(O_MERGE_LAST, MLP - MSPLIT)
+    leaves(merge.at[MSPLIT:, 256:], merge_ref.at[MSPLIT:, 256:])
+
+
+def second_half(part, refs, staged, leaves):
+    _, _, _, down_ref, _, merge_ref, _, _ = refs
+    _, down, _, merge, _, _ = staged
+    for b in range(2):
+        merge[:, 128 * b : 128 * b + 128] = part(O_MERGE + MLP * b, MLP)
+    leaves(merge.at[:, :256], merge_ref.at[:, :256])
+    for b in range(6):
+        down[:, 128 * b : 128 * b + 128] = part(O_DOWN + C * b, C)
+    leaves(down, down_ref)
+    merge[:MSPLIT, 256:] = part(O_MERGE + 2 * MLP, MSPLIT)
+    leaves(merge.at[:MSPLIT, 256:], merge_ref.at[:MSPLIT, 256:])
 
 
 def half_kernel(factor, own, core_ref, sums_ref, *refs):
@@ -638,7 +695,7 @@
         for level in range(LEVELS):
             field[level, HALF:] = east[:HALF, :, C * level : C * (level + 1)].astype(BF)
         field[:, :HALF] = field_keep_ref[...]
-        copies.append(pltpu.make_async_copy(field, outs[1], sems.at[4]))
+        copies.append(pltpu.make_async_copy(field, outs[1], sems.at[5]))
         copies[-1].start()
         cells = east[HALF:].reshape(72, 2 * C)
         for lat in range(12):
@@ -646,19 +703,25 @@
                 row = (lat * 3 + lon) * 2
                 merged[lat, HALF // 2 + lon] = cells[row : row + 2].astype(BF)
         merged[:, : HALF // 2] = merged_keep_ref[...]
-        copies.append(pltpu.make_async_copy(merged, outs[0], sems.at[5]))
+        copies.append(pltpu.make_async_copy(merged, outs[0], sems.at[6]))
         copies[-1].start()
 
     def part_of(base):
         return lambda start, rows: sums_ref[start - base : start - base + rows, :].astype(F32) * factor
 
-    @pl.when(half == 0)
-    def _():
-        first_half(part_of(0), outs, staged, sems)
-
-    @pl.when(half == 1)
-    def _():
-        second_half(part_of(O_MERGE), outs, staged, sems)
+    for which, fill, base in ((0, first_half, 0), (1, second_half, O_MERGE)):
+
+        @pl.when(half == which)
+        def _():
+            begun = []
+
+            def leaves(source, target):
+                begun.append(pltpu.make_async_copy(source, target, sems.at[len(begun)]))
+                begun[-1].start()
+
+            fill(part_of(base), outs, staged, leaves)
+            for copy in begun:
+                copy.wait()
 
     for copy in copies:
         copy.wait()
@@ -677,7 +740,7 @@
         shape((C, C), F32),
         shape((HEADS, TYPES, BPOS), F32),
     ]
-    scratch = [pltpu.VMEM(item.shape, F32) for item in sums] + [pltpu.SemaphoreType.DMA((6,))]
+    scratch = [pltpu.VMEM(item.shape, F32) for item in sums] + [pltpu.SemaphoreType.DMA((7,))]
     grid = [shape((12, HALF, LEVELS, 2 * C), BF), shape((LEVELS, 2 * HALF, LAT, C), BF)]
     params = pltpu.CompilerParams(vmem_limit_bytes=16 * 1024 * 1024)
     begun = pl.pallas_call(
@@ -715,12 +778,12 @@
     ]
 
 
-def summed_over(keep, send, axis, partner, forward):
+def summed_over(keep, send, axis, joined, partner, forward):
     count = lax.axis_size(axis)
     along = count // (CORES * ACROSS)
     pairs = [(i, i ^ 1) for i in range(count)]
     arrived = lax.ppermute(send, axis, pairs)
-    held = (keep.astype(F32) + arrived.astype(F32)).astype(BF)
+    held = joined(keep, arrived)
 
     def exchanged(value, apart, size):
         return lax.all_to_all(value, axis, 0, 0, axis_index_groups=groups_of(count, apart, size))
@@ -768,9 +831,8 @@
     table, core = lax.optimization_barrier((table, core))
     bias, bias_tail = bias_rows(table, index, region_ids)
     half_rows = -(-O_END // (count * 2)) * 2 * count // CORES
-    keep, send, *results = block(
+    grads, tokens, scores, *results = block(
         half_rows,
-        core,
         by_lon,
         west,
         by_lat,
@@ -785,16 +847,21 @@
         merge_weight,
         bias,
         bias_tail,
-        index,
     )
+    pairs = [(i, i ^ 1) for i in range(count)]
+    partner_scores = lax.ppermute(scores, "lon", pairs)
+    keep, send = pack(core, grads, tokens, results[1])
     merged_keep, field_keep, home = to_grid(*results, qkv_weight, norm_gain.reshape(1, C), merge_weight)
-    partner = lax.ppermute(home, "lon", [(i, i ^ 1) for i in range(count)])
+    partner = lax.ppermute(home, "lon", pairs)
 
     def forward(held, leaving):
         held, leaving = lax.optimization_barrier((held, leaving))
         return held, lax.ppermute(leaving, "lon", [(i, (i - CORES) % count) for i in range(1, count, CORES)])
 
-    held, other, partner, forwarded = summed_over(keep, send, "lon", partner, forward)
+    table = table_sum(core, scores, partner_scores, index)
+    held, other, partner, forwarded = summed_over(
+        keep, send, "lon", lambda kept, arrived: join(core, kept, arrived, table), partner, forward
+    )
     factor = float(LEVELS * LAT * fields.shape[2] * count) ** (-0.5)
     merged, field_grad, up_grad, down_grad, qkv_grad, merge_grad, proj_grad, table_grad = finish(
         core, held, other, (partner, forwarded, merged_keep, field_keep), factor

time: 129 us -> 122 us (0.946)
  starting transfers between devices: 26.9 us -> 33.6 us
  waiting for transfers between devices: 25.5 us -> 20.4 us
  blocking collectives: 46.4 us -> 43.4 us
  Pallas kernels: 24.7 us -> 21.8 us
    ppermute x1 -> x2, starting transfers between devices: 0.5 us -> 11.9 us  [the longest x1 8.04 us: local(): partner_scores = lax.ppermute(scores, 'lon', pairs)]
    ppermute x1, starting transfers between devices: 8.02 us -> 0.15 us  [summed_over(): arrived = lax.ppermute(send, axis, pairs)]
    all_to_all x1, waiting for transfers between devices: 9.24 us -> 3.25 us  [exchanged(): lax.all_to_all(value, axis, 0, 0, axis_index_groups=groups_of(count, apar...]
    all_to_all x3, blocking collectives: 46.4 us -> 43.4 us  [exchanged(): lax.all_to_all(value, axis, 0, 0, axis_index_groups=groups_of(count, apar...]
    pallas_call x1 -> x4, Pallas kernels: 14 us -> 11.1 us  [the longest x1 9.45 us: block(): pl.pallas_call(block_kernel, out_shape=[shape((2 * half_rows, LANES), BF)...]
    ppermute x1, starting transfers between devices: 6.84 us -> 8.7 us  [summed_over(): return (held, lax.ppermute(held, axis, pairs), partner, forwarded)]
    ppermute x1 -> x2, waiting for transfers between devices: 0.01 us -> 1.62 us  [the longest x1 1.62 us: local(): partner_scores = lax.ppermute(scores, 'lon', pairs)]
    ppermute x1, starting transfers between devices: 4.18 us -> 5.68 us  [forward(): lax.ppermute(leaving, 'lon', [(i, (i - CORES) % count) for i in range(1,...]
  transfers between devices with their start and end apart: 7 -> 8, of which waited for: 5 -> 6; matrix products, arithmetic and copies ran while one was open for 1% -> 1% of each run, Pallas kernels for 6% -> 7%
where the time goes in v5:
time: 122 us
  blocking collectives  43.4 us (36%)
  starting transfers between devices  33.6 us (28%)
  Pallas kernels  21.8 us (18%)
  waiting for transfers between devices  20.4 us (17%)
  other arithmetic  1.5 us (1%)
    all_to_all x3, blocking collectives, exchanged(): lax.all_to_all(value, axis, 0, 0, axis_index_groups=groups_of(count, apar...  43.4 us
    ppermute x2, waiting for transfers between devices, passed_along(): lax.ppermute(value, axis, [(source, (source + steps) % count) for source...  13.4 us
    pallas_call x1, Pallas kernels, block(): pl.pallas_call(block_kernel, out_shape=[shape((2 * half_rows, LANES), BF)...  9.45 us
    ppermute x1, starting transfers between devices, summed_over(): return (held, lax.ppermute(held, axis, pairs), partner, forwarded)  8.7 us
    ppermute x1, starting transfers between devices, local(): partner_scores = lax.ppermute(scores, 'lon', pairs)  8.04 us
    ppermute x1, starting transfers between devices, forward(): lax.ppermute(leaving, 'lon', [(i, (i - CORES) % count) for i in range(1,...  5.68 us
    pallas_call x1, Pallas kernels, bias_rows(): pl.pallas_call(bias_kernel, out_shape=[jax.ShapeDtypeStruct((TH * WIN, LA...  5.14 us
    all_to_all x1, starting transfers between devices, exchanged(): lax.all_to_all(value, axis, 0, 0, axis_index_groups=groups_of(count, apar...  4.28 us
  transfers between devices with their start and end apart: 8, of which 6 were waited for; matrix products, arithmetic and copies ran while one was open for 1% of the time, Pallas kernels for 7%

profile of v5, /device:TPU:33, one launch (start us, length us, event | category | flops | bytes accessed | tf_op | source)
XLA Modules:
  0.0 122.0 jit_solution(14974455992377302093)
XLA Ops:
  0.6 1.2 stage.1
  1.8 2.8 %collective-permute-start.1 = (bf16[12,3,2,384]{3,2,1,0:T(2,128)(2,1)S(1)}, bf16[12,3,2,384]{3,2,1,0:T(2,128)(2,1)S(1)}, u32[]{:S(2)}, u32[]{:S(2)}) collective-permute-start(bf16[12,3,2,384]{3,2,1,0:T(2,128)(2,1)S(1)} %get-tuple-element.51), channel_id=1, source_target_pairs={{0,1},{1,2},{2,3},{3,4},{4,5},{5,6},{6,7},{7,8},{8,9},{9,10},{10,1... | collective-permute-start | bytes 165896 | tf_op jit(solution)/shard_map/ppermute | solution.py:770
  4.6 0.1 collective-permute-start
  4.7 0.0 copy-start
  4.7 0.0 copy-start.1
  4.7 0.0 copy-start.2
  4.7 0.0 copy-start.3
  4.7 0.0 copy-start.4
  4.7 0.0 copy-start.5
  4.7 0.0 copy-start.6
  4.8 0.0 copy-start.7
  4.8 0.0 copy-start.8
  4.8 5.1 %bias_rows.1 = (f32[3456,128]{1,0:T(8,128)S(1)}, f32[3456,128]{1,0:T(8,128)S(1)}) custom-call(f32[6,4,3312]{2,1,0:T(4,128)S(1)} %get-tuple-element.53.table_ref, s32[144,144]{1,0:T(8,128)S(1)} %get-tuple-element.54.index_ref, s32[2,24]{1,0:T(2,128)} %regions_ref.1), custom_call_target="tpu_custom_call" | custom-call | flops 14000000000 | bytes 4000000 | tf_op jit(solution)/shard_map/bias_rows/pallas_call | solution.py:256
  9.9 13.1 %collective-permute-done.1.west_cotangent_ref = bf16[12,3,2,384]{3,2,1,0:T(2,128)(2,1)S(1)} collective-permute-done((bf16[12,3,2,384]{3,2,1,0:T(2,128)(2,1)S(1)}, bf16[12,3,2,384]{3,2,1,0:T(2,128)(2,1)S(1)}, u32[]{:S(2)}, u32[]{:S(2)}) %collective-permute-start.1) | collective-permute-done | bytes 55328 | tf_op jit(solution)/shard_map/ppermute | solution.py:770
  23.1 0.3 collective-permute-done.west_ref
  23.3 0.0 copy-done
  23.3 0.0 copy-done.1
  23.3 0.0 copy-done.2
  23.4 0.0 copy-done.3
  23.4 0.0 copy-done.4
  23.4 0.0 copy-done.5
  23.4 0.0 copy-done.6
  23.4 0.0 copy-done.7
  23.4 0.0 copy-done.8
  23.4 9.4 %block.1 = (bf16[6400,128]{1,0:T(8,128)(2,1)S(1)}, bf16[576,192]{1,0:T(8,128)(2,1)S(1)}, bf16[4224,128]{1,0:T(8,128)(2,1)S(1)}, bf16[4,160,192]{2,1,0:T(8,128)(2...) custom-call(bf16[2,12,24,192]{3,2,1,0:T(8,128)(2,1)S(1)} %bitcast.18, ...), custom_call_target="tpu_custom_call" | custom-call | flops 24000000000 | bytes 12000000 | tf_op jit(solution)/shard_map/block/pallas_call | solution.py:472
  32.9 8.0 %collective-permute-start.3 = (bf16[4224,128]{1,0:T(8,128)(2,1)S(1)}, bf16[4224,128]{1,0:T(8,128)(2,1)S(1)}, u32[]{:S(2)}, u32[]{:S(2)}) collective-permute-start(bf16[4224,128]{1,0:T(8,128)(2,1)S(1)} %get-tuple-element.62.own_ref), channel_id=1, source_target_pairs={{0,1},{1,0},{2,3},{3,2},{4,5},{5,4},{6,7},{7,6},{8,9},{9,8},{10,11... | collective-permute-start | bytes 3244040 | tf_op jit(solution)/shard_map/ppermute | solution.py:852
  40.9 0.5 pack.1
  41.5 0.2 collective-permute-start.2
  41.6 1.6 %collective-permute-done.3.partner_ref = bf16[4224,128]{1,0:T(8,128)(2,1)S(1)} collective-permute-done((bf16[4224,128]{1,0:T(8,128)(2,1)S(1)}, bf16[4224,128]{1,0:T(8,128)(2,1)S(1)}, u32[]{:S(2)}, u32[]{:S(2)}) %collective-permute-start.3) | collective-permute-done | bytes 1081376 | tf_op jit(solution)/shard_map/ppermute | solution.py:852
  43.3 1.1 collective-permute-done.2.arrived_ref
  44.4 1.1 join.1
  45.5 4.3 %all-to-all-start = ((bf16[4,800,128]{2,1,0:T(8,128)(2,1)}), bf16[4,800,128]{2,1,0:T(8,128)(2,1)}, u32[]{:S(2)}, u32[]{:S(2)}) async-start(bf16[4,800,128]{2,1,0:T(8,128)(2,1)} %bitcast.7), calls=%async_computation | async-start | bytes 1638400 | tf_op jit(solution)/shard_map/all_to_all | solution.py:789
  49.8 1.7 %to_grid.1 = (bf16[12,3,2,384]{3,2,1,0:T(2,128)(2,1)S(1)}, bf16[2,6,24,192]{3,2,1,0:T(8,128)(2,1)S(1)}, bf16[9,24,384]{2,1,0:T(8,128)(2,1)S(1)}) custom-call(bf16[4,160,192]{2,1,0:T(8,128)(2,1)S(1)} %get-tuple-element.63.normed_merge_ref, bf16[576,576]{1,0:T(8,128)(2,1)S(1)} %get-tuple-element.59.triple_ref, ...), custom_call_target="tpu_custom_call" | custom-call | flops 1500000000 | bytes 3000000 | tf_op jit(solution)/shard_map/to_grid/pallas_call | solution.py:623
  51.4 3.8 %collective-permute-start.4 = (bf16[9,24,384]{2,1,0:T(8,128)(2,1)S(1)}, bf16[9,24,384]{2,1,0:T(8,128)(2,1)S(1)}, u32[]{:S(2)}, u32[]{:S(2)}) collective-permute-start(bf16[9,24,384]{2,1,0:T(8,128)(2,1)S(1)} %get-tuple-element.67), channel_id=1, source_target_pairs={{0,1},{1,0},{2,3},{3,2},{4,5},{5,4},{6,7},{7,6},{8,9},{9,8},{10,11... | collective-permute-start | bytes 497672 | tf_op jit(solution)/shard_map/ppermute | solution.py:855
  55.3 3.2 %all-to-all-done = bf16[4,800,128]{2,1,0:T(8,128)(2,1)} async-done(((bf16[4,800,128]{2,1,0:T(8,128)(2,1)}), bf16[4,800,128]{2,1,0:T(8,128)(2,1)}, u32[]{:S(2)}, u32[]{:S(2)}) %all-to-all-start) | async-done | bytes 819232 | tf_op jit(solution)/shard_map/all_to_all | solution.py:789
  58.5 1.3 %reduce_sum.24 = bf16[800,128]{1,0:T(8,128)(2,1)S(1)} reduce(bf16[4,800,128]{2,1,0:T(8,128)(2,1)} %all-to-all-done, bf16[]{:T(256)} %constant.20.clone.1), dimensions={0}, to_apply=%region_0.1 | reduce | flops 307200 | bytes 1024002 | tf_op jit(solution)/shard_map/reduce_sum | solution.py:793
  59.8 0.0 collective-permute-done.4.refs_2_
  59.8 15.2 %all_to_all.20 = bf16[16,25,2,128]{3,2,1,0:T(2,128)(2,1)S(1)} all-to-all(bf16[16,25,2,128]{3,2,1,0:T(2,128)(2,1)S(1)} %bitcast.25), channel_id=1, replica_groups={{0,8,16,24,32,40,48,56,64,72,80,88,96,104,112,120},{1,9,17,25,33,41,49,..., dimensions={0} | all-to-all | bytes 409600 | tf_op jit(solution)/shard_map/all_to_all | solution.py:789
  75.0 0.2 reduce_sum.25
  75.2 0.1 broadcast_in_dim.6
  75.3 17.3 %all_to_all.21 = bf16[16,25,2,128]{3,2,1,0:T(2,128)(2,1)S(1)} all-to-all(bf16[16,25,2,128]{3,2,1,0:T(2,128)(2,1)S(1)} %broadcast_in_dim.6), channel_id=1, replica_groups={{0,8,16,24,32,40,48,56,64,72,80,88,96,104,112,120},{1,9,17,25,33,41,49,..., dimensions={0} | all-to-all | bytes 409600 | tf_op jit(solution)/shard_map/all_to_all | solution.py:789
  92.6 0.1 broadcast_in_dim.15
  92.8 10.9 %all_to_all.22 = bf16[4,800,128]{2,1,0:T(8,128)(2,1)S(1)} all-to-all(bf16[4,800,128]{2,1,0:T(8,128)(2,1)S(1)} %broadcast_in_dim.15), channel_id=1, replica_groups={{0,2,4,6},{1,3,5,7},{8,10,12,14},{9,11,13,15},{16,18,20,22},{17,19,21,2..., dimensions={0} | all-to-all | bytes 1638400 | tf_op jit(solution)/shard_map/all_to_all | solution.py:789
  103.7 8.7 %collective-permute-start.5 = (bf16[3200,128]{1,0:T(8,128)(2,1)S(1)}, bf16[3200,128]{1,0:T(8,128)(2,1)S(1)}, u32[]{:S(2)}, u32[]{:S(2)}) collective-permute-start(bf16[3200,128]{1,0:T(8,128)(2,1)S(1)} %bitcast.15), channel_id=1, source_target_pairs={{0,1},{1,0},{2,3},{3,2},{4,5},{5,4},{6,7},{7,6},{8,9},{9,8},{10,11... | collective-permute-start | bytes 2457608 | tf_op jit(solution)/shard_map/ppermute | solution.py:804
  112.4 5.7 %collective-permute-start.6 = (bf16[9,24,384]{2,1,0:T(8,128)(2,1)S(1)}, bf16[9,24,384]{2,1,0:T(8,128)(2,1)S(1)}, u32[]{:S(2)}, u32[]{:S(2)}) collective-permute-start(bf16[9,24,384]{2,1,0:T(8,128)(2,1)S(1)} %collective-permute-done.4.refs_2_), channel_id=1, source_target_pairs={{1,127},{3,1},{5,3},{7,5},{9,7},{11,9},{13,11},{15,13},{17,15},{19... | collective-permute-start | bytes 497672 | tf_op jit(solution)/shard_map/ppermute | solution.py:859
  118.1 1.3 %finish_own.1 = (f32[192,768]{1,0:T(8,128)}, f32[192,768]{1,0:T(8,128)}, f32[192,576]{1,0:T(8,128)}, f32[768,384]{1,0:T(8,128)}, f32[192,192]{1,0:T(8,128)}, /*index=5*/f32[6,4,3312]{2,1,0:T(4,128)}) custom-call(s32[1]{0:T(128)} %bitcast.3.core_ref.refs_0_, bf16[3200,128]{1,0:T(8,128)(2,1)S(1)} %bitcast.16), custom_call_target="tpu_custom_call" | custom-call | flops 400000 | bytes 2500000 | tf_op jit(solution)/shard_map/finish_own/pallas_call | solution.py:746
  119.4 1.0 collective-permute-done.6.refs_3_
  120.3 0.0 collective-permute-done.5.refs_1_
  120.3 1.5 %finish_other.1 = (bf16[12,6,2,384]{3,2,1,0:T(2,128)(2,1)}, bf16[2,12,24,192]{3,2,1,0:T(8,128)(2,1)}, f32[192,768]{1,0:T(8,128)}, f32[192,768]{1,0:T(8,128)}, f3...) custom-call(s32[1]{0:T(128)} %bitcast.3.core_ref.refs_0_, ...), custom_call_target="tpu_custom_call", output_to_operand_aliasing={{2}: (6, {}), {3}: (7, {}), {4}: (8, {}), {5}: (9, {}), {6}... | custom-call | tf_op jit(solution)/shard_map/finish_other/pallas_call | solution.py:756
  (1 shorter events, 0.0 us)
Async XLA Ops:
  1.8 21.3 %collective-permute-start.1 = (bf16[12,3,2,384]{3,2,1,0:T(2,128)(2,1)S(1)}, bf16[12,3,2,384]{3,2,1,0:T(2,128)(2,1)S(1)}, u32[]{:S(2)}, u32[]{:S(2)}) collective-permute-start(bf16[12,3,2,384]{3,2,1,0:T(2,128)(2,1)S(1)} %get-tuple-element.51), channel_id=1, source_target_pairs={{0,1},{1,2},{2,3},{3,4},{4,5},{5,6},{6,7},{7,8},{8,9},{9,10},{10,1... | collective-permute-start | bytes 165896 | tf_op jit(solution)/shard_map/ppermute | solution.py:770
  4.6 18.8 %collective-permute-start = (bf16[2,6,24,192]{3,2,1,0:T(8,128)(2,1)S(1)}, bf16[2,6,24,192]{3,2,1,0:T(8,128)(2,1)S(1)}, u32[]{:S(2)}, u32[]{:S(2)}) collective-permute-start(bf16[2,6,24,192]{3,2,1,0:T(8,128)(2,1)S(1)} %get-tuple-element.50), channel_id=1, source_target_pairs={{0,1},{1,2},{2,3},{3,4},{4,5},{5,6},{6,7},{7,8},{8,9},{9,10},{10,1... | collective-permute-start | bytes 331784 | tf_op jit(solution)/shard_map/ppermute | solution.py:770
  4.7 18.6 %copy-start = (bf16[2,24,12,192]{3,1,2,0:T(8,128)(2,1)S(1)}, bf16[2,24,12,192]{3,1,2,0:T(8,128)(2,1)}, u32[]{:S(2)}) copy-start(bf16[2,24,12,192]{3,1,2,0:T(8,128)(2,1)} %param.13) | copy-start | bytes 663556
  4.7 18.6 %copy-start.1 = (bf16[2,12,6,384]{3,0,2,1:T(2,128)(2,1)S(1)}, bf16[2,12,6,384]{3,0,2,1:T(2,128)(2,1)}, u32[]{:S(2)}) copy-start(bf16[2,12,6,384]{3,0,2,1:T(2,128)(2,1)} %param.25) | copy-start | bytes 331780
  4.7 18.6 %copy-start.2 = (bf16[768,384]{1,0:T(8,128)(2,1)S(1)}, bf16[768,384]{1,0:T(8,128)(2,1)}, u32[]{:S(2)}) copy-start(bf16[768,384]{1,0:T(8,128)(2,1)} %merge_ref.3) | copy-start | bytes 1769476
  4.7 18.6 %copy-start.3 = (bf16[192,768]{1,0:T(8,128)(2,1)S(1)}, bf16[192,768]{1,0:T(8,128)(2,1)}, u32[]{:S(2)}) copy-start(bf16[192,768]{1,0:T(8,128)(2,1)} %up_ref.1) | copy-start | bytes 884740
  4.7 18.6 %copy-start.4 = (bf16[768,192]{0,1:T(8,128)(2,1)S(1)}, bf16[768,192]{0,1:T(8,128)(2,1)}, u32[]{:S(2)}) copy-start(bf16[768,192]{0,1:T(8,128)(2,1)} %param.22) | copy-start | bytes 884740
  4.7 18.6 %copy-start.5 = (bf16[192,576]{1,0:T(8,128)(2,1)S(1)}, bf16[192,576]{1,0:T(8,128)(2,1)}, u32[]{:S(2)}) copy-start(bf16[192,576]{1,0:T(8,128)(2,1)} %qkv_ref.3) | copy-start | bytes 663556
  4.7 18.6 %copy-start.6 = (bf16[192,192]{1,0:T(8,128)(2,1)S(1)}, bf16[192,192]{1,0:T(8,128)(2,1)}, u32[]{:S(2)}) copy-start(bf16[192,192]{1,0:T(8,128)(2,1)} %proj_ref.1) | copy-start | bytes 221188
  4.8 18.6 %copy-start.7 = (f32[192]{0:T(256)S(1)}, f32[192]{0:T(256)}, u32[]{:S(2)}) copy-start(f32[192]{0:T(256)} %param.20) | copy-start | bytes 2308
  4.8 18.6 %copy-start.8 = (f32[192]{0:T(256)S(1)}, f32[192]{0:T(256)}, u32[]{:S(2)}) copy-start(f32[192]{0:T(256)} %param.14) | copy-start | bytes 2308
  32.9 10.4 %collective-permute-start.3 = (bf16[4224,128]{1,0:T(8,128)(2,1)S(1)}, bf16[4224,128]{1,0:T(8,128)(2,1)S(1)}, u32[]{:S(2)}, u32[]{:S(2)}) collective-permute-start(bf16[4224,128]{1,0:T(8,128)(2,1)S(1)} %get-tuple-element.62.own_ref), channel_id=1, source_target_pairs={{0,1},{1,0},{2,3},{3,2},{4,5},{5,4},{6,7},{7,6},{8,9},{9,8},{10,11... | collective-permute-start | bytes 3244040 | tf_op jit(solution)/shard_map/ppermute | solution.py:852
  41.5 2.9 %collective-permute-start.2 = (bf16[3200,128]{1,0:T(8,128)(2,1)S(1)}, bf16[3200,128]{1,0:T(8,128)(2,1)S(1)}, u32[]{:S(2)}, u32[]{:S(2)}) collective-permute-start(bf16[3200,128]{1,0:T(8,128)(2,1)S(1)} %get-tuple-element.61), channel_id=1, source_target_pairs={{0,1},{1,0},{2,3},{3,2},{4,5},{5,4},{6,7},{7,6},{8,9},{9,8},{10,11... | collective-permute-start | bytes 2457608 | tf_op jit(solution)/shard_map/ppermute | solution.py:785
  45.5 13.0 %all-to-all-start = ((bf16[4,800,128]{2,1,0:T(8,128)(2,1)}), bf16[4,800,128]{2,1,0:T(8,128)(2,1)}, u32[]{:S(2)}, u32[]{:S(2)}) async-start(bf16[4,800,128]{2,1,0:T(8,128)(2,1)} %bitcast.7), calls=%async_computation | async-start | bytes 1638400 | tf_op jit(solution)/shard_map/all_to_all | solution.py:789
  51.4 8.4 %collective-permute-start.4 = (bf16[9,24,384]{2,1,0:T(8,128)(2,1)S(1)}, bf16[9,24,384]{2,1,0:T(8,128)(2,1)S(1)}, u32[]{:S(2)}, u32[]{:S(2)}) collective-permute-start(bf16[9,24,384]{2,1,0:T(8,128)(2,1)S(1)} %get-tuple-element.67), channel_id=1, source_target_pairs={{0,1},{1,0},{2,3},{3,2},{4,5},{5,4},{6,7},{7,6},{8,9},{9,8},{10,11... | collective-permute-start | bytes 497672 | tf_op jit(solution)/shard_map/ppermute | solution.py:855
  103.7 16.7 %collective-permute-start.5 = (bf16[3200,128]{1,0:T(8,128)(2,1)S(1)}, bf16[3200,128]{1,0:T(8,128)(2,1)S(1)}, u32[]{:S(2)}, u32[]{:S(2)}) collective-permute-start(bf16[3200,128]{1,0:T(8,128)(2,1)S(1)} %bitcast.15), channel_id=1, source_target_pairs={{0,1},{1,0},{2,3},{3,2},{4,5},{5,4},{6,7},{7,6},{8,9},{9,8},{10,11... | collective-permute-start | bytes 2457608 | tf_op jit(solution)/shard_map/ppermute | solution.py:804
  112.4 7.9 %collective-permute-start.6 = (bf16[9,24,384]{2,1,0:T(8,128)(2,1)S(1)}, bf16[9,24,384]{2,1,0:T(8,128)(2,1)S(1)}, u32[]{:S(2)}, u32[]{:S(2)}) collective-permute-start(bf16[9,24,384]{2,1,0:T(8,128)(2,1)S(1)} %collective-permute-done.4.refs_2_), channel_id=1, source_target_pairs={{1,127},{3,1},{5,3},{7,5},{9,7},{11,9},{13,11},{15,13},{17,15},{19... | collective-permute-start | bytes 497672 | tf_op jit(solution)/shard_map/ppermute | solution.py:859

commit v6 on v5

--- a/solution.py
+++ b/solution.py
@@ -679,52 +679,52 @@
     leaves(merge.at[:MSPLIT, 256:], merge_ref.at[:MSPLIT, 256:])
 
 
-def half_kernel(factor, own, core_ref, sums_ref, *refs):
-    if own:
-        outs, scratch = (None, None, *refs[:6]), refs[6:]
-    else:
-        partner_ref, forwarded_ref, merged_keep_ref, field_keep_ref = refs[:4]
-        outs, scratch = refs[10:18], refs[18:]
-    staged, sems = scratch[:6], scratch[6]
-    core = core_ref[0]
-    half = core if own else 1 - core
-    copies = []
-    if not own:
-        merged, field = scratch[7:9]
-        east = jnp.where(core == 0, partner_ref[...].astype(F32), forwarded_ref[...].astype(F32))
-        for level in range(LEVELS):
-            field[level, HALF:] = east[:HALF, :, C * level : C * (level + 1)].astype(BF)
-        field[:, :HALF] = field_keep_ref[...]
-        copies.append(pltpu.make_async_copy(field, outs[1], sems.at[5]))
-        copies[-1].start()
-        cells = east[HALF:].reshape(72, 2 * C)
-        for lat in range(12):
-            for lon in range(HALF // 2):
-                row = (lat * 3 + lon) * 2
-                merged[lat, HALF // 2 + lon] = cells[row : row + 2].astype(BF)
-        merged[:, : HALF // 2] = merged_keep_ref[...]
-        copies.append(pltpu.make_async_copy(merged, outs[0], sems.at[6]))
-        copies[-1].start()
-
-    def part_of(base):
-        return lambda start, rows: sums_ref[start - base : start - base + rows, :].astype(F32) * factor
-
+def scaled(factor, half, sums_ref, outs, staged, sems):
     for which, fill, base in ((0, first_half, 0), (1, second_half, O_MERGE)):
 
         @pl.when(half == which)
         def _():
             begun = []
 
+            def part(start, rows):
+                return sums_ref[start - base : start - base + rows, :].astype(F32) * factor
+
             def leaves(source, target):
                 begun.append(pltpu.make_async_copy(source, target, sems.at[len(begun)]))
                 begun[-1].start()
 
-            fill(part_of(base), outs, staged, leaves)
+            fill(part, outs, staged, leaves)
             for copy in begun:
                 copy.wait()
 
+
+def finish_own_kernel(
+    factor, core_ref, held_ref, partner_ref, forwarded_ref, merged_keep_ref, field_keep_ref, *refs
+):
+    outs, staged, (sems, merged, field) = refs[:8], refs[8:14], refs[14:]
+    core = core_ref[0]
+    east = jnp.where(core == 0, partner_ref[...].astype(F32), forwarded_ref[...].astype(F32))
+    for level in range(LEVELS):
+        field[level, HALF:] = east[:HALF, :, C * level : C * (level + 1)].astype(BF)
+    field[:, :HALF] = field_keep_ref[...]
+    copies = [pltpu.make_async_copy(field, outs[1], sems.at[5])]
+    copies[-1].start()
+    cells = east[HALF:].reshape(72, 2 * C)
+    for lat in range(12):
+        for lon in range(HALF // 2):
+            row = (lat * 3 + lon) * 2
+            merged[lat, HALF // 2 + lon] = cells[row : row + 2].astype(BF)
+    merged[:, : HALF // 2] = merged_keep_ref[...]
+    copies.append(pltpu.make_async_copy(merged, outs[0], sems.at[6]))
+    copies[-1].start()
+    scaled(factor, core, held_ref, outs, staged, sems)
     for copy in copies:
         copy.wait()
+
+
+def finish_other_kernel(factor, core_ref, other_ref, *refs):
+    outs, staged, sems = refs[6:12], refs[12:18], refs[18]
+    scaled(factor, 1 - core_ref[0], other_ref, (None, None, *outs), staged, sems)
 
 
 def finish(core, held, other, cells, factor):
@@ -743,26 +743,27 @@
     scratch = [pltpu.VMEM(item.shape, F32) for item in sums] + [pltpu.SemaphoreType.DMA((7,))]
     grid = [shape((12, HALF, LEVELS, 2 * C), BF), shape((LEVELS, 2 * HALF, LAT, C), BF)]
     params = pltpu.CompilerParams(vmem_limit_bytes=16 * 1024 * 1024)
-    begun = pl.pallas_call(
-        lambda *refs: half_kernel(factor, True, *refs),
-        out_shape=sums,
-        in_specs=[scalar, whole],
-        out_specs=[place] * 6,
-        scratch_shapes=scratch,
+    merged, field, *begun = pl.pallas_call(
+        lambda *refs: finish_own_kernel(factor, *refs),
+        out_shape=[*grid, *sums],
+        in_specs=[scalar] + [whole] * 5,
+        out_specs=[place] * 8,
+        scratch_shapes=scratch + [pltpu.VMEM(item.shape, BF) for item in grid],
         compiler_params=params,
         cost_estimate=pl.CostEstimate(flops=400_000, bytes_accessed=2_500_000, transcendentals=0),
         name="finish_own",
-    )(core, held)
-    return pl.pallas_call(
-        lambda *refs: half_kernel(factor, False, *refs),
-        out_shape=[*grid, *sums],
-        in_specs=[scalar] + [whole] * 5 + [place] * 6,
-        out_specs=[place] * 8,
-        scratch_shapes=scratch + [pltpu.VMEM(item.shape, BF) for item in grid],
-        input_output_aliases={6 + n: 2 + n for n in range(6)},
+    )(core, held, *cells)
+    rest = pl.pallas_call(
+        lambda *refs: finish_other_kernel(factor, *refs),
+        out_shape=sums,
+        in_specs=[scalar, whole] + [place] * 6,
+        out_specs=[place] * 6,
+        scratch_shapes=scratch,
+        input_output_aliases={2 + n: n for n in range(6)},
         compiler_params=params,
         name="finish_other",
-    )(core, other, *cells, *begun)
+    )(core, other, *begun)
+    return merged, field, *rest
 
 
 def passed_along(value, axis, steps):
@@ -799,8 +800,8 @@
     held, partner = lax.optimization_barrier((held, partner))
     held = reduced(held.reshape(-1, 2, LANES), CORES * ACROSS, along)
     held = gathered(held, CORES * ACROSS, along).reshape(-1, LANES)
+    held, forwarded = forward(held, partner)
     held = gathered(held, CORES, ACROSS)
-    held, forwarded = forward(held, partner)
     return held, lax.ppermute(held, axis, pairs), partner, forwarded
 
 

time: 122 us -> 124 us (1.016)
  waiting for transfers between devices: 20.4 us -> 21.7 us
    ppermute x1, waiting for transfers between devices: 0.97 us -> 2.26 us  [forward(): lax.ppermute(leaving, 'lon', [(i, (i - CORES) % count) for i in range(1,...]
where the time goes in v6:
time: 124 us; the launch traced here: 123 us
  blocking collectives  43.4 us (35%)
  starting transfers between devices  33.6 us (27%)
  Pallas kernels  21.8 us (18%)
  waiting for transfers between devices  21.7 us (18%)
  other arithmetic  1.5 us (1%)
    all_to_all x3, blocking collectives, exchanged(): lax.all_to_all(value, axis, 0, 0, axis_index_groups=groups_of(count, apar...  43.4 us
    ppermute x2, waiting for transfers between devices, passed_along(): lax.ppermute(value, axis, [(source, (source + steps) % count) for source...  13.4 us
    pallas_call x1, Pallas kernels, block(): pl.pallas_call(block_kernel, out_shape=[shape((2 * half_rows, LANES), BF)...  9.45 us
    ppermute x1, starting transfers between devices, summed_over(): return (held, lax.ppermute(held, axis, pairs), partner, forwarded)  8.7 us
    ppermute x1, starting transfers between devices, local(): partner_scores = lax.ppermute(scores, 'lon', pairs)  8.04 us
    ppermute x1, starting transfers between devices, forward(): lax.ppermute(leaving, 'lon', [(i, (i - CORES) % count) for i in range(1,...  5.68 us
    pallas_call x1, Pallas kernels, bias_rows(): pl.pallas_call(bias_kernel, out_shape=[jax.ShapeDtypeStruct((TH * WIN, LA...  5.14 us
    all_to_all x1, starting transfers between devices, exchanged(): lax.all_to_all(value, axis, 0, 0, axis_index_groups=groups_of(count, apar...  4.28 us
  transfers between devices with their start and end apart: 8, of which 6 were waited for; matrix products, arithmetic and copies ran while one was open for 1% of the time, Pallas kernels for 7%

profile of v6, /device:TPU:33, one launch (start us, length us, event | category | flops | bytes accessed | tf_op | source)
XLA Modules:
  0.0 123.3 jit_solution(10856792326754048489)
XLA Ops:
  0.6 1.2 stage.1
  1.8 2.8 %collective-permute-start.1 = (bf16[12,3,2,384]{3,2,1,0:T(2,128)(2,1)S(1)}, bf16[12,3,2,384]{3,2,1,0:T(2,128)(2,1)S(1)}, u32[]{:S(2)}, u32[]{:S(2)}) collective-permute-start(bf16[12,3,2,384]{3,2,1,0:T(2,128)(2,1)S(1)} %get-tuple-element.51), channel_id=1, source_target_pairs={{0,1},{1,2},{2,3},{3,4},{4,5},{5,6},{6,7},{7,8},{8,9},{9,10},{10,1... | collective-permute-start | bytes 165896 | tf_op jit(solution)/shard_map/ppermute | solution.py:771
  4.6 0.1 collective-permute-start
  4.7 0.0 copy-start
  4.7 0.0 copy-start.1
  4.7 0.0 copy-start.2
  4.7 0.0 copy-start.3
  4.7 0.0 copy-start.4
  4.7 0.0 copy-start.5
  4.7 0.0 copy-start.6
  4.8 0.0 copy-start.7
  4.8 0.0 copy-start.8
  4.8 5.1 %bias_rows.1 = (f32[3456,128]{1,0:T(8,128)S(1)}, f32[3456,128]{1,0:T(8,128)S(1)}) custom-call(f32[6,4,3312]{2,1,0:T(4,128)S(1)} %get-tuple-element.53.table_ref, s32[144,144]{1,0:T(8,128)S(1)} %get-tuple-element.54.index_ref, s32[2,24]{1,0:T(2,128)} %regions_ref.1), custom_call_target="tpu_custom_call" | custom-call | flops 14000000000 | bytes 4000000 | tf_op jit(solution)/shard_map/bias_rows/pallas_call | solution.py:256
  9.9 13.1 %collective-permute-done.1.west_cotangent_ref = bf16[12,3,2,384]{3,2,1,0:T(2,128)(2,1)S(1)} collective-permute-done((bf16[12,3,2,384]{3,2,1,0:T(2,128)(2,1)S(1)}, bf16[12,3,2,384]{3,2,1,0:T(2,128)(2,1)S(1)}, u32[]{:S(2)}, u32[]{:S(2)}) %collective-permute-start.1) | collective-permute-done | bytes 55328 | tf_op jit(solution)/shard_map/ppermute | solution.py:771
  23.1 0.3 collective-permute-done.west_ref
  23.3 0.0 copy-done
  23.3 0.0 copy-done.1
  23.3 0.0 copy-done.2
  23.4 0.0 copy-done.3
  23.4 0.0 copy-done.4
  23.4 0.0 copy-done.5
  23.4 0.0 copy-done.6
  23.4 0.0 copy-done.7
  23.4 0.0 copy-done.8
  23.4 9.4 %block.1 = (bf16[6400,128]{1,0:T(8,128)(2,1)S(1)}, bf16[576,192]{1,0:T(8,128)(2,1)S(1)}, bf16[4224,128]{1,0:T(8,128)(2,1)S(1)}, bf16[4,160,192]{2,1,0:T(8,128)(2...) custom-call(bf16[2,12,24,192]{3,2,1,0:T(8,128)(2,1)S(1)} %bitcast.18, ...), custom_call_target="tpu_custom_call" | custom-call | flops 24000000000 | bytes 12000000 | tf_op jit(solution)/shard_map/block/pallas_call | solution.py:472
  32.9 8.0 %collective-permute-start.3 = (bf16[4224,128]{1,0:T(8,128)(2,1)S(1)}, bf16[4224,128]{1,0:T(8,128)(2,1)S(1)}, u32[]{:S(2)}, u32[]{:S(2)}) collective-permute-start(bf16[4224,128]{1,0:T(8,128)(2,1)S(1)} %get-tuple-element.62.own_ref), channel_id=1, source_target_pairs={{0,1},{1,0},{2,3},{3,2},{4,5},{5,4},{6,7},{7,6},{8,9},{9,8},{10,11... | collective-permute-start | bytes 3244040 | tf_op jit(solution)/shard_map/ppermute | solution.py:853
  40.9 0.5 pack.1
  41.5 0.2 collective-permute-start.2
  41.6 1.6 %collective-permute-done.3.partner_ref = bf16[4224,128]{1,0:T(8,128)(2,1)S(1)} collective-permute-done((bf16[4224,128]{1,0:T(8,128)(2,1)S(1)}, bf16[4224,128]{1,0:T(8,128)(2,1)S(1)}, u32[]{:S(2)}, u32[]{:S(2)}) %collective-permute-start.3) | collective-permute-done | bytes 1081376 | tf_op jit(solution)/shard_map/ppermute | solution.py:853
  43.3 1.1 collective-permute-done.2.arrived_ref
  44.4 1.1 join.1
  45.5 4.3 %all-to-all-start = ((bf16[4,800,128]{2,1,0:T(8,128)(2,1)}), bf16[4,800,128]{2,1,0:T(8,128)(2,1)}, u32[]{:S(2)}, u32[]{:S(2)}) async-start(bf16[4,800,128]{2,1,0:T(8,128)(2,1)} %bitcast.7), calls=%async_computation | async-start | bytes 1638400 | tf_op jit(solution)/shard_map/all_to_all | solution.py:790
  49.8 1.7 %to_grid.1 = (bf16[12,3,2,384]{3,2,1,0:T(2,128)(2,1)S(1)}, bf16[2,6,24,192]{3,2,1,0:T(8,128)(2,1)S(1)}, bf16[9,24,384]{2,1,0:T(8,128)(2,1)S(1)}) custom-call(bf16[4,160,192]{2,1,0:T(8,128)(2,1)S(1)} %get-tuple-element.63.normed_merge_ref, bf16[576,576]{1,0:T(8,128)(2,1)S(1)} %get-tuple-element.59.triple_ref, ...), custom_call_target="tpu_custom_call" | custom-call | flops 1500000000 | bytes 3000000 | tf_op jit(solution)/shard_map/to_grid/pallas_call | solution.py:623
  51.4 3.8 %collective-permute-start.4 = (bf16[9,24,384]{2,1,0:T(8,128)(2,1)S(1)}, bf16[9,24,384]{2,1,0:T(8,128)(2,1)S(1)}, u32[]{:S(2)}, u32[]{:S(2)}) collective-permute-start(bf16[9,24,384]{2,1,0:T(8,128)(2,1)S(1)} %get-tuple-element.67), channel_id=1, source_target_pairs={{0,1},{1,0},{2,3},{3,2},{4,5},{5,4},{6,7},{7,6},{8,9},{9,8},{10,11... | collective-permute-start | bytes 497672 | tf_op jit(solution)/shard_map/ppermute | solution.py:856
  55.3 3.2 %all-to-all-done = bf16[4,800,128]{2,1,0:T(8,128)(2,1)} async-done(((bf16[4,800,128]{2,1,0:T(8,128)(2,1)}), bf16[4,800,128]{2,1,0:T(8,128)(2,1)}, u32[]{:S(2)}, u32[]{:S(2)}) %all-to-all-start) | async-done | bytes 819232 | tf_op jit(solution)/shard_map/all_to_all | solution.py:790
  58.5 1.3 %reduce_sum.24 = bf16[800,128]{1,0:T(8,128)(2,1)S(1)} reduce(bf16[4,800,128]{2,1,0:T(8,128)(2,1)} %all-to-all-done, bf16[]{:T(256)} %constant.20.clone.1), dimensions={0}, to_apply=%region_0.1 | reduce | flops 307200 | bytes 1024002 | tf_op jit(solution)/shard_map/reduce_sum | solution.py:794
  59.8 0.0 collective-permute-done.4.refs_2_
  59.8 15.2 %all_to_all.20 = bf16[16,25,2,128]{3,2,1,0:T(2,128)(2,1)S(1)} all-to-all(bf16[16,25,2,128]{3,2,1,0:T(2,128)(2,1)S(1)} %bitcast.25), channel_id=1, replica_groups={{0,8,16,24,32,40,48,56,64,72,80,88,96,104,112,120},{1,9,17,25,33,41,49,..., dimensions={0} | all-to-all | bytes 409600 | tf_op jit(solution)/shard_map/all_to_all | solution.py:790
  75.0 0.2 reduce_sum.25
  75.2 0.1 broadcast_in_dim.4
  75.3 17.3 %all_to_all.21 = bf16[16,25,2,128]{3,2,1,0:T(2,128)(2,1)S(1)} all-to-all(bf16[16,25,2,128]{3,2,1,0:T(2,128)(2,1)S(1)} %broadcast_in_dim.4), channel_id=1, replica_groups={{0,8,16,24,32,40,48,56,64,72,80,88,96,104,112,120},{1,9,17,25,33,41,49,..., dimensions={0} | all-to-all | bytes 409600 | tf_op jit(solution)/shard_map/all_to_all | solution.py:790
  92.6 0.1 broadcast_in_dim.5
  92.8 10.9 %all_to_all.22 = bf16[4,800,128]{2,1,0:T(8,128)(2,1)S(1)} all-to-all(bf16[4,800,128]{2,1,0:T(8,128)(2,1)S(1)} %broadcast_in_dim.5), channel_id=1, replica_groups={{0,2,4,6},{1,3,5,7},{8,10,12,14},{9,11,13,15},{16,18,20,22},{17,19,21,2..., dimensions={0} | all-to-all | bytes 1638400 | tf_op jit(solution)/shard_map/all_to_all | solution.py:790
  103.7 8.7 %collective-permute-start.6 = (bf16[3200,128]{1,0:T(8,128)(2,1)S(1)}, bf16[3200,128]{1,0:T(8,128)(2,1)S(1)}, u32[]{:S(2)}, u32[]{:S(2)}) collective-permute-start(bf16[3200,128]{1,0:T(8,128)(2,1)S(1)} %bitcast.15), channel_id=1, source_target_pairs={{0,1},{1,0},{2,3},{3,2},{4,5},{5,4},{6,7},{7,6},{8,9},{9,8},{10,11... | collective-permute-start | bytes 2457608 | tf_op jit(solution)/shard_map/ppermute | solution.py:805
  112.4 5.7 %collective-permute-start.5 = (bf16[9,24,384]{2,1,0:T(8,128)(2,1)S(1)}, bf16[9,24,384]{2,1,0:T(8,128)(2,1)S(1)}, u32[]{:S(2)}, u32[]{:S(2)}) collective-permute-start(bf16[9,24,384]{2,1,0:T(8,128)(2,1)S(1)} %collective-permute-done.4.refs_2_), channel_id=1, source_target_pairs={{1,127},{3,1},{5,3},{7,5},{9,7},{11,9},{13,11},{15,13},{17,15},{19... | collective-permute-start | bytes 497672 | tf_op jit(solution)/shard_map/ppermute | solution.py:860
  118.1 2.3 %collective-permute-done.5.refs_3_ = bf16[9,24,384]{2,1,0:T(8,128)(2,1)S(1)} collective-permute-done((bf16[9,24,384]{2,1,0:T(8,128)(2,1)S(1)}, bf16[9,24,384]{2,1,0:T(8,128)(2,1)S(1)}, u32[]{:S(2)}, u32[]{:S(2)}) %collective-permute-start.5) | collective-permute-done | bytes 165920 | tf_op jit(solution)/shard_map/ppermute | solution.py:860
  120.3 1.5 %finish_own.1 = (bf16[12,6,2,384]{3,2,1,0:T(2,128)(2,1)}, bf16[2,12,24,192]{3,2,1,0:T(8,128)(2,1)}, f32[192,768]{1,0:T(8,128)}, f32[192,768]{1,0:T(8,128)}, f32[...) custom-call(s32[1]{0:T(128)} %bitcast.3.core_ref.refs_0_, ...), custom_call_target="tpu_custom_call" | custom-call | flops 400000 | bytes 2500000 | tf_op jit(solution)/shard_map/finish_own/pallas_call | solution.py:746
  121.8 0.0 collective-permute-done.6.refs_1_
  121.8 1.3 %finish_other.1 = (f32[192,768]{1,0:T(8,128)}, f32[192,768]{1,0:T(8,128)}, f32[192,576]{1,0:T(8,128)}, f32[768,384]{1,0:T(8,128)}, f32[192,192]{1,0:T(8,128)}, /*index=5*/f32[6,4,3312]{2,1,0:T(4,128)}) custom-call(s32[1]{0:T(128)} %bitcast.3.core_ref.refs_0_, ...), custom_call_target="tpu_custom_call", output_to_operand_aliasing={{0}: (2, {}), {1}: (3, {}), {2}: (4, {}), {3}: (5, {}), {4}... | custom-call | tf_op jit(solution)/shard_map/finish_other/pallas_call | solution.py:756
  (1 shorter events, 0.0 us)
Async XLA Ops:
  1.8 21.3 %collective-permute-start.1 = (bf16[12,3,2,384]{3,2,1,0:T(2,128)(2,1)S(1)}, bf16[12,3,2,384]{3,2,1,0:T(2,128)(2,1)S(1)}, u32[]{:S(2)}, u32[]{:S(2)}) collective-permute-start(bf16[12,3,2,384]{3,2,1,0:T(2,128)(2,1)S(1)} %get-tuple-element.51), channel_id=1, source_target_pairs={{0,1},{1,2},{2,3},{3,4},{4,5},{5,6},{6,7},{7,8},{8,9},{9,10},{10,1... | collective-permute-start | bytes 165896 | tf_op jit(solution)/shard_map/ppermute | solution.py:771
  4.6 18.8 %collective-permute-start = (bf16[2,6,24,192]{3,2,1,0:T(8,128)(2,1)S(1)}, bf16[2,6,24,192]{3,2,1,0:T(8,128)(2,1)S(1)}, u32[]{:S(2)}, u32[]{:S(2)}) collective-permute-start(bf16[2,6,24,192]{3,2,1,0:T(8,128)(2,1)S(1)} %get-tuple-element.50), channel_id=1, source_target_pairs={{0,1},{1,2},{2,3},{3,4},{4,5},{5,6},{6,7},{7,8},{8,9},{9,10},{10,1... | collective-permute-start | bytes 331784 | tf_op jit(solution)/shard_map/ppermute | solution.py:771
  4.7 18.6 %copy-start = (bf16[2,24,12,192]{3,1,2,0:T(8,128)(2,1)S(1)}, bf16[2,24,12,192]{3,1,2,0:T(8,128)(2,1)}, u32[]{:S(2)}) copy-start(bf16[2,24,12,192]{3,1,2,0:T(8,128)(2,1)} %param.13) | copy-start | bytes 663556
  4.7 18.6 %copy-start.1 = (bf16[2,12,6,384]{3,0,2,1:T(2,128)(2,1)S(1)}, bf16[2,12,6,384]{3,0,2,1:T(2,128)(2,1)}, u32[]{:S(2)}) copy-start(bf16[2,12,6,384]{3,0,2,1:T(2,128)(2,1)} %param.25) | copy-start | bytes 331780
  4.7 18.6 %copy-start.2 = (bf16[768,384]{1,0:T(8,128)(2,1)S(1)}, bf16[768,384]{1,0:T(8,128)(2,1)}, u32[]{:S(2)}) copy-start(bf16[768,384]{1,0:T(8,128)(2,1)} %merge_ref.3) | copy-start | bytes 1769476
  4.7 18.6 %copy-start.3 = (bf16[192,768]{1,0:T(8,128)(2,1)S(1)}, bf16[192,768]{1,0:T(8,128)(2,1)}, u32[]{:S(2)}) copy-start(bf16[192,768]{1,0:T(8,128)(2,1)} %up_ref.1) | copy-start | bytes 884740
  4.7 18.6 %copy-start.4 = (bf16[768,192]{0,1:T(8,128)(2,1)S(1)}, bf16[768,192]{0,1:T(8,128)(2,1)}, u32[]{:S(2)}) copy-start(bf16[768,192]{0,1:T(8,128)(2,1)} %param.22) | copy-start | bytes 884740
  4.7 18.6 %copy-start.5 = (bf16[192,576]{1,0:T(8,128)(2,1)S(1)}, bf16[192,576]{1,0:T(8,128)(2,1)}, u32[]{:S(2)}) copy-start(bf16[192,576]{1,0:T(8,128)(2,1)} %qkv_ref.3) | copy-start | bytes 663556
  4.7 18.6 %copy-start.6 = (bf16[192,192]{1,0:T(8,128)(2,1)S(1)}, bf16[192,192]{1,0:T(8,128)(2,1)}, u32[]{:S(2)}) copy-start(bf16[192,192]{1,0:T(8,128)(2,1)} %proj_ref.1) | copy-start | bytes 221188
  4.8 18.6 %copy-start.7 = (f32[192]{0:T(256)S(1)}, f32[192]{0:T(256)}, u32[]{:S(2)}) copy-start(f32[192]{0:T(256)} %param.20) | copy-start | bytes 2308
  4.8 18.6 %copy-start.8 = (f32[192]{0:T(256)S(1)}, f32[192]{0:T(256)}, u32[]{:S(2)}) copy-start(f32[192]{0:T(256)} %param.14) | copy-start | bytes 2308
  32.9 10.4 %collective-permute-start.3 = (bf16[4224,128]{1,0:T(8,128)(2,1)S(1)}, bf16[4224,128]{1,0:T(8,128)(2,1)S(1)}, u32[]{:S(2)}, u32[]{:S(2)}) collective-permute-start(bf16[4224,128]{1,0:T(8,128)(2,1)S(1)} %get-tuple-element.62.own_ref), channel_id=1, source_target_pairs={{0,1},{1,0},{2,3},{3,2},{4,5},{5,4},{6,7},{7,6},{8,9},{9,8},{10,11... | collective-permute-start | bytes 3244040 | tf_op jit(solution)/shard_map/ppermute | solution.py:853
  41.5 2.9 %collective-permute-start.2 = (bf16[3200,128]{1,0:T(8,128)(2,1)S(1)}, bf16[3200,128]{1,0:T(8,128)(2,1)S(1)}, u32[]{:S(2)}, u32[]{:S(2)}) collective-permute-start(bf16[3200,128]{1,0:T(8,128)(2,1)S(1)} %get-tuple-element.61), channel_id=1, source_target_pairs={{0,1},{1,0},{2,3},{3,2},{4,5},{5,4},{6,7},{7,6},{8,9},{9,8},{10,11... | collective-permute-start | bytes 2457608 | tf_op jit(solution)/shard_map/ppermute | solution.py:786
  45.5 13.0 %all-to-all-start = ((bf16[4,800,128]{2,1,0:T(8,128)(2,1)}), bf16[4,800,128]{2,1,0:T(8,128)(2,1)}, u32[]{:S(2)}, u32[]{:S(2)}) async-start(bf16[4,800,128]{2,1,0:T(8,128)(2,1)} %bitcast.7), calls=%async_computation | async-start | bytes 1638400 | tf_op jit(solution)/shard_map/all_to_all | solution.py:790
  51.4 8.4 %collective-permute-start.4 = (bf16[9,24,384]{2,1,0:T(8,128)(2,1)S(1)}, bf16[9,24,384]{2,1,0:T(8,128)(2,1)S(1)}, u32[]{:S(2)}, u32[]{:S(2)}) collective-permute-start(bf16[9,24,384]{2,1,0:T(8,128)(2,1)S(1)} %get-tuple-element.67), channel_id=1, source_target_pairs={{0,1},{1,0},{2,3},{3,2},{4,5},{5,4},{6,7},{7,6},{8,9},{9,8},{10,11... | collective-permute-start | bytes 497672 | tf_op jit(solution)/shard_map/ppermute | solution.py:856
  103.7 18.1 %collective-permute-start.6 = (bf16[3200,128]{1,0:T(8,128)(2,1)S(1)}, bf16[3200,128]{1,0:T(8,128)(2,1)S(1)}, u32[]{:S(2)}, u32[]{:S(2)}) collective-permute-start(bf16[3200,128]{1,0:T(8,128)(2,1)S(1)} %bitcast.15), channel_id=1, source_target_pairs={{0,1},{1,0},{2,3},{3,2},{4,5},{5,4},{6,7},{7,6},{8,9},{9,8},{10,11... | collective-permute-start | bytes 2457608 | tf_op jit(solution)/shard_map/ppermute | solution.py:805
  112.4 7.9 %collective-permute-start.5 = (bf16[9,24,384]{2,1,0:T(8,128)(2,1)S(1)}, bf16[9,24,384]{2,1,0:T(8,128)(2,1)S(1)}, u32[]{:S(2)}, u32[]{:S(2)}) collective-permute-start(bf16[9,24,384]{2,1,0:T(8,128)(2,1)S(1)} %collective-permute-done.4.refs_2_), channel_id=1, source_target_pairs={{1,127},{3,1},{5,3},{7,5},{9,7},{11,9},{13,11},{15,13},{17,15},{19... | collective-permute-start | bytes 497672 | tf_op jit(solution)/shard_map/ppermute | solution.py:860

commit v7 on v6

--- a/solution.py
+++ b/solution.py
@@ -294,14 +294,6 @@
         ordered = dot(to_tokens, cells)
         for kind in range(TYPES):
             x_ref[WIN * kind + 72 * level : WIN * kind + 72 * level + 72, :] = ordered[72 * kind : 72 * kind + 72]
-    unit, scale = normalised(x_ref[...])
-    unit_ref[...] = unit
-    scale_ref[...] = scale
-    tokens = (unit * norm_gain_ref[...]).astype(BF)
-    tokens_ref[...] = tokens
-    q_ref[...] = dot(tokens, qkv_ref[:, 0:C]).astype(BF)
-    k_ref[...] = dot(tokens, qkv_ref[:, C : 2 * C]).astype(BF)
-    v_ref[...] = dot(tokens, qkv_ref[:, 2 * C :]).astype(BF)
     for lat in range(12):
         for lon in range(HALF // 2):
             row = (lat * 3 + lon) * 2
@@ -311,6 +303,14 @@
     for n in range(4):
         value = rounded(dot_nt(grad_merged_ref[...], merge_ref[C * n : C * (n + 1), :]))
         scaled_ref[n] = value * merge_gain_ref[:, C * n : C * (n + 1)]
+    unit, scale = normalised(x_ref[...])
+    unit_ref[...] = unit
+    scale_ref[...] = scale
+    tokens = (unit * norm_gain_ref[...]).astype(BF)
+    tokens_ref[...] = tokens
+    q_ref[...] = dot(tokens, qkv_ref[:, 0:C]).astype(BF)
+    k_ref[...] = dot(tokens, qkv_ref[:, C : 2 * C]).astype(BF)
+    v_ref[...] = dot(tokens, qkv_ref[:, 2 * C :]).astype(BF)
     lane = lax.broadcasted_iota(jnp.int32, (1, C), 1)
     of_head = [
         jnp.where((lane >= HEAD * h) & (lane < HEAD * (h + 1)), 1.0, 0.0).astype(BF) for h in range(HEADS)
@@ -356,9 +356,9 @@
         for quarter in range(4):
             group_ref[quarter, 40 * kind : 40 * kind + 40, :] = grouped[40 * quarter : 40 * quarter + 40]
     quarters = [group_ref[n] for n in range(4)]
-    mean = sum(jnp.sum(v, axis=-1, keepdims=True) for v in quarters) * (1.0 / MLP)
+    mean = jnp.sum(sum(quarters), axis=-1, keepdims=True) * (1.0 / MLP)
     centred = [v - mean for v in quarters]
-    variance = sum(jnp.sum(v * v, axis=-1, keepdims=True) for v in centred) * (1.0 / MLP)
+    variance = jnp.sum(sum(v * v for v in centred), axis=-1, keepdims=True) * (1.0 / MLP)
     scale_merge = lax.rsqrt(variance + EPS)
     for n in range(4):
         unit = centred[n] * scale_merge
@@ -368,11 +368,11 @@
     scaled, total, along = [], 0.0, 0.0
     for n in range(4):
         value = scaled_ref[n]
-        total = total + jnp.sum(value, axis=-1, keepdims=True)
-        along = along + jnp.sum(value * group_ref[n], axis=-1, keepdims=True)
+        total = total + value
+        along = along + value * group_ref[n]
         scaled.append(value)
-    total = total * (1.0 / MLP)
-    along = along * (1.0 / MLP)
+    total = jnp.sum(total, axis=-1, keepdims=True) * (1.0 / MLP)
+    along = jnp.sum(along, axis=-1, keepdims=True) * (1.0 / MLP)
     for n in range(4):
         group_ref[n] = scale_merge * (scaled[n] - total - group_ref[n] * along)
     from_groups = onehot(WIN, 160, of_row=group_of_token)
@@ -538,7 +538,7 @@
     def _():
         ds_ref[...] = own_ref[...].astype(F32) + partner_ref[...].astype(F32)
         turned_ref[...] = jnp.transpose(index_ref[:, MAIN:])
-        table = lax.fori_loop(0, WIN // 8, row_block, jnp.zeros((TROWS, LOW), F32), unroll=9)
+        table = lax.fori_loop(0, WIN // 8, row_block, jnp.zeros((TROWS, LOW), F32), unroll=True)
         index = jnp.concatenate([turned_ref[n : n + 1, :MAIN] for n in range(REST)], axis=1)
         slab = jnp.concatenate([ds_ref[pl.ds(DS_TAIL + n, TH, stride=REST), :] for n in range(REST)], axis=1)
         table = table + table_terms(index, slab)
@@ -594,7 +594,9 @@
     normed_merge_ref, triple_ref, grad_attn_ref, unit_ref, scale_ref, qkv_ref, gain_ref, merge_ref,
     merged_keep_ref, field_keep_ref, home_ref, x_ref,
 ):
+    merged = sum(dot(normed_merge_ref[n], merge_ref[C * n : C * (n + 1), :]) for n in range(4))
     grad_normed = rounded(dot_nt(triple_ref[...], qkv_ref[...]))
+    merged_cells = dot(onehot(144, MTOK, of_col=cell_of_merged), merged.astype(BF))
     x_ref[...] = grad_attn_ref[...].astype(F32) + norm_grad(
         grad_normed, unit_ref[...], scale_ref[...], gain_ref[...]
     )
@@ -608,8 +610,6 @@
         leaving.append(cells[:144])
         field_keep_ref[level] = cells[144:].reshape(HALF, LAT, C).astype(BF)
     home_ref[:HALF] = jnp.concatenate(leaving, axis=1).reshape(HALF, LAT, 2 * C).astype(BF)
-    merged = sum(dot(normed_merge_ref[n], merge_ref[C * n : C * (n + 1), :]) for n in range(4))
-    merged_cells = dot(onehot(144, MTOK, of_col=cell_of_merged), merged.astype(BF))
     for lat in range(12):
         for lon in range(HALF // 2):
             row = 72 + (lat * 3 + lon) * 2
@@ -800,8 +800,8 @@
     held, partner = lax.optimization_barrier((held, partner))
     held = reduced(held.reshape(-1, 2, LANES), CORES * ACROSS, along)
     held = gathered(held, CORES * ACROSS, along).reshape(-1, LANES)
+    held = gathered(held, CORES, ACROSS)
     held, forwarded = forward(held, partner)
-    held = gathered(held, CORES, ACROSS)
     return held, lax.ppermute(held, axis, pairs), partner, forwarded
 
 

time: 124 us -> 123 us (level)
  waiting for transfers between devices: 21.7 us -> 23.6 us
  starting transfers between devices: 33.6 us -> 32.1 us
    all_to_all x1, waiting for transfers between devices: 3.25 us -> 5.1 us  [exchanged(): lax.all_to_all(value, axis, 0, 0, axis_index_groups=groups_of(count, apar...]
where the time goes in v7:
time: 123 us
  blocking collectives  43.3 us (35%)
  starting transfers between devices  32.1 us (26%)
  waiting for transfers between devices  23.6 us (19%)
  Pallas kernels  21.3 us (17%)
  other arithmetic  1.5 us (1%)
    all_to_all x3, blocking collectives, exchanged(): lax.all_to_all(value, axis, 0, 0, axis_index_groups=groups_of(count, apar...  43.3 us
    ppermute x2, waiting for transfers between devices, passed_along(): lax.ppermute(value, axis, [(source, (source + steps) % count) for source...  13.4 us
    pallas_call x1, Pallas kernels, block(): pl.pallas_call(block_kernel, out_shape=[shape((2 * half_rows, LANES), BF)...  9.19 us
    ppermute x1, starting transfers between devices, local(): partner_scores = lax.ppermute(scores, 'lon', pairs)  8.03 us
    ppermute x1, starting transfers between devices, summed_over(): return (held, lax.ppermute(held, axis, pairs), partner, forwarded)  7.74 us
    ppermute x1, starting transfers between devices, forward(): lax.ppermute(leaving, 'lon', [(i, (i - CORES) % count) for i in range(1,...  5.95 us
    pallas_call x1, Pallas kernels, bias_rows(): pl.pallas_call(bias_kernel, out_shape=[jax.ShapeDtypeStruct((TH * WIN, LA...  5.14 us
    all_to_all x1, waiting for transfers between devices, exchanged(): lax.all_to_all(value, axis, 0, 0, axis_index_groups=groups_of(count, apar...  5.1 us
  transfers between devices with their start and end apart: 8, of which 6 were waited for; matrix products, arithmetic and copies ran while one was open for 1% of the time, Pallas kernels for 7%

profile of v7, /device:TPU:33, one launch (start us, length us, event | category | flops | bytes accessed | tf_op | source)
XLA Modules:
  0.0 123.0 jit_solution(1854008692182436593)
XLA Ops:
  0.6 1.2 stage.1
  1.8 2.8 %collective-permute-start.1 = (bf16[12,3,2,384]{3,2,1,0:T(2,128)(2,1)S(1)}, bf16[12,3,2,384]{3,2,1,0:T(2,128)(2,1)S(1)}, u32[]{:S(2)}, u32[]{:S(2)}) collective-permute-start(bf16[12,3,2,384]{3,2,1,0:T(2,128)(2,1)S(1)} %get-tuple-element.51), channel_id=1, source_target_pairs={{0,1},{1,2},{2,3},{3,4},{4,5},{5,6},{6,7},{7,8},{8,9},{9,10},{10,1... | collective-permute-start | bytes 165896 | tf_op jit(solution)/shard_map/ppermute | solution.py:771
  4.6 0.1 collective-permute-start
  4.7 0.0 copy-start
  4.7 0.0 copy-start.1
  4.7 0.0 copy-start.2
  4.7 0.0 copy-start.3
  4.7 0.0 copy-start.4
  4.7 0.0 copy-start.5
  4.7 0.0 copy-start.6
  4.8 0.0 copy-start.7
  4.8 0.0 copy-start.8
  4.8 5.1 %bias_rows.1 = (f32[3456,128]{1,0:T(8,128)S(1)}, f32[3456,128]{1,0:T(8,128)S(1)}) custom-call(f32[6,4,3312]{2,1,0:T(4,128)S(1)} %get-tuple-element.53.table_ref, s32[144,144]{1,0:T(8,128)S(1)} %get-tuple-element.54.index_ref, s32[2,24]{1,0:T(2,128)} %regions_ref.1), custom_call_target="tpu_custom_call" | custom-call | flops 14000000000 | bytes 4000000 | tf_op jit(solution)/shard_map/bias_rows/pallas_call | solution.py:256
  9.9 13.1 %collective-permute-done.1.west_cotangent_ref = bf16[12,3,2,384]{3,2,1,0:T(2,128)(2,1)S(1)} collective-permute-done((bf16[12,3,2,384]{3,2,1,0:T(2,128)(2,1)S(1)}, bf16[12,3,2,384]{3,2,1,0:T(2,128)(2,1)S(1)}, u32[]{:S(2)}, u32[]{:S(2)}) %collective-permute-start.1) | collective-permute-done | bytes 55328 | tf_op jit(solution)/shard_map/ppermute | solution.py:771
  23.1 0.3 collective-permute-done.west_ref
  23.3 0.0 copy-done
  23.3 0.0 copy-done.1
  23.3 0.0 copy-done.2
  23.4 0.0 copy-done.3
  23.4 0.0 copy-done.4
  23.4 0.0 copy-done.5
  23.4 0.0 copy-done.6
  23.4 0.0 copy-done.7
  23.4 0.0 copy-done.8
  23.4 9.2 %block.1 = (bf16[6400,128]{1,0:T(8,128)(2,1)S(1)}, bf16[576,192]{1,0:T(8,128)(2,1)S(1)}, bf16[4224,128]{1,0:T(8,128)(2,1)S(1)}, bf16[4,160,192]{2,1,0:T(8,128)(2...) custom-call(bf16[2,12,24,192]{3,2,1,0:T(8,128)(2,1)S(1)} %bitcast.18, ...), custom_call_target="tpu_custom_call" | custom-call | flops 24000000000 | bytes 12000000 | tf_op jit(solution)/shard_map/block/pallas_call | solution.py:472
  32.6 8.0 %collective-permute-start.3 = (bf16[4224,128]{1,0:T(8,128)(2,1)S(1)}, bf16[4224,128]{1,0:T(8,128)(2,1)S(1)}, u32[]{:S(2)}, u32[]{:S(2)}) collective-permute-start(bf16[4224,128]{1,0:T(8,128)(2,1)S(1)} %get-tuple-element.62.own_ref), channel_id=1, source_target_pairs={{0,1},{1,0},{2,3},{3,2},{4,5},{5,4},{6,7},{7,6},{8,9},{9,8},{10,11... | collective-permute-start | bytes 3244040 | tf_op jit(solution)/shard_map/ppermute | solution.py:853
  40.6 0.6 pack.1
  41.2 0.2 collective-permute-start.2
  41.3 1.6 %collective-permute-done.3.partner_ref = bf16[4224,128]{1,0:T(8,128)(2,1)S(1)} collective-permute-done((bf16[4224,128]{1,0:T(8,128)(2,1)S(1)}, bf16[4224,128]{1,0:T(8,128)(2,1)S(1)}, u32[]{:S(2)}, u32[]{:S(2)}) %collective-permute-start.3) | collective-permute-done | bytes 1081376 | tf_op jit(solution)/shard_map/ppermute | solution.py:853
  43.0 1.1 collective-permute-done.2.arrived_ref
  44.1 1.1 join.1
  45.2 4.3 %all-to-all-start = ((bf16[4,800,128]{2,1,0:T(8,128)(2,1)}), bf16[4,800,128]{2,1,0:T(8,128)(2,1)}, u32[]{:S(2)}, u32[]{:S(2)}) async-start(bf16[4,800,128]{2,1,0:T(8,128)(2,1)} %bitcast.7), calls=%async_computation | async-start | bytes 1638400 | tf_op jit(solution)/shard_map/all_to_all | solution.py:790
  49.5 1.4 %to_grid.1 = (bf16[12,3,2,384]{3,2,1,0:T(2,128)(2,1)S(1)}, bf16[2,6,24,192]{3,2,1,0:T(8,128)(2,1)S(1)}, bf16[9,24,384]{2,1,0:T(8,128)(2,1)S(1)}) custom-call(bf16[4,160,192]{2,1,0:T(8,128)(2,1)S(1)} %get-tuple-element.63.normed_merge_ref, bf16[576,576]{1,0:T(8,128)(2,1)S(1)} %get-tuple-element.59.triple_ref, ...), custom_call_target="tpu_custom_call" | custom-call | flops 1500000000 | bytes 3000000 | tf_op jit(solution)/shard_map/to_grid/pallas_call | solution.py:623
  50.9 3.0 %collective-permute-start.4 = (bf16[9,24,384]{2,1,0:T(8,128)(2,1)S(1)}, bf16[9,24,384]{2,1,0:T(8,128)(2,1)S(1)}, u32[]{:S(2)}, u32[]{:S(2)}) collective-permute-start(bf16[9,24,384]{2,1,0:T(8,128)(2,1)S(1)} %get-tuple-element.67), channel_id=1, source_target_pairs={{0,1},{1,0},{2,3},{3,2},{4,5},{5,4},{6,7},{7,6},{8,9},{9,8},{10,11... | collective-permute-start | bytes 497672 | tf_op jit(solution)/shard_map/ppermute | solution.py:856
  53.9 5.1 %all-to-all-done = bf16[4,800,128]{2,1,0:T(8,128)(2,1)} async-done(((bf16[4,800,128]{2,1,0:T(8,128)(2,1)}), bf16[4,800,128]{2,1,0:T(8,128)(2,1)}, u32[]{:S(2)}, u32[]{:S(2)}) %all-to-all-start) | async-done | bytes 819232 | tf_op jit(solution)/shard_map/all_to_all | solution.py:790
  59.0 1.3 %reduce_sum.24 = bf16[800,128]{1,0:T(8,128)(2,1)S(1)} reduce(bf16[4,800,128]{2,1,0:T(8,128)(2,1)} %all-to-all-done, bf16[]{:T(256)} %constant.20.clone.1), dimensions={0}, to_apply=%region_0.1 | reduce | flops 307200 | bytes 1024002 | tf_op jit(solution)/shard_map/reduce_sum | solution.py:794
  60.4 0.0 collective-permute-done.4.refs_2_
  60.4 15.1 %all_to_all.20 = bf16[16,25,2,128]{3,2,1,0:T(2,128)(2,1)S(1)} all-to-all(bf16[16,25,2,128]{3,2,1,0:T(2,128)(2,1)S(1)} %bitcast.25), channel_id=1, replica_groups={{0,8,16,24,32,40,48,56,64,72,80,88,96,104,112,120},{1,9,17,25,33,41,49,..., dimensions={0} | all-to-all | bytes 409600 | tf_op jit(solution)/shard_map/all_to_all | solution.py:790
  75.5 0.2 reduce_sum.25
  75.7 0.1 broadcast_in_dim.6
  75.8 17.3 %all_to_all.21 = bf16[16,25,2,128]{3,2,1,0:T(2,128)(2,1)S(1)} all-to-all(bf16[16,25,2,128]{3,2,1,0:T(2,128)(2,1)S(1)} %broadcast_in_dim.6), channel_id=1, replica_groups={{0,8,16,24,32,40,48,56,64,72,80,88,96,104,112,120},{1,9,17,25,33,41,49,..., dimensions={0} | all-to-all | bytes 409600 | tf_op jit(solution)/shard_map/all_to_all | solution.py:790
  93.1 0.1 broadcast_in_dim.15
  93.2 10.9 %all_to_all.22 = bf16[4,800,128]{2,1,0:T(8,128)(2,1)S(1)} all-to-all(bf16[4,800,128]{2,1,0:T(8,128)(2,1)S(1)} %broadcast_in_dim.15), channel_id=1, replica_groups={{0,2,4,6},{1,3,5,7},{8,10,12,14},{9,11,13,15},{16,18,20,22},{17,19,21,2..., dimensions={0} | all-to-all | bytes 1638400 | tf_op jit(solution)/shard_map/all_to_all | solution.py:790
  104.1 7.7 %collective-permute-start.6 = (bf16[3200,128]{1,0:T(8,128)(2,1)S(1)}, bf16[3200,128]{1,0:T(8,128)(2,1)S(1)}, u32[]{:S(2)}, u32[]{:S(2)}) collective-permute-start(bf16[3200,128]{1,0:T(8,128)(2,1)S(1)} %bitcast.15), channel_id=1, source_target_pairs={{0,1},{1,0},{2,3},{3,2},{4,5},{5,4},{6,7},{7,6},{8,9},{9,8},{10,11... | collective-permute-start | bytes 2457608 | tf_op jit(solution)/shard_map/ppermute | solution.py:805
  111.9 6.0 %collective-permute-start.5 = (bf16[9,24,384]{2,1,0:T(8,128)(2,1)S(1)}, bf16[9,24,384]{2,1,0:T(8,128)(2,1)S(1)}, u32[]{:S(2)}, u32[]{:S(2)}) collective-permute-start(bf16[9,24,384]{2,1,0:T(8,128)(2,1)S(1)} %collective-permute-done.4.refs_2_), channel_id=1, source_target_pairs={{1,127},{3,1},{5,3},{7,5},{9,7},{11,9},{13,11},{15,13},{17,15},{19... | collective-permute-start | bytes 497672 | tf_op jit(solution)/shard_map/ppermute | solution.py:860
  117.8 2.3 %collective-permute-done.5.refs_3_ = bf16[9,24,384]{2,1,0:T(8,128)(2,1)S(1)} collective-permute-done((bf16[9,24,384]{2,1,0:T(8,128)(2,1)S(1)}, bf16[9,24,384]{2,1,0:T(8,128)(2,1)S(1)}, u32[]{:S(2)}, u32[]{:S(2)}) %collective-permute-start.5) | collective-permute-done | bytes 165920 | tf_op jit(solution)/shard_map/ppermute | solution.py:860
  120.1 1.5 %finish_own.1 = (bf16[12,6,2,384]{3,2,1,0:T(2,128)(2,1)}, bf16[2,12,24,192]{3,2,1,0:T(8,128)(2,1)}, f32[192,768]{1,0:T(8,128)}, f32[192,768]{1,0:T(8,128)}, f32[...) custom-call(s32[1]{0:T(128)} %bitcast.3.core_ref.refs_0_, ...), custom_call_target="tpu_custom_call" | custom-call | flops 400000 | bytes 2500000 | tf_op jit(solution)/shard_map/finish_own/pallas_call | solution.py:746
  121.5 0.0 collective-permute-done.6.refs_1_
  121.6 1.3 %finish_other.1 = (f32[192,768]{1,0:T(8,128)}, f32[192,768]{1,0:T(8,128)}, f32[192,576]{1,0:T(8,128)}, f32[768,384]{1,0:T(8,128)}, f32[192,192]{1,0:T(8,128)}, /*index=5*/f32[6,4,3312]{2,1,0:T(4,128)}) custom-call(s32[1]{0:T(128)} %bitcast.3.core_ref.refs_0_, ...), custom_call_target="tpu_custom_call", output_to_operand_aliasing={{0}: (2, {}), {1}: (3, {}), {2}: (4, {}), {3}: (5, {}), {4}... | custom-call | tf_op jit(solution)/shard_map/finish_other/pallas_call | solution.py:756
  (1 shorter events, 0.0 us)
Async XLA Ops:
  1.8 21.3 %collective-permute-start.1 = (bf16[12,3,2,384]{3,2,1,0:T(2,128)(2,1)S(1)}, bf16[12,3,2,384]{3,2,1,0:T(2,128)(2,1)S(1)}, u32[]{:S(2)}, u32[]{:S(2)}) collective-permute-start(bf16[12,3,2,384]{3,2,1,0:T(2,128)(2,1)S(1)} %get-tuple-element.51), channel_id=1, source_target_pairs={{0,1},{1,2},{2,3},{3,4},{4,5},{5,6},{6,7},{7,8},{8,9},{9,10},{10,1... | collective-permute-start | bytes 165896 | tf_op jit(solution)/shard_map/ppermute | solution.py:771
  4.6 18.8 %collective-permute-start = (bf16[2,6,24,192]{3,2,1,0:T(8,128)(2,1)S(1)}, bf16[2,6,24,192]{3,2,1,0:T(8,128)(2,1)S(1)}, u32[]{:S(2)}, u32[]{:S(2)}) collective-permute-start(bf16[2,6,24,192]{3,2,1,0:T(8,128)(2,1)S(1)} %get-tuple-element.50), channel_id=1, source_target_pairs={{0,1},{1,2},{2,3},{3,4},{4,5},{5,6},{6,7},{7,8},{8,9},{9,10},{10,1... | collective-permute-start | bytes 331784 | tf_op jit(solution)/shard_map/ppermute | solution.py:771
  4.7 18.6 %copy-start = (bf16[2,24,12,192]{3,1,2,0:T(8,128)(2,1)S(1)}, bf16[2,24,12,192]{3,1,2,0:T(8,128)(2,1)}, u32[]{:S(2)}) copy-start(bf16[2,24,12,192]{3,1,2,0:T(8,128)(2,1)} %param.13) | copy-start | bytes 663556
  4.7 18.6 %copy-start.1 = (bf16[2,12,6,384]{3,0,2,1:T(2,128)(2,1)S(1)}, bf16[2,12,6,384]{3,0,2,1:T(2,128)(2,1)}, u32[]{:S(2)}) copy-start(bf16[2,12,6,384]{3,0,2,1:T(2,128)(2,1)} %param.25) | copy-start | bytes 331780
  4.7 18.6 %copy-start.2 = (bf16[768,384]{1,0:T(8,128)(2,1)S(1)}, bf16[768,384]{1,0:T(8,128)(2,1)}, u32[]{:S(2)}) copy-start(bf16[768,384]{1,0:T(8,128)(2,1)} %merge_ref.3) | copy-start | bytes 1769476
  4.7 18.6 %copy-start.3 = (bf16[192,768]{1,0:T(8,128)(2,1)S(1)}, bf16[192,768]{1,0:T(8,128)(2,1)}, u32[]{:S(2)}) copy-start(bf16[192,768]{1,0:T(8,128)(2,1)} %up_ref.1) | copy-start | bytes 884740
  4.7 18.6 %copy-start.4 = (bf16[768,192]{0,1:T(8,128)(2,1)S(1)}, bf16[768,192]{0,1:T(8,128)(2,1)}, u32[]{:S(2)}) copy-start(bf16[768,192]{0,1:T(8,128)(2,1)} %param.22) | copy-start | bytes 884740
  4.7 18.6 %copy-start.5 = (bf16[192,576]{1,0:T(8,128)(2,1)S(1)}, bf16[192,576]{1,0:T(8,128)(2,1)}, u32[]{:S(2)}) copy-start(bf16[192,576]{1,0:T(8,128)(2,1)} %qkv_ref.3) | copy-start | bytes 663556
  4.7 18.6 %copy-start.6 = (bf16[192,192]{1,0:T(8,128)(2,1)S(1)}, bf16[192,192]{1,0:T(8,128)(2,1)}, u32[]{:S(2)}) copy-start(bf16[192,192]{1,0:T(8,128)(2,1)} %proj_ref.1) | copy-start | bytes 221188
  4.8 18.6 %copy-start.7 = (f32[192]{0:T(256)S(1)}, f32[192]{0:T(256)}, u32[]{:S(2)}) copy-start(f32[192]{0:T(256)} %param.20) | copy-start | bytes 2308
  4.8 18.6 %copy-start.8 = (f32[192]{0:T(256)S(1)}, f32[192]{0:T(256)}, u32[]{:S(2)}) copy-start(f32[192]{0:T(256)} %param.14) | copy-start | bytes 2308
  32.6 10.4 %collective-permute-start.3 = (bf16[4224,128]{1,0:T(8,128)(2,1)S(1)}, bf16[4224,128]{1,0:T(8,128)(2,1)S(1)}, u32[]{:S(2)}, u32[]{:S(2)}) collective-permute-start(bf16[4224,128]{1,0:T(8,128)(2,1)S(1)} %get-tuple-element.62.own_ref), channel_id=1, source_target_pairs={{0,1},{1,0},{2,3},{3,2},{4,5},{5,4},{6,7},{7,6},{8,9},{9,8},{10,11... | collective-permute-start | bytes 3244040 | tf_op jit(solution)/shard_map/ppermute | solution.py:853
  41.2 2.9 %collective-permute-start.2 = (bf16[3200,128]{1,0:T(8,128)(2,1)S(1)}, bf16[3200,128]{1,0:T(8,128)(2,1)S(1)}, u32[]{:S(2)}, u32[]{:S(2)}) collective-permute-start(bf16[3200,128]{1,0:T(8,128)(2,1)S(1)} %get-tuple-element.61), channel_id=1, source_target_pairs={{0,1},{1,0},{2,3},{3,2},{4,5},{5,4},{6,7},{7,6},{8,9},{9,8},{10,11... | collective-permute-start | bytes 2457608 | tf_op jit(solution)/shard_map/ppermute | solution.py:786
  45.2 13.8 %all-to-all-start = ((bf16[4,800,128]{2,1,0:T(8,128)(2,1)}), bf16[4,800,128]{2,1,0:T(8,128)(2,1)}, u32[]{:S(2)}, u32[]{:S(2)}) async-start(bf16[4,800,128]{2,1,0:T(8,128)(2,1)} %bitcast.7), calls=%async_computation | async-start | bytes 1638400 | tf_op jit(solution)/shard_map/all_to_all | solution.py:790
  50.9 9.5 %collective-permute-start.4 = (bf16[9,24,384]{2,1,0:T(8,128)(2,1)S(1)}, bf16[9,24,384]{2,1,0:T(8,128)(2,1)S(1)}, u32[]{:S(2)}, u32[]{:S(2)}) collective-permute-start(bf16[9,24,384]{2,1,0:T(8,128)(2,1)S(1)} %get-tuple-element.67), channel_id=1, source_target_pairs={{0,1},{1,0},{2,3},{3,2},{4,5},{5,4},{6,7},{7,6},{8,9},{9,8},{10,11... | collective-permute-start | bytes 497672 | tf_op jit(solution)/shard_map/ppermute | solution.py:856
  104.1 17.4 %collective-permute-start.6 = (bf16[3200,128]{1,0:T(8,128)(2,1)S(1)}, bf16[3200,128]{1,0:T(8,128)(2,1)S(1)}, u32[]{:S(2)}, u32[]{:S(2)}) collective-permute-start(bf16[3200,128]{1,0:T(8,128)(2,1)S(1)} %bitcast.15), channel_id=1, source_target_pairs={{0,1},{1,0},{2,3},{3,2},{4,5},{5,4},{6,7},{7,6},{8,9},{9,8},{10,11... | collective-permute-start | bytes 2457608 | tf_op jit(solution)/shard_map/ppermute | solution.py:805
  111.9 8.2 %collective-permute-start.5 = (bf16[9,24,384]{2,1,0:T(8,128)(2,1)S(1)}, bf16[9,24,384]{2,1,0:T(8,128)(2,1)S(1)}, u32[]{:S(2)}, u32[]{:S(2)}) collective-permute-start(bf16[9,24,384]{2,1,0:T(8,128)(2,1)S(1)} %collective-permute-done.4.refs_2_), channel_id=1, source_target_pairs={{1,127},{3,1},{5,3},{7,5},{9,7},{11,9},{13,11},{15,13},{17,15},{19... | collective-permute-start | bytes 497672 | tf_op jit(solution)/shard_map/ppermute | solution.py:860

commit v8 on v7

--- a/solution.py
+++ b/solution.py
@@ -186,11 +186,11 @@
     def row_block(block, carry):
         base = pl.multiple_of(block * 8, 8)
         rows = index_ref[pl.ds(base, 8), :MAIN]
-        for part in range(2):
-            index = jnp.concatenate([rows[4 * part + n : 4 * part + n + 1] for n in range(4)], axis=1)
+        for part in range(4):
+            index = jnp.concatenate([rows[2 * part + n : 2 * part + n + 1] for n in range(2)], axis=1)
             got = looked_up(index)
-            for n in range(4):
-                row = base + 4 * part + n
+            for n in range(2):
+                row = base + 2 * part + n
                 mask = mask_ref[pl.ds(pl.multiple_of(div(row, 12) * TH, 8), TH), :]
                 main_ref[pl.ds(row, TH, stride=WIN), :] = got[:, n * MAIN : (n + 1) * MAIN] + mask
         return carry

time: 123 us -> 123 us (level)
  no operation moved by 1% of the time
where the time goes in v8:
time: 123 us
  blocking collectives  43.3 us (35%)
  starting transfers between devices  32.1 us (26%)
  waiting for transfers between devices  23.9 us (19%)
  Pallas kernels  20.9 us (17%)
  other arithmetic  1.5 us (1%)
    all_to_all x3, blocking collectives, exchanged(): lax.all_to_all(value, axis, 0, 0, axis_index_groups=groups_of(count, apar...  43.3 us
    ppermute x2, waiting for transfers between devices, passed_along(): lax.ppermute(value, axis, [(source, (source + steps) % count) for source...  13.7 us
    pallas_call x1, Pallas kernels, block(): pl.pallas_call(block_kernel, out_shape=[shape((2 * half_rows, LANES), BF)...  9.18 us
    ppermute x1, starting transfers between devices, local(): partner_scores = lax.ppermute(scores, 'lon', pairs)  8.03 us
    ppermute x1, starting transfers between devices, summed_over(): return (held, lax.ppermute(held, axis, pairs), partner, forwarded)  7.74 us
    ppermute x1, starting transfers between devices, forward(): lax.ppermute(leaving, 'lon', [(i, (i - CORES) % count) for i in range(1,...  5.95 us
    all_to_all x1, waiting for transfers between devices, exchanged(): lax.all_to_all(value, axis, 0, 0, axis_index_groups=groups_of(count, apar...  5.1 us
    pallas_call x1, Pallas kernels, bias_rows(): pl.pallas_call(bias_kernel, out_shape=[jax.ShapeDtypeStruct((TH * WIN, LA...  4.82 us
  transfers between devices with their start and end apart: 8, of which 6 were waited for; matrix products, arithmetic and copies ran while one was open for 1% of the time, Pallas kernels for 7%

profile of v8, /device:TPU:33, one launch (start us, length us, event | category | flops | bytes accessed | tf_op | source)
XLA Modules:
  0.0 123.0 jit_solution(14354091006652876440)
XLA Ops:
  0.6 1.2 stage.1
  1.8 2.8 %collective-permute-start.1 = (bf16[12,3,2,384]{3,2,1,0:T(2,128)(2,1)S(1)}, bf16[12,3,2,384]{3,2,1,0:T(2,128)(2,1)S(1)}, u32[]{:S(2)}, u32[]{:S(2)}) collective-permute-start(bf16[12,3,2,384]{3,2,1,0:T(2,128)(2,1)S(1)} %get-tuple-element.51), channel_id=1, source_target_pairs={{0,1},{1,2},{2,3},{3,4},{4,5},{5,6},{6,7},{7,8},{8,9},{9,10},{10,1... | collective-permute-start | bytes 165896 | tf_op jit(solution)/shard_map/ppermute | solution.py:771
  4.6 0.1 collective-permute-start
  4.7 0.0 copy-start
  4.7 0.0 copy-start.1
  4.7 0.0 copy-start.2
  4.7 0.0 copy-start.3
  4.7 0.0 copy-start.4
  4.7 0.0 copy-start.5
  4.7 0.0 copy-start.6
  4.8 0.0 copy-start.7
  4.8 0.0 copy-start.8
  4.8 4.8 %bias_rows.1 = (f32[3456,128]{1,0:T(8,128)S(1)}, f32[3456,128]{1,0:T(8,128)S(1)}) custom-call(f32[6,4,3312]{2,1,0:T(4,128)S(1)} %get-tuple-element.53.table_ref, s32[144,144]{1,0:T(8,128)S(1)} %get-tuple-element.54.index_ref, s32[2,24]{1,0:T(2,128)} %regions_ref.1), custom_call_target="tpu_custom_call" | custom-call | flops 14000000000 | bytes 4000000 | tf_op jit(solution)/shard_map/bias_rows/pallas_call | solution.py:256
  9.6 13.5 %collective-permute-done.1.west_cotangent_ref = bf16[12,3,2,384]{3,2,1,0:T(2,128)(2,1)S(1)} collective-permute-done((bf16[12,3,2,384]{3,2,1,0:T(2,128)(2,1)S(1)}, bf16[12,3,2,384]{3,2,1,0:T(2,128)(2,1)S(1)}, u32[]{:S(2)}, u32[]{:S(2)}) %collective-permute-start.1) | collective-permute-done | bytes 55328 | tf_op jit(solution)/shard_map/ppermute | solution.py:771
  23.1 0.3 collective-permute-done.west_ref
  23.3 0.0 copy-done
  23.3 0.0 copy-done.1
  23.3 0.0 copy-done.2
  23.4 0.0 copy-done.3
  23.4 0.0 copy-done.4
  23.4 0.0 copy-done.5
  23.4 0.0 copy-done.6
  23.4 0.0 copy-done.7
  23.4 0.0 copy-done.8
  23.4 9.2 %block.1 = (bf16[6400,128]{1,0:T(8,128)(2,1)S(1)}, bf16[576,192]{1,0:T(8,128)(2,1)S(1)}, bf16[4224,128]{1,0:T(8,128)(2,1)S(1)}, bf16[4,160,192]{2,1,0:T(8,128)(2...) custom-call(bf16[2,12,24,192]{3,2,1,0:T(8,128)(2,1)S(1)} %bitcast.18, ...), custom_call_target="tpu_custom_call" | custom-call | flops 24000000000 | bytes 12000000 | tf_op jit(solution)/shard_map/block/pallas_call | solution.py:472
  32.6 8.0 %collective-permute-start.3 = (bf16[4224,128]{1,0:T(8,128)(2,1)S(1)}, bf16[4224,128]{1,0:T(8,128)(2,1)S(1)}, u32[]{:S(2)}, u32[]{:S(2)}) collective-permute-start(bf16[4224,128]{1,0:T(8,128)(2,1)S(1)} %get-tuple-element.62.own_ref), channel_id=1, source_target_pairs={{0,1},{1,0},{2,3},{3,2},{4,5},{5,4},{6,7},{7,6},{8,9},{9,8},{10,11... | collective-permute-start | bytes 3244040 | tf_op jit(solution)/shard_map/ppermute | solution.py:853
  40.6 0.5 pack.1
  41.2 0.2 collective-permute-start.2
  41.3 1.6 %collective-permute-done.3.partner_ref = bf16[4224,128]{1,0:T(8,128)(2,1)S(1)} collective-permute-done((bf16[4224,128]{1,0:T(8,128)(2,1)S(1)}, bf16[4224,128]{1,0:T(8,128)(2,1)S(1)}, u32[]{:S(2)}, u32[]{:S(2)}) %collective-permute-start.3) | collective-permute-done | bytes 1081376 | tf_op jit(solution)/shard_map/ppermute | solution.py:853
  43.0 1.1 collective-permute-done.2.arrived_ref
  44.1 1.1 join.1
  45.2 4.3 %all-to-all-start = ((bf16[4,800,128]{2,1,0:T(8,128)(2,1)}), bf16[4,800,128]{2,1,0:T(8,128)(2,1)}, u32[]{:S(2)}, u32[]{:S(2)}) async-start(bf16[4,800,128]{2,1,0:T(8,128)(2,1)} %bitcast.7), calls=%async_computation | async-start | bytes 1638400 | tf_op jit(solution)/shard_map/all_to_all | solution.py:790
  49.5 1.4 %to_grid.1 = (bf16[12,3,2,384]{3,2,1,0:T(2,128)(2,1)S(1)}, bf16[2,6,24,192]{3,2,1,0:T(8,128)(2,1)S(1)}, bf16[9,24,384]{2,1,0:T(8,128)(2,1)S(1)}) custom-call(bf16[4,160,192]{2,1,0:T(8,128)(2,1)S(1)} %get-tuple-element.63.normed_merge_ref, bf16[576,576]{1,0:T(8,128)(2,1)S(1)} %get-tuple-element.59.triple_ref, ...), custom_call_target="tpu_custom_call" | custom-call | flops 1500000000 | bytes 3000000 | tf_op jit(solution)/shard_map/to_grid/pallas_call | solution.py:623
  50.9 3.0 %collective-permute-start.4 = (bf16[9,24,384]{2,1,0:T(8,128)(2,1)S(1)}, bf16[9,24,384]{2,1,0:T(8,128)(2,1)S(1)}, u32[]{:S(2)}, u32[]{:S(2)}) collective-permute-start(bf16[9,24,384]{2,1,0:T(8,128)(2,1)S(1)} %get-tuple-element.67), channel_id=1, source_target_pairs={{0,1},{1,0},{2,3},{3,2},{4,5},{5,4},{6,7},{7,6},{8,9},{9,8},{10,11... | collective-permute-start | bytes 497672 | tf_op jit(solution)/shard_map/ppermute | solution.py:856
  53.9 5.1 %all-to-all-done = bf16[4,800,128]{2,1,0:T(8,128)(2,1)} async-done(((bf16[4,800,128]{2,1,0:T(8,128)(2,1)}), bf16[4,800,128]{2,1,0:T(8,128)(2,1)}, u32[]{:S(2)}, u32[]{:S(2)}) %all-to-all-start) | async-done | bytes 819232 | tf_op jit(solution)/shard_map/all_to_all | solution.py:790
  59.0 1.3 %reduce_sum.24 = bf16[800,128]{1,0:T(8,128)(2,1)S(1)} reduce(bf16[4,800,128]{2,1,0:T(8,128)(2,1)} %all-to-all-done, bf16[]{:T(256)} %constant.20.clone.1), dimensions={0}, to_apply=%region_0.1 | reduce | flops 307200 | bytes 1024002 | tf_op jit(solution)/shard_map/reduce_sum | solution.py:794
  60.3 0.0 collective-permute-done.4.refs_2_
  60.3 15.1 %all_to_all.20 = bf16[16,25,2,128]{3,2,1,0:T(2,128)(2,1)S(1)} all-to-all(bf16[16,25,2,128]{3,2,1,0:T(2,128)(2,1)S(1)} %bitcast.25), channel_id=1, replica_groups={{0,8,16,24,32,40,48,56,64,72,80,88,96,104,112,120},{1,9,17,25,33,41,49,..., dimensions={0} | all-to-all | bytes 409600 | tf_op jit(solution)/shard_map/all_to_all | solution.py:790
  75.5 0.2 reduce_sum.25
  75.7 0.1 broadcast_in_dim.6
  75.8 17.3 %all_to_all.21 = bf16[16,25,2,128]{3,2,1,0:T(2,128)(2,1)S(1)} all-to-all(bf16[16,25,2,128]{3,2,1,0:T(2,128)(2,1)S(1)} %broadcast_in_dim.6), channel_id=1, replica_groups={{0,8,16,24,32,40,48,56,64,72,80,88,96,104,112,120},{1,9,17,25,33,41,49,..., dimensions={0} | all-to-all | bytes 409600 | tf_op jit(solution)/shard_map/all_to_all | solution.py:790
  93.1 0.1 broadcast_in_dim.15
  93.2 10.9 %all_to_all.22 = bf16[4,800,128]{2,1,0:T(8,128)(2,1)S(1)} all-to-all(bf16[4,800,128]{2,1,0:T(8,128)(2,1)S(1)} %broadcast_in_dim.15), channel_id=1, replica_groups={{0,2,4,6},{1,3,5,7},{8,10,12,14},{9,11,13,15},{16,18,20,22},{17,19,21,2..., dimensions={0} | all-to-all | bytes 1638400 | tf_op jit(solution)/shard_map/all_to_all | solution.py:790
  104.1 7.7 %collective-permute-start.6 = (bf16[3200,128]{1,0:T(8,128)(2,1)S(1)}, bf16[3200,128]{1,0:T(8,128)(2,1)S(1)}, u32[]{:S(2)}, u32[]{:S(2)}) collective-permute-start(bf16[3200,128]{1,0:T(8,128)(2,1)S(1)} %bitcast.15), channel_id=1, source_target_pairs={{0,1},{1,0},{2,3},{3,2},{4,5},{5,4},{6,7},{7,6},{8,9},{9,8},{10,11... | collective-permute-start | bytes 2457608 | tf_op jit(solution)/shard_map/ppermute | solution.py:805
  111.8 6.0 %collective-permute-start.5 = (bf16[9,24,384]{2,1,0:T(8,128)(2,1)S(1)}, bf16[9,24,384]{2,1,0:T(8,128)(2,1)S(1)}, u32[]{:S(2)}, u32[]{:S(2)}) collective-permute-start(bf16[9,24,384]{2,1,0:T(8,128)(2,1)S(1)} %collective-permute-done.4.refs_2_), channel_id=1, source_target_pairs={{1,127},{3,1},{5,3},{7,5},{9,7},{11,9},{13,11},{15,13},{17,15},{19... | collective-permute-start | bytes 497672 | tf_op jit(solution)/shard_map/ppermute | solution.py:860
  117.8 2.3 %collective-permute-done.5.refs_3_ = bf16[9,24,384]{2,1,0:T(8,128)(2,1)S(1)} collective-permute-done((bf16[9,24,384]{2,1,0:T(8,128)(2,1)S(1)}, bf16[9,24,384]{2,1,0:T(8,128)(2,1)S(1)}, u32[]{:S(2)}, u32[]{:S(2)}) %collective-permute-start.5) | collective-permute-done | bytes 165920 | tf_op jit(solution)/shard_map/ppermute | solution.py:860
  120.1 1.5 %finish_own.1 = (bf16[12,6,2,384]{3,2,1,0:T(2,128)(2,1)}, bf16[2,12,24,192]{3,2,1,0:T(8,128)(2,1)}, f32[192,768]{1,0:T(8,128)}, f32[192,768]{1,0:T(8,128)}, f32[...) custom-call(s32[1]{0:T(128)} %bitcast.3.core_ref.refs_0_, ...), custom_call_target="tpu_custom_call" | custom-call | flops 400000 | bytes 2500000 | tf_op jit(solution)/shard_map/finish_own/pallas_call | solution.py:746
  121.5 0.0 collective-permute-done.6.refs_1_
  121.5 1.3 %finish_other.1 = (f32[192,768]{1,0:T(8,128)}, f32[192,768]{1,0:T(8,128)}, f32[192,576]{1,0:T(8,128)}, f32[768,384]{1,0:T(8,128)}, f32[192,192]{1,0:T(8,128)}, /*index=5*/f32[6,4,3312]{2,1,0:T(4,128)}) custom-call(s32[1]{0:T(128)} %bitcast.3.core_ref.refs_0_, ...), custom_call_target="tpu_custom_call", output_to_operand_aliasing={{0}: (2, {}), {1}: (3, {}), {2}: (4, {}), {3}: (5, {}), {4}... | custom-call | tf_op jit(solution)/shard_map/finish_other/pallas_call | solution.py:756
  (1 shorter events, 0.0 us)
Async XLA Ops:
  1.8 21.3 %collective-permute-start.1 = (bf16[12,3,2,384]{3,2,1,0:T(2,128)(2,1)S(1)}, bf16[12,3,2,384]{3,2,1,0:T(2,128)(2,1)S(1)}, u32[]{:S(2)}, u32[]{:S(2)}) collective-permute-start(bf16[12,3,2,384]{3,2,1,0:T(2,128)(2,1)S(1)} %get-tuple-element.51), channel_id=1, source_target_pairs={{0,1},{1,2},{2,3},{3,4},{4,5},{5,6},{6,7},{7,8},{8,9},{9,10},{10,1... | collective-permute-start | bytes 165896 | tf_op jit(solution)/shard_map/ppermute | solution.py:771
  4.6 18.8 %collective-permute-start = (bf16[2,6,24,192]{3,2,1,0:T(8,128)(2,1)S(1)}, bf16[2,6,24,192]{3,2,1,0:T(8,128)(2,1)S(1)}, u32[]{:S(2)}, u32[]{:S(2)}) collective-permute-start(bf16[2,6,24,192]{3,2,1,0:T(8,128)(2,1)S(1)} %get-tuple-element.50), channel_id=1, source_target_pairs={{0,1},{1,2},{2,3},{3,4},{4,5},{5,6},{6,7},{7,8},{8,9},{9,10},{10,1... | collective-permute-start | bytes 331784 | tf_op jit(solution)/shard_map/ppermute | solution.py:771
  4.7 18.6 %copy-start = (bf16[2,24,12,192]{3,1,2,0:T(8,128)(2,1)S(1)}, bf16[2,24,12,192]{3,1,2,0:T(8,128)(2,1)}, u32[]{:S(2)}) copy-start(bf16[2,24,12,192]{3,1,2,0:T(8,128)(2,1)} %param.13) | copy-start | bytes 663556
  4.7 18.6 %copy-start.1 = (bf16[2,12,6,384]{3,0,2,1:T(2,128)(2,1)S(1)}, bf16[2,12,6,384]{3,0,2,1:T(2,128)(2,1)}, u32[]{:S(2)}) copy-start(bf16[2,12,6,384]{3,0,2,1:T(2,128)(2,1)} %param.25) | copy-start | bytes 331780
  4.7 18.6 %copy-start.2 = (bf16[768,384]{1,0:T(8,128)(2,1)S(1)}, bf16[768,384]{1,0:T(8,128)(2,1)}, u32[]{:S(2)}) copy-start(bf16[768,384]{1,0:T(8,128)(2,1)} %merge_ref.3) | copy-start | bytes 1769476
  4.7 18.6 %copy-start.3 = (bf16[192,768]{1,0:T(8,128)(2,1)S(1)}, bf16[192,768]{1,0:T(8,128)(2,1)}, u32[]{:S(2)}) copy-start(bf16[192,768]{1,0:T(8,128)(2,1)} %up_ref.1) | copy-start | bytes 884740
  4.7 18.6 %copy-start.4 = (bf16[768,192]{0,1:T(8,128)(2,1)S(1)}, bf16[768,192]{0,1:T(8,128)(2,1)}, u32[]{:S(2)}) copy-start(bf16[768,192]{0,1:T(8,128)(2,1)} %param.22) | copy-start | bytes 884740
  4.7 18.6 %copy-start.5 = (bf16[192,576]{1,0:T(8,128)(2,1)S(1)}, bf16[192,576]{1,0:T(8,128)(2,1)}, u32[]{:S(2)}) copy-start(bf16[192,576]{1,0:T(8,128)(2,1)} %qkv_ref.3) | copy-start | bytes 663556
  4.7 18.6 %copy-start.6 = (bf16[192,192]{1,0:T(8,128)(2,1)S(1)}, bf16[192,192]{1,0:T(8,128)(2,1)}, u32[]{:S(2)}) copy-start(bf16[192,192]{1,0:T(8,128)(2,1)} %proj_ref.1) | copy-start | bytes 221188
  4.8 18.6 %copy-start.7 = (f32[192]{0:T(256)S(1)}, f32[192]{0:T(256)}, u32[]{:S(2)}) copy-start(f32[192]{0:T(256)} %param.20) | copy-start | bytes 2308
  4.8 18.6 %copy-start.8 = (f32[192]{0:T(256)S(1)}, f32[192]{0:T(256)}, u32[]{:S(2)}) copy-start(f32[192]{0:T(256)} %param.14) | copy-start | bytes 2308
  32.6 10.4 %collective-permute-start.3 = (bf16[4224,128]{1,0:T(8,128)(2,1)S(1)}, bf16[4224,128]{1,0:T(8,128)(2,1)S(1)}, u32[]{:S(2)}, u32[]{:S(2)}) collective-permute-start(bf16[4224,128]{1,0:T(8,128)(2,1)S(1)} %get-tuple-element.62.own_ref), channel_id=1, source_target_pairs={{0,1},{1,0},{2,3},{3,2},{4,5},{5,4},{6,7},{7,6},{8,9},{9,8},{10,11... | collective-permute-start | bytes 3244040 | tf_op jit(solution)/shard_map/ppermute | solution.py:853
  41.2 2.9 %collective-permute-start.2 = (bf16[3200,128]{1,0:T(8,128)(2,1)S(1)}, bf16[3200,128]{1,0:T(8,128)(2,1)S(1)}, u32[]{:S(2)}, u32[]{:S(2)}) collective-permute-start(bf16[3200,128]{1,0:T(8,128)(2,1)S(1)} %get-tuple-element.61), channel_id=1, source_target_pairs={{0,1},{1,0},{2,3},{3,2},{4,5},{5,4},{6,7},{7,6},{8,9},{9,8},{10,11... | collective-permute-start | bytes 2457608 | tf_op jit(solution)/shard_map/ppermute | solution.py:786
  45.2 13.8 %all-to-all-start = ((bf16[4,800,128]{2,1,0:T(8,128)(2,1)}), bf16[4,800,128]{2,1,0:T(8,128)(2,1)}, u32[]{:S(2)}, u32[]{:S(2)}) async-start(bf16[4,800,128]{2,1,0:T(8,128)(2,1)} %bitcast.7), calls=%async_computation | async-start | bytes 1638400 | tf_op jit(solution)/shard_map/all_to_all | solution.py:790
  50.9 9.5 %collective-permute-start.4 = (bf16[9,24,384]{2,1,0:T(8,128)(2,1)S(1)}, bf16[9,24,384]{2,1,0:T(8,128)(2,1)S(1)}, u32[]{:S(2)}, u32[]{:S(2)}) collective-permute-start(bf16[9,24,384]{2,1,0:T(8,128)(2,1)S(1)} %get-tuple-element.67), channel_id=1, source_target_pairs={{0,1},{1,0},{2,3},{3,2},{4,5},{5,4},{6,7},{7,6},{8,9},{9,8},{10,11... | collective-permute-start | bytes 497672 | tf_op jit(solution)/shard_map/ppermute | solution.py:856
  104.1 17.4 %collective-permute-start.6 = (bf16[3200,128]{1,0:T(8,128)(2,1)S(1)}, bf16[3200,128]{1,0:T(8,128)(2,1)S(1)}, u32[]{:S(2)}, u32[]{:S(2)}) collective-permute-start(bf16[3200,128]{1,0:T(8,128)(2,1)S(1)} %bitcast.15), channel_id=1, source_target_pairs={{0,1},{1,0},{2,3},{3,2},{4,5},{5,4},{6,7},{7,6},{8,9},{9,8},{10,11... | collective-permute-start | bytes 2457608 | tf_op jit(solution)/shard_map/ppermute | solution.py:805
  111.8 8.2 %collective-permute-start.5 = (bf16[9,24,384]{2,1,0:T(8,128)(2,1)S(1)}, bf16[9,24,384]{2,1,0:T(8,128)(2,1)S(1)}, u32[]{:S(2)}, u32[]{:S(2)}) collective-permute-start(bf16[9,24,384]{2,1,0:T(8,128)(2,1)S(1)} %collective-permute-done.4.refs_2_), channel_id=1, source_target_pairs={{1,127},{3,1},{5,3},{7,5},{9,7},{11,9},{13,11},{15,13},{17,15},{19... | collective-permute-start | bytes 497672 | tf_op jit(solution)/shard_map/ppermute | solution.py:860

commit v9 on v8

--- a/solution.py
+++ b/solution.py
@@ -212,7 +212,7 @@
         tail_ref[rows, :REST] = jnp.transpose(last_ref[(TH + th) * REST : (TH + th + 1) * REST, :])[:REST]
 
 
-def stage_kernel(fields_ref, cotangent_ref, table_ref, index_ref, gain_ref, field_ref, half_ref, table_out, index_out, gain_out, sems):
+def stage_kernel(fields_ref, cotangent_ref, table_ref, index_ref, gain_ref, leaving_ref, table_out, index_out, gain_out, field_ref, half_ref, cells_ref, sems):
     copies = [
         pltpu.make_async_copy(source, target, sems.at[n])
         for n, (source, target) in enumerate(
@@ -227,7 +227,15 @@
     ]
     for copy in copies:
         copy.start()
-    for copy in copies:
+    for copy in copies[:2]:
+        copy.wait()
+    leaving_ref[:HALF] = jnp.concatenate([field_ref[level].astype(F32) for level in range(LEVELS)], axis=-1).astype(BF)
+    for lat in range(12):
+        for lon in range(HALF // 2):
+            row = (lat * 3 + lon) * 2
+            cells_ref[row : row + 2, :] = half_ref[lat, lon].astype(F32)
+    leaving_ref[HALF:] = cells_ref[...].reshape(3, LAT, 2 * C).astype(BF)
+    for copy in copies[2:]:
         copy.wait()
 
 
@@ -237,15 +245,19 @@
     return pl.pallas_call(
         stage_kernel,
         out_shape=[
-            shape((LEVELS, HALF, LAT, C), BF),
-            shape((12, HALF // 2, LEVELS, 2 * C), BF),
+            shape((HALF + 3, LAT, 2 * C), BF),
             shape(table.shape, F32),
             shape(index.shape, jnp.int32),
             shape((1, 4 * C), F32),
         ],
         in_specs=[pl.BlockSpec(memory_space=pltpu.HBM)] * 5,
-        out_specs=[whole] * 5,
-        scratch_shapes=[pltpu.SemaphoreType.DMA((5,))],
+        out_specs=[whole] * 4,
+        scratch_shapes=[
+            pltpu.VMEM((LEVELS, HALF, LAT, C), BF),
+            pltpu.VMEM((12, HALF // 2, LEVELS, 2 * C), BF),
+            pltpu.VMEM((72, 2 * C), F32),
+            pltpu.SemaphoreType.DMA((5,)),
+        ],
         compiler_params=pltpu.CompilerParams(vmem_limit_bytes=4 * 1024 * 1024),
         name="stage",
     )(*(pltpu.with_memory_space_constraint(a, pltpu.HBM) for a in (fields, cotangent, table, index, gain)))
@@ -273,7 +285,7 @@
 
 
 def block_kernel(
-    own_ref, west_ref, own_cotangent_ref, west_cotangent_ref,
+    own_ref, west_ref, own_cotangent_ref,
     norm_gain_ref, qkv_ref, proj_ref, mlp_gain_ref, up_ref, down_ref, merge_gain_ref, merge_ref,
     bias_ref, bias_tail_ref,
     grads_ref, tokens_ref, ds_ref, normed_merge_ref, triple_ref, grad_attn_ref, unit_ref, scale_ref,
@@ -283,10 +295,11 @@
     cells_ref, grad_merged_ref, scaled_ref,
 ):
     to_tokens = onehot(288, 288, of_row=cell_of_token)
+    west = west_ref[:HALF].astype(F32).reshape(144, 2 * C)
     for level in range(LEVELS):
         cells = jnp.concatenate(
             [
-                west_ref[level].astype(F32).reshape(144, C),
+                west[:, C * level : C * (level + 1)],
                 own_ref[level, :HALF].astype(F32).reshape(144, C),
             ],
             axis=0,
@@ -294,10 +307,10 @@
         ordered = dot(to_tokens, cells)
         for kind in range(TYPES):
             x_ref[WIN * kind + 72 * level : WIN * kind + 72 * level + 72, :] = ordered[72 * kind : 72 * kind + 72]
+    cells_ref[:72, :] = west_ref[HALF:].astype(F32).reshape(72, 2 * C)
     for lat in range(12):
         for lon in range(HALF // 2):
             row = (lat * 3 + lon) * 2
-            cells_ref[row : row + 2, :] = west_cotangent_ref[lat, lon].astype(F32)
             cells_ref[72 + row : 74 + row, :] = own_cotangent_ref[lat, lon].astype(F32)
     grad_merged_ref[...] = dot(onehot(MTOK, 144, of_row=cell_of_merged), cells_ref[...].astype(BF)).astype(BF)
     for n in range(4):
@@ -824,11 +837,10 @@
     core = (lax.axis_index("lon") % CORES).astype(jnp.int32).reshape(1)
     by_lon = fields.transpose(0, 2, 1, 3)
     by_lat = cotangent.transpose(1, 2, 0, 3)
-    field_last, cotangent_last, table, index, merge_gain = stage(
+    leaving, table, index, merge_gain = stage(
         by_lon, by_lat, bias_table.transpose(1, 0, 2), bias_index, merge_gain
     )
-    west = passed_along(field_last, "lon", 1)
-    west_cotangent = passed_along(cotangent_last, "lon", 1)
+    west = passed_along(leaving, "lon", 1)
     table, core = lax.optimization_barrier((table, core))
     bias, bias_tail = bias_rows(table, index, region_ids)
     half_rows = -(-O_END // (count * 2)) * 2 * count // CORES
@@ -837,7 +849,6 @@
         by_lon,
         west,
         by_lat,
-        west_cotangent,
         norm_gain.reshape(1, C),
         qkv_weight,
         proj_weight,

time: 123 us -> 123 us (level)
    ppermute x2 -> x1, starting transfers between devices: 2.91 us -> 2.77 us  [passed_along(): lax.ppermute(value, axis, [(source, (source + steps) % count) for source...]
    ppermute x2 -> x1, waiting for transfers between devices: 13.7 us -> 13.8 us  [passed_along(): lax.ppermute(value, axis, [(source, (source + steps) % count) for source...]
  transfers between devices with their start and end apart: 8 -> 7, of which waited for: 6 -> 5; matrix products, arithmetic and copies ran while one was open for 1% -> 1% of each run, Pallas kernels for 7% -> 7%
where the time goes in v9:
time: 123 us
  blocking collectives  43.4 us (35%)
  starting transfers between devices  31.7 us (26%)
  waiting for transfers between devices  23.8 us (19%)
  Pallas kernels  21 us (17%)
  other arithmetic  1.5 us (1%)
    all_to_all x3, blocking collectives, exchanged(): lax.all_to_all(value, axis, 0, 0, axis_index_groups=groups_of(count, apar...  43.4 us
    ppermute x1, waiting for transfers between devices, passed_along(): lax.ppermute(value, axis, [(source, (source + steps) % count) for source...  13.8 us
    pallas_call x1, Pallas kernels, block(): pl.pallas_call(block_kernel, out_shape=[shape((2 * half_rows, LANES), BF)...  9.25 us
    ppermute x1, starting transfers between devices, local(): partner_scores = lax.ppermute(scores, 'lon', pairs)  7.74 us
    ppermute x1, starting transfers between devices, summed_over(): return (held, lax.ppermute(held, axis, pairs), partner, forwarded)  7.68 us
    ppermute x1, starting transfers between devices, forward(): lax.ppermute(leaving, 'lon', [(i, (i - CORES) % count) for i in range(1,...  5.95 us
    all_to_all x1, waiting for transfers between devices, exchanged(): lax.all_to_all(value, axis, 0, 0, axis_index_groups=groups_of(count, apar...  5.02 us
    pallas_call x1, Pallas kernels, bias_rows(): pl.pallas_call(bias_kernel, out_shape=[jax.ShapeDtypeStruct((TH * WIN, LA...  4.81 us
  transfers between devices with their start and end apart: 7, of which 5 were waited for; matrix products, arithmetic and copies ran while one was open for 1% of the time, Pallas kernels for 7%

profile of v9, /device:TPU:33, one launch (start us, length us, event | category | flops | bytes accessed | tf_op | source)
XLA Modules:
  0.0 122.7 jit_solution(10308422579778598398)
XLA Ops:
  0.6 1.2 stage.1
  1.8 2.8 %collective-permute-start = (bf16[9,24,384]{2,1,0:T(8,128)(2,1)S(1)}, bf16[9,24,384]{2,1,0:T(8,128)(2,1)S(1)}, u32[]{:S(2)}, u32[]{:S(2)}) collective-permute-start(bf16[9,24,384]{2,1,0:T(8,128)(2,1)S(1)} %get-tuple-element.49), channel_id=1, source_target_pairs={{0,1},{1,2},{2,3},{3,4},{4,5},{5,6},{6,7},{7,8},{8,9},{9,10},{10,1... | collective-permute-start | bytes 497672 | tf_op jit(solution)/shard_map/ppermute | solution.py:784
  4.6 0.0 copy-start
  4.6 0.0 copy-start.1
  4.6 0.0 copy-start.2
  4.6 0.0 copy-start.3
  4.6 0.0 copy-start.4
  4.6 0.0 copy-start.5
  4.6 0.0 copy-start.6
  4.6 0.0 copy-start.7
  4.6 0.0 copy-start.8
  4.6 4.8 %bias_rows.1 = (f32[3456,128]{1,0:T(8,128)S(1)}, f32[3456,128]{1,0:T(8,128)S(1)}) custom-call(f32[6,4,3312]{2,1,0:T(4,128)S(1)} %get-tuple-element.51.table_ref, s32[144,144]{1,0:T(8,128)S(1)} %get-tuple-element.52.index_ref, s32[2,24]{1,0:T(2,128)} %regions_ref.1), custom_call_target="tpu_custom_call" | custom-call | flops 14000000000 | bytes 4000000 | tf_op jit(solution)/shard_map/bias_rows/pallas_call | solution.py:268
  9.5 13.8 %collective-permute-done.west_ref = bf16[9,24,384]{2,1,0:T(8,128)(2,1)S(1)} collective-permute-done((bf16[9,24,384]{2,1,0:T(8,128)(2,1)S(1)}, bf16[9,24,384]{2,1,0:T(8,128)(2,1)S(1)}, u32[]{:S(2)}, u32[]{:S(2)}) %collective-permute-start) | collective-permute-done | bytes 165920 | tf_op jit(solution)/shard_map/ppermute | solution.py:784
  23.2 0.0 copy-done
  23.2 0.0 copy-done.1
  23.2 0.0 copy-done.2
  23.2 0.0 copy-done.3
  23.2 0.0 copy-done.4
  23.3 0.0 copy-done.5
  23.3 0.0 copy-done.6
  23.3 0.0 copy-done.7
  23.3 0.0 copy-done.8
  23.3 9.3 %block.1 = (bf16[6400,128]{1,0:T(8,128)(2,1)S(1)}, bf16[576,192]{1,0:T(8,128)(2,1)S(1)}, bf16[4224,128]{1,0:T(8,128)(2,1)S(1)}, bf16[4,160,192]{2,1,0:T(8,128)(2...) custom-call(bf16[2,12,24,192]{3,2,1,0:T(8,128)(2,1)S(1)} %bitcast.18, ...), custom_call_target="tpu_custom_call" | custom-call | flops 24000000000 | bytes 12000000 | tf_op jit(solution)/shard_map/block/pallas_call | solution.py:485
  32.5 7.7 %collective-permute-start.2 = (bf16[4224,128]{1,0:T(8,128)(2,1)S(1)}, bf16[4224,128]{1,0:T(8,128)(2,1)S(1)}, u32[]{:S(2)}, u32[]{:S(2)}) collective-permute-start(bf16[4224,128]{1,0:T(8,128)(2,1)S(1)} %get-tuple-element.60.own_ref), channel_id=1, source_target_pairs={{0,1},{1,0},{2,3},{3,2},{4,5},{5,4},{6,7},{7,6},{8,9},{9,8},{10,11... | collective-permute-start | bytes 3244040 | tf_op jit(solution)/shard_map/ppermute | solution.py:864
  40.3 0.6 pack.1
  40.9 0.2 collective-permute-start.1
  41.0 1.6 %collective-permute-done.2.partner_ref = bf16[4224,128]{1,0:T(8,128)(2,1)S(1)} collective-permute-done((bf16[4224,128]{1,0:T(8,128)(2,1)S(1)}, bf16[4224,128]{1,0:T(8,128)(2,1)S(1)}, u32[]{:S(2)}, u32[]{:S(2)}) %collective-permute-start.2) | collective-permute-done | bytes 1081376 | tf_op jit(solution)/shard_map/ppermute | solution.py:864
  42.6 1.1 collective-permute-done.1.arrived_ref
  43.8 1.1 join.1
  44.9 4.3 %all-to-all-start = ((bf16[4,800,128]{2,1,0:T(8,128)(2,1)}), bf16[4,800,128]{2,1,0:T(8,128)(2,1)}, u32[]{:S(2)}, u32[]{:S(2)}) async-start(bf16[4,800,128]{2,1,0:T(8,128)(2,1)} %bitcast.7), calls=%async_computation | async-start | bytes 1638400 | tf_op jit(solution)/shard_map/all_to_all | solution.py:803
  49.2 1.4 %to_grid.1 = (bf16[12,3,2,384]{3,2,1,0:T(2,128)(2,1)S(1)}, bf16[2,6,24,192]{3,2,1,0:T(8,128)(2,1)S(1)}, bf16[9,24,384]{2,1,0:T(8,128)(2,1)S(1)}) custom-call(bf16[4,160,192]{2,1,0:T(8,128)(2,1)S(1)} %get-tuple-element.61.normed_merge_ref, bf16[576,576]{1,0:T(8,128)(2,1)S(1)} %get-tuple-element.57.triple_ref, ...), custom_call_target="tpu_custom_call" | custom-call | flops 1500000000 | bytes 3000000 | tf_op jit(solution)/shard_map/to_grid/pallas_call | solution.py:636
  50.6 3.1 %collective-permute-start.3 = (bf16[9,24,384]{2,1,0:T(8,128)(2,1)S(1)}, bf16[9,24,384]{2,1,0:T(8,128)(2,1)S(1)}, u32[]{:S(2)}, u32[]{:S(2)}) collective-permute-start(bf16[9,24,384]{2,1,0:T(8,128)(2,1)S(1)} %get-tuple-element.65), channel_id=1, source_target_pairs={{0,1},{1,0},{2,3},{3,2},{4,5},{5,4},{6,7},{7,6},{8,9},{9,8},{10,11... | collective-permute-start | bytes 497672 | tf_op jit(solution)/shard_map/ppermute | solution.py:867
  53.6 5.0 %all-to-all-done = bf16[4,800,128]{2,1,0:T(8,128)(2,1)} async-done(((bf16[4,800,128]{2,1,0:T(8,128)(2,1)}), bf16[4,800,128]{2,1,0:T(8,128)(2,1)}, u32[]{:S(2)}, u32[]{:S(2)}) %all-to-all-start) | async-done | bytes 819232 | tf_op jit(solution)/shard_map/all_to_all | solution.py:803
  58.7 1.3 %reduce_sum.24 = bf16[800,128]{1,0:T(8,128)(2,1)S(1)} reduce(bf16[4,800,128]{2,1,0:T(8,128)(2,1)} %all-to-all-done, bf16[]{:T(256)} %constant.20.clone.1), dimensions={0}, to_apply=%region_0.1 | reduce | flops 307200 | bytes 1024002 | tf_op jit(solution)/shard_map/reduce_sum | solution.py:807
  60.0 0.0 collective-permute-done.3.refs_2_
  60.0 15.1 %all_to_all.20 = bf16[16,25,2,128]{3,2,1,0:T(2,128)(2,1)S(1)} all-to-all(bf16[16,25,2,128]{3,2,1,0:T(2,128)(2,1)S(1)} %bitcast.25), channel_id=1, replica_groups={{0,8,16,24,32,40,48,56,64,72,80,88,96,104,112,120},{1,9,17,25,33,41,49,..., dimensions={0} | all-to-all | bytes 409600 | tf_op jit(solution)/shard_map/all_to_all | solution.py:803
  75.1 0.2 reduce_sum.25
  75.3 0.1 broadcast_in_dim.6
  75.4 17.4 %all_to_all.21 = bf16[16,25,2,128]{3,2,1,0:T(2,128)(2,1)S(1)} all-to-all(bf16[16,25,2,128]{3,2,1,0:T(2,128)(2,1)S(1)} %broadcast_in_dim.6), channel_id=1, replica_groups={{0,8,16,24,32,40,48,56,64,72,80,88,96,104,112,120},{1,9,17,25,33,41,49,..., dimensions={0} | all-to-all | bytes 409600 | tf_op jit(solution)/shard_map/all_to_all | solution.py:803
  92.8 0.1 broadcast_in_dim.15
  92.9 10.9 %all_to_all.22 = bf16[4,800,128]{2,1,0:T(8,128)(2,1)S(1)} all-to-all(bf16[4,800,128]{2,1,0:T(8,128)(2,1)S(1)} %broadcast_in_dim.15), channel_id=1, replica_groups={{0,2,4,6},{1,3,5,7},{8,10,12,14},{9,11,13,15},{16,18,20,22},{17,19,21,2..., dimensions={0} | all-to-all | bytes 1638400 | tf_op jit(solution)/shard_map/all_to_all | solution.py:803
  103.8 7.7 %collective-permute-start.5 = (bf16[3200,128]{1,0:T(8,128)(2,1)S(1)}, bf16[3200,128]{1,0:T(8,128)(2,1)S(1)}, u32[]{:S(2)}, u32[]{:S(2)}) collective-permute-start(bf16[3200,128]{1,0:T(8,128)(2,1)S(1)} %bitcast.15), channel_id=1, source_target_pairs={{0,1},{1,0},{2,3},{3,2},{4,5},{5,4},{6,7},{7,6},{8,9},{9,8},{10,11... | collective-permute-start | bytes 2457608 | tf_op jit(solution)/shard_map/ppermute | solution.py:818
  111.5 6.0 %collective-permute-start.4 = (bf16[9,24,384]{2,1,0:T(8,128)(2,1)S(1)}, bf16[9,24,384]{2,1,0:T(8,128)(2,1)S(1)}, u32[]{:S(2)}, u32[]{:S(2)}) collective-permute-start(bf16[9,24,384]{2,1,0:T(8,128)(2,1)S(1)} %collective-permute-done.3.refs_2_), channel_id=1, source_target_pairs={{1,127},{3,1},{5,3},{7,5},{9,7},{11,9},{13,11},{15,13},{17,15},{19... | collective-permute-start | bytes 497672 | tf_op jit(solution)/shard_map/ppermute | solution.py:871
  117.5 2.3 %collective-permute-done.4.refs_3_ = bf16[9,24,384]{2,1,0:T(8,128)(2,1)S(1)} collective-permute-done((bf16[9,24,384]{2,1,0:T(8,128)(2,1)S(1)}, bf16[9,24,384]{2,1,0:T(8,128)(2,1)S(1)}, u32[]{:S(2)}, u32[]{:S(2)}) %collective-permute-start.4) | collective-permute-done | bytes 165920 | tf_op jit(solution)/shard_map/ppermute | solution.py:871
  119.7 1.5 %finish_own.1 = (bf16[12,6,2,384]{3,2,1,0:T(2,128)(2,1)}, bf16[2,12,24,192]{3,2,1,0:T(8,128)(2,1)}, f32[192,768]{1,0:T(8,128)}, f32[192,768]{1,0:T(8,128)}, f32[...) custom-call(s32[1]{0:T(128)} %bitcast.3.core_ref.refs_0_, ...), custom_call_target="tpu_custom_call" | custom-call | flops 400000 | bytes 2500000 | tf_op jit(solution)/shard_map/finish_own/pallas_call | solution.py:759
  121.2 0.0 collective-permute-done.5.refs_1_
  121.2 1.3 %finish_other.1 = (f32[192,768]{1,0:T(8,128)}, f32[192,768]{1,0:T(8,128)}, f32[192,576]{1,0:T(8,128)}, f32[768,384]{1,0:T(8,128)}, f32[192,192]{1,0:T(8,128)}, /*index=5*/f32[6,4,3312]{2,1,0:T(4,128)}) custom-call(s32[1]{0:T(128)} %bitcast.3.core_ref.refs_0_, ...), custom_call_target="tpu_custom_call", output_to_operand_aliasing={{0}: (2, {}), {1}: (3, {}), {2}: (4, {}), {3}: (5, {}), {4}... | custom-call | tf_op jit(solution)/shard_map/finish_other/pallas_call | solution.py:769
  (1 shorter events, 0.0 us)
Async XLA Ops:
  1.8 21.4 %collective-permute-start = (bf16[9,24,384]{2,1,0:T(8,128)(2,1)S(1)}, bf16[9,24,384]{2,1,0:T(8,128)(2,1)S(1)}, u32[]{:S(2)}, u32[]{:S(2)}) collective-permute-start(bf16[9,24,384]{2,1,0:T(8,128)(2,1)S(1)} %get-tuple-element.49), channel_id=1, source_target_pairs={{0,1},{1,2},{2,3},{3,4},{4,5},{5,6},{6,7},{7,8},{8,9},{9,10},{10,1... | collective-permute-start | bytes 497672 | tf_op jit(solution)/shard_map/ppermute | solution.py:784
  4.6 18.7 %copy-start = (bf16[2,24,12,192]{3,1,2,0:T(8,128)(2,1)S(1)}, bf16[2,24,12,192]{3,1,2,0:T(8,128)(2,1)}, u32[]{:S(2)}) copy-start(bf16[2,24,12,192]{3,1,2,0:T(8,128)(2,1)} %param.13) | copy-start | bytes 663556
  4.6 18.7 %copy-start.1 = (bf16[2,12,6,384]{3,0,2,1:T(2,128)(2,1)S(1)}, bf16[2,12,6,384]{3,0,2,1:T(2,128)(2,1)}, u32[]{:S(2)}) copy-start(bf16[2,12,6,384]{3,0,2,1:T(2,128)(2,1)} %param.25) | copy-start | bytes 331780
  4.6 18.7 %copy-start.2 = (bf16[768,384]{1,0:T(8,128)(2,1)S(1)}, bf16[768,384]{1,0:T(8,128)(2,1)}, u32[]{:S(2)}) copy-start(bf16[768,384]{1,0:T(8,128)(2,1)} %merge_ref.3) | copy-start | bytes 1769476
  4.6 18.7 %copy-start.3 = (bf16[192,768]{1,0:T(8,128)(2,1)S(1)}, bf16[192,768]{1,0:T(8,128)(2,1)}, u32[]{:S(2)}) copy-start(bf16[192,768]{1,0:T(8,128)(2,1)} %up_ref.1) | copy-start | bytes 884740
  4.6 18.7 %copy-start.4 = (bf16[768,192]{0,1:T(8,128)(2,1)S(1)}, bf16[768,192]{0,1:T(8,128)(2,1)}, u32[]{:S(2)}) copy-start(bf16[768,192]{0,1:T(8,128)(2,1)} %param.22) | copy-start | bytes 884740
  4.6 18.7 %copy-start.5 = (bf16[192,576]{1,0:T(8,128)(2,1)S(1)}, bf16[192,576]{1,0:T(8,128)(2,1)}, u32[]{:S(2)}) copy-start(bf16[192,576]{1,0:T(8,128)(2,1)} %qkv_ref.3) | copy-start | bytes 663556
  4.6 18.7 %copy-start.6 = (bf16[192,192]{1,0:T(8,128)(2,1)S(1)}, bf16[192,192]{1,0:T(8,128)(2,1)}, u32[]{:S(2)}) copy-start(bf16[192,192]{1,0:T(8,128)(2,1)} %proj_ref.1) | copy-start | bytes 221188
  4.6 18.7 %copy-start.7 = (f32[192]{0:T(256)S(1)}, f32[192]{0:T(256)}, u32[]{:S(2)}) copy-start(f32[192]{0:T(256)} %param.20) | copy-start | bytes 2308
  4.6 18.7 %copy-start.8 = (f32[192]{0:T(256)S(1)}, f32[192]{0:T(256)}, u32[]{:S(2)}) copy-start(f32[192]{0:T(256)} %param.14) | copy-start | bytes 2308
  32.5 10.1 %collective-permute-start.2 = (bf16[4224,128]{1,0:T(8,128)(2,1)S(1)}, bf16[4224,128]{1,0:T(8,128)(2,1)S(1)}, u32[]{:S(2)}, u32[]{:S(2)}) collective-permute-start(bf16[4224,128]{1,0:T(8,128)(2,1)S(1)} %get-tuple-element.60.own_ref), channel_id=1, source_target_pairs={{0,1},{1,0},{2,3},{3,2},{4,5},{5,4},{6,7},{7,6},{8,9},{9,8},{10,11... | collective-permute-start | bytes 3244040 | tf_op jit(solution)/shard_map/ppermute | solution.py:864
  40.9 2.9 %collective-permute-start.1 = (bf16[3200,128]{1,0:T(8,128)(2,1)S(1)}, bf16[3200,128]{1,0:T(8,128)(2,1)S(1)}, u32[]{:S(2)}, u32[]{:S(2)}) collective-permute-start(bf16[3200,128]{1,0:T(8,128)(2,1)S(1)} %get-tuple-element.59), channel_id=1, source_target_pairs={{0,1},{1,0},{2,3},{3,2},{4,5},{5,4},{6,7},{7,6},{8,9},{9,8},{10,11... | collective-permute-start | bytes 2457608 | tf_op jit(solution)/shard_map/ppermute | solution.py:799
  44.9 13.8 %all-to-all-start = ((bf16[4,800,128]{2,1,0:T(8,128)(2,1)}), bf16[4,800,128]{2,1,0:T(8,128)(2,1)}, u32[]{:S(2)}, u32[]{:S(2)}) async-start(bf16[4,800,128]{2,1,0:T(8,128)(2,1)} %bitcast.7), calls=%async_computation | async-start | bytes 1638400 | tf_op jit(solution)/shard_map/all_to_all | solution.py:803
  50.6 9.4 %collective-permute-start.3 = (bf16[9,24,384]{2,1,0:T(8,128)(2,1)S(1)}, bf16[9,24,384]{2,1,0:T(8,128)(2,1)S(1)}, u32[]{:S(2)}, u32[]{:S(2)}) collective-permute-start(bf16[9,24,384]{2,1,0:T(8,128)(2,1)S(1)} %get-tuple-element.65), channel_id=1, source_target_pairs={{0,1},{1,0},{2,3},{3,2},{4,5},{5,4},{6,7},{7,6},{8,9},{9,8},{10,11... | collective-permute-start | bytes 497672 | tf_op jit(solution)/shard_map/ppermute | solution.py:867
  103.8 17.4 %collective-permute-start.5 = (bf16[3200,128]{1,0:T(8,128)(2,1)S(1)}, bf16[3200,128]{1,0:T(8,128)(2,1)S(1)}, u32[]{:S(2)}, u32[]{:S(2)}) collective-permute-start(bf16[3200,128]{1,0:T(8,128)(2,1)S(1)} %bitcast.15), channel_id=1, source_target_pairs={{0,1},{1,0},{2,3},{3,2},{4,5},{5,4},{6,7},{7,6},{8,9},{9,8},{10,11... | collective-permute-start | bytes 2457608 | tf_op jit(solution)/shard_map/ppermute | solution.py:818
  111.5 8.2 %collective-permute-start.4 = (bf16[9,24,384]{2,1,0:T(8,128)(2,1)S(1)}, bf16[9,24,384]{2,1,0:T(8,128)(2,1)S(1)}, u32[]{:S(2)}, u32[]{:S(2)}) collective-permute-start(bf16[9,24,384]{2,1,0:T(8,128)(2,1)S(1)} %collective-permute-done.3.refs_2_), channel_id=1, source_target_pairs={{1,127},{3,1},{5,3},{7,5},{9,7},{11,9},{13,11},{15,13},{17,15},{19... | collective-permute-start | bytes 497672 | tf_op jit(solution)/shard_map/ppermute | solution.py:871

commit v10 on v9

--- a/solution.py
+++ b/solution.py
@@ -603,6 +603,28 @@
     )(core, keep, arrived, table)
 
 
+def spread_kernel(got_ref, out_ref):
+    total = got_ref[0].astype(F32)
+    for n in range(1, got_ref.shape[0]):
+        total = total + got_ref[n].astype(F32)
+    total = total.astype(BF)
+    for n in range(got_ref.shape[0]):
+        out_ref[n] = total
+
+
+def added_and_spread(got):
+    whole = pl.BlockSpec(memory_space=pltpu.VMEM)
+    return pl.pallas_call(
+        spread_kernel,
+        out_shape=jax.ShapeDtypeStruct(got.shape, BF),
+        in_specs=[whole],
+        out_specs=whole,
+        compiler_params=pltpu.CompilerParams(vmem_limit_bytes=8 * 1024 * 1024),
+        cost_estimate=pl.CostEstimate(flops=200_000, bytes_accessed=400_000, transcendentals=0),
+        name="added_and_spread",
+    )(got)
+
+
 def cells_kernel(
     normed_merge_ref, triple_ref, grad_attn_ref, unit_ref, scale_ref, qkv_ref, gain_ref, merge_ref,
     merged_keep_ref, field_keep_ref, home_ref, x_ref,
@@ -811,8 +833,8 @@
 
     held = reduced(held, CORES, ACROSS)
     held, partner = lax.optimization_barrier((held, partner))
-    held = reduced(held.reshape(-1, 2, LANES), CORES * ACROSS, along)
-    held = gathered(held, CORES * ACROSS, along).reshape(-1, LANES)
+    held = exchanged(held.reshape(along, -1, 2, LANES), CORES * ACROSS, along)
+    held = exchanged(added_and_spread(held), CORES * ACROSS, along).reshape(-1, LANES)
     held = gathered(held, CORES, ACROSS)
     held, forwarded = forward(held, partner)
     return held, lax.ppermute(held, axis, pairs), partner, forwarded

time: 123 us -> 123 us (level)
  no operation moved by 1% of the time
where the time goes in v10:
time: 123 us
  blocking collectives  43.4 us (35%)
  starting transfers between devices  31.7 us (26%)
  waiting for transfers between devices  23.8 us (19%)
  Pallas kernels  21.2 us (17%)
  other arithmetic  1.32 us (1%)
    all_to_all x3, blocking collectives, exchanged(): lax.all_to_all(value, axis, 0, 0, axis_index_groups=groups_of(count, apar...  43.4 us
    ppermute x1, waiting for transfers between devices, passed_along(): lax.ppermute(value, axis, [(source, (source + steps) % count) for source...  13.8 us
    pallas_call x1, Pallas kernels, block(): pl.pallas_call(block_kernel, out_shape=[shape((2 * half_rows, LANES), BF)...  9.25 us
    ppermute x1, starting transfers between devices, local(): partner_scores = lax.ppermute(scores, 'lon', pairs)  7.74 us
    ppermute x1, starting transfers between devices, summed_over(): return (held, lax.ppermute(held, axis, pairs), partner, forwarded)  7.68 us
    ppermute x1, starting transfers between devices, forward(): lax.ppermute(leaving, 'lon', [(i, (i - CORES) % count) for i in range(1,...  5.95 us
    all_to_all x1, waiting for transfers between devices, exchanged(): lax.all_to_all(value, axis, 0, 0, axis_index_groups=groups_of(count, apar...  5.02 us
    pallas_call x1, Pallas kernels, bias_rows(): pl.pallas_call(bias_kernel, out_shape=[jax.ShapeDtypeStruct((TH * WIN, LA...  4.81 us
  transfers between devices with their start and end apart: 7, of which 5 were waited for; matrix products, arithmetic and copies ran while one was open for 1% of the time, Pallas kernels for 7%

profile of v10, /device:TPU:33, one launch (start us, length us, event | category | flops | bytes accessed | tf_op | source)
XLA Modules:
  0.0 122.5 jit_solution(18356180489686433421)
XLA Ops:
  0.6 1.2 stage.1
  1.8 2.8 %collective-permute-start = (bf16[9,24,384]{2,1,0:T(8,128)(2,1)S(1)}, bf16[9,24,384]{2,1,0:T(8,128)(2,1)S(1)}, u32[]{:S(2)}, u32[]{:S(2)}) collective-permute-start(bf16[9,24,384]{2,1,0:T(8,128)(2,1)S(1)} %get-tuple-element.49), channel_id=1, source_target_pairs={{0,1},{1,2},{2,3},{3,4},{4,5},{5,6},{6,7},{7,8},{8,9},{9,10},{10,1... | collective-permute-start | bytes 497672 | tf_op jit(solution)/shard_map/ppermute | solution.py:806
  4.6 0.0 copy-start
  4.6 0.0 copy-start.1
  4.6 0.0 copy-start.2
  4.6 0.0 copy-start.3
  4.6 0.0 copy-start.4
  4.6 0.0 copy-start.5
  4.6 0.0 copy-start.6
  4.6 0.0 copy-start.7
  4.6 0.0 copy-start.8
  4.6 4.8 %bias_rows.1 = (f32[3456,128]{1,0:T(8,128)S(1)}, f32[3456,128]{1,0:T(8,128)S(1)}) custom-call(f32[6,4,3312]{2,1,0:T(4,128)S(1)} %get-tuple-element.51.table_ref, s32[144,144]{1,0:T(8,128)S(1)} %get-tuple-element.52.index_ref, s32[2,24]{1,0:T(2,128)} %regions_ref.1), custom_call_target="tpu_custom_call" | custom-call | flops 14000000000 | bytes 4000000 | tf_op jit(solution)/shard_map/bias_rows/pallas_call | solution.py:268
  9.5 13.8 %collective-permute-done.west_ref = bf16[9,24,384]{2,1,0:T(8,128)(2,1)S(1)} collective-permute-done((bf16[9,24,384]{2,1,0:T(8,128)(2,1)S(1)}, bf16[9,24,384]{2,1,0:T(8,128)(2,1)S(1)}, u32[]{:S(2)}, u32[]{:S(2)}) %collective-permute-start) | collective-permute-done | bytes 165920 | tf_op jit(solution)/shard_map/ppermute | solution.py:806
  23.2 0.0 copy-done
  23.2 0.0 copy-done.1
  23.2 0.0 copy-done.2
  23.2 0.0 copy-done.3
  23.2 0.0 copy-done.4
  23.3 0.0 copy-done.5
  23.3 0.0 copy-done.6
  23.3 0.0 copy-done.7
  23.3 0.0 copy-done.8
  23.3 9.3 %block.1 = (bf16[6400,128]{1,0:T(8,128)(2,1)S(1)}, bf16[576,192]{1,0:T(8,128)(2,1)S(1)}, bf16[4224,128]{1,0:T(8,128)(2,1)S(1)}, bf16[4,160,192]{2,1,0:T(8,128)(2...) custom-call(bf16[2,12,24,192]{3,2,1,0:T(8,128)(2,1)S(1)} %bitcast.18, ...), custom_call_target="tpu_custom_call" | custom-call | flops 24000000000 | bytes 12000000 | tf_op jit(solution)/shard_map/block/pallas_call | solution.py:485
  32.5 7.7 %collective-permute-start.2 = (bf16[4224,128]{1,0:T(8,128)(2,1)S(1)}, bf16[4224,128]{1,0:T(8,128)(2,1)S(1)}, u32[]{:S(2)}, u32[]{:S(2)}) collective-permute-start(bf16[4224,128]{1,0:T(8,128)(2,1)S(1)} %get-tuple-element.60.own_ref), channel_id=1, source_target_pairs={{0,1},{1,0},{2,3},{3,2},{4,5},{5,4},{6,7},{7,6},{8,9},{9,8},{10,11... | collective-permute-start | bytes 3244040 | tf_op jit(solution)/shard_map/ppermute | solution.py:886
  40.3 0.6 pack.1
  40.9 0.2 collective-permute-start.1
  41.0 1.6 %collective-permute-done.2.partner_ref = bf16[4224,128]{1,0:T(8,128)(2,1)S(1)} collective-permute-done((bf16[4224,128]{1,0:T(8,128)(2,1)S(1)}, bf16[4224,128]{1,0:T(8,128)(2,1)S(1)}, u32[]{:S(2)}, u32[]{:S(2)}) %collective-permute-start.2) | collective-permute-done | bytes 1081376 | tf_op jit(solution)/shard_map/ppermute | solution.py:886
  42.6 1.1 collective-permute-done.1.arrived_ref
  43.8 1.1 join.1
  44.9 4.3 %all-to-all-start = ((bf16[4,800,128]{2,1,0:T(8,128)(2,1)}), bf16[4,800,128]{2,1,0:T(8,128)(2,1)}, u32[]{:S(2)}, u32[]{:S(2)}) async-start(bf16[4,800,128]{2,1,0:T(8,128)(2,1)} %bitcast.7), calls=%async_computation | async-start | bytes 1638400 | tf_op jit(solution)/shard_map/all_to_all | solution.py:825
  49.2 1.4 %to_grid.1 = (bf16[12,3,2,384]{3,2,1,0:T(2,128)(2,1)S(1)}, bf16[2,6,24,192]{3,2,1,0:T(8,128)(2,1)S(1)}, bf16[9,24,384]{2,1,0:T(8,128)(2,1)S(1)}) custom-call(bf16[4,160,192]{2,1,0:T(8,128)(2,1)S(1)} %get-tuple-element.61.normed_merge_ref, bf16[576,576]{1,0:T(8,128)(2,1)S(1)} %get-tuple-element.57.triple_ref, ...), custom_call_target="tpu_custom_call" | custom-call | flops 1500000000 | bytes 3000000 | tf_op jit(solution)/shard_map/to_grid/pallas_call | solution.py:658
  50.5 3.1 %collective-permute-start.3 = (bf16[9,24,384]{2,1,0:T(8,128)(2,1)S(1)}, bf16[9,24,384]{2,1,0:T(8,128)(2,1)S(1)}, u32[]{:S(2)}, u32[]{:S(2)}) collective-permute-start(bf16[9,24,384]{2,1,0:T(8,128)(2,1)S(1)} %get-tuple-element.65), channel_id=1, source_target_pairs={{0,1},{1,0},{2,3},{3,2},{4,5},{5,4},{6,7},{7,6},{8,9},{9,8},{10,11... | collective-permute-start | bytes 497672 | tf_op jit(solution)/shard_map/ppermute | solution.py:889
  53.6 5.0 %all-to-all-done = bf16[4,800,128]{2,1,0:T(8,128)(2,1)} async-done(((bf16[4,800,128]{2,1,0:T(8,128)(2,1)}), bf16[4,800,128]{2,1,0:T(8,128)(2,1)}, u32[]{:S(2)}, u32[]{:S(2)}) %all-to-all-start) | async-done | bytes 819232 | tf_op jit(solution)/shard_map/all_to_all | solution.py:825
  58.6 1.3 %reduce_sum.12 = bf16[800,128]{1,0:T(8,128)(2,1)S(1)} reduce(bf16[4,800,128]{2,1,0:T(8,128)(2,1)} %all-to-all-done, bf16[]{:T(256)} %constant.19.clone.1), dimensions={0}, to_apply=%region_0.1 | reduce | flops 307200 | bytes 1024002 | tf_op jit(solution)/shard_map/reduce_sum | solution.py:829
  60.0 0.0 collective-permute-done.3.refs_2_
  60.0 15.1 %all_to_all.20.got_ref = bf16[16,25,2,128]{3,2,1,0:T(2,128)(2,1)S(1)} all-to-all(bf16[16,25,2,128]{3,2,1,0:T(2,128)(2,1)S(1)} %bitcast.25), channel_id=1, replica_groups={{0,8,16,24,32,40,48,56,64,72,80,88,96,104,112,120},{1,9,17,25,33,41,49,..., dimensions={0} | all-to-all | bytes 409600 | tf_op jit(solution)/shard_map/all_to_all | solution.py:825
  75.1 0.1 added_and_spread.1
  75.3 17.4 %all_to_all.21 = bf16[16,25,2,128]{3,2,1,0:T(2,128)(2,1)S(1)} all-to-all(bf16[16,25,2,128]{3,2,1,0:T(2,128)(2,1)S(1)} %added_and_spread.1), channel_id=1, replica_groups={{0,8,16,24,32,40,48,56,64,72,80,88,96,104,112,120},{1,9,17,25,33,41,49,..., dimensions={0} | all-to-all | bytes 409600 | tf_op jit(solution)/shard_map/all_to_all | solution.py:825
  92.6 0.1 broadcast_in_dim.8
  92.8 10.9 %all_to_all.22 = bf16[4,800,128]{2,1,0:T(8,128)(2,1)S(1)} all-to-all(bf16[4,800,128]{2,1,0:T(8,128)(2,1)S(1)} %broadcast_in_dim.8), channel_id=1, replica_groups={{0,2,4,6},{1,3,5,7},{8,10,12,14},{9,11,13,15},{16,18,20,22},{17,19,21,2..., dimensions={0} | all-to-all | bytes 1638400 | tf_op jit(solution)/shard_map/all_to_all | solution.py:825
  103.7 7.7 %collective-permute-start.5 = (bf16[3200,128]{1,0:T(8,128)(2,1)S(1)}, bf16[3200,128]{1,0:T(8,128)(2,1)S(1)}, u32[]{:S(2)}, u32[]{:S(2)}) collective-permute-start(bf16[3200,128]{1,0:T(8,128)(2,1)S(1)} %bitcast.15), channel_id=1, source_target_pairs={{0,1},{1,0},{2,3},{3,2},{4,5},{5,4},{6,7},{7,6},{8,9},{9,8},{10,11... | collective-permute-start | bytes 2457608 | tf_op jit(solution)/shard_map/ppermute | solution.py:840
  111.4 6.0 %collective-permute-start.4 = (bf16[9,24,384]{2,1,0:T(8,128)(2,1)S(1)}, bf16[9,24,384]{2,1,0:T(8,128)(2,1)S(1)}, u32[]{:S(2)}, u32[]{:S(2)}) collective-permute-start(bf16[9,24,384]{2,1,0:T(8,128)(2,1)S(1)} %collective-permute-done.3.refs_2_), channel_id=1, source_target_pairs={{1,127},{3,1},{5,3},{7,5},{9,7},{11,9},{13,11},{15,13},{17,15},{19... | collective-permute-start | bytes 497672 | tf_op jit(solution)/shard_map/ppermute | solution.py:893
  117.3 2.3 %collective-permute-done.4.refs_3_ = bf16[9,24,384]{2,1,0:T(8,128)(2,1)S(1)} collective-permute-done((bf16[9,24,384]{2,1,0:T(8,128)(2,1)S(1)}, bf16[9,24,384]{2,1,0:T(8,128)(2,1)S(1)}, u32[]{:S(2)}, u32[]{:S(2)}) %collective-permute-start.4) | collective-permute-done | bytes 165920 | tf_op jit(solution)/shard_map/ppermute | solution.py:893
  119.6 1.5 %finish_own.1 = (bf16[12,6,2,384]{3,2,1,0:T(2,128)(2,1)}, bf16[2,12,24,192]{3,2,1,0:T(8,128)(2,1)}, f32[192,768]{1,0:T(8,128)}, f32[192,768]{1,0:T(8,128)}, f32[...) custom-call(s32[1]{0:T(128)} %bitcast.3.core_ref.refs_0_, ...), custom_call_target="tpu_custom_call" | custom-call | flops 400000 | bytes 2500000 | tf_op jit(solution)/shard_map/finish_own/pallas_call | solution.py:781
  121.1 0.0 collective-permute-done.5.refs_1_
  121.1 1.3 %finish_other.1 = (f32[192,768]{1,0:T(8,128)}, f32[192,768]{1,0:T(8,128)}, f32[192,576]{1,0:T(8,128)}, f32[768,384]{1,0:T(8,128)}, f32[192,192]{1,0:T(8,128)}, /*index=5*/f32[6,4,3312]{2,1,0:T(4,128)}) custom-call(s32[1]{0:T(128)} %bitcast.3.core_ref.refs_0_, ...), custom_call_target="tpu_custom_call", output_to_operand_aliasing={{0}: (2, {}), {1}: (3, {}), {2}: (4, {}), {3}: (5, {}), {4}... | custom-call | tf_op jit(solution)/shard_map/finish_other/pallas_call | solution.py:791
  (1 shorter events, 0.0 us)
Async XLA Ops:
  1.8 21.4 %collective-permute-start = (bf16[9,24,384]{2,1,0:T(8,128)(2,1)S(1)}, bf16[9,24,384]{2,1,0:T(8,128)(2,1)S(1)}, u32[]{:S(2)}, u32[]{:S(2)}) collective-permute-start(bf16[9,24,384]{2,1,0:T(8,128)(2,1)S(1)} %get-tuple-element.49), channel_id=1, source_target_pairs={{0,1},{1,2},{2,3},{3,4},{4,5},{5,6},{6,7},{7,8},{8,9},{9,10},{10,1... | collective-permute-start | bytes 497672 | tf_op jit(solution)/shard_map/ppermute | solution.py:806
  4.6 18.7 %copy-start = (bf16[2,24,12,192]{3,1,2,0:T(8,128)(2,1)S(1)}, bf16[2,24,12,192]{3,1,2,0:T(8,128)(2,1)}, u32[]{:S(2)}) copy-start(bf16[2,24,12,192]{3,1,2,0:T(8,128)(2,1)} %param.13) | copy-start | bytes 663556
  4.6 18.7 %copy-start.1 = (bf16[2,12,6,384]{3,0,2,1:T(2,128)(2,1)S(1)}, bf16[2,12,6,384]{3,0,2,1:T(2,128)(2,1)}, u32[]{:S(2)}) copy-start(bf16[2,12,6,384]{3,0,2,1:T(2,128)(2,1)} %param.25) | copy-start | bytes 331780
  4.6 18.7 %copy-start.2 = (bf16[768,384]{1,0:T(8,128)(2,1)S(1)}, bf16[768,384]{1,0:T(8,128)(2,1)}, u32[]{:S(2)}) copy-start(bf16[768,384]{1,0:T(8,128)(2,1)} %merge_ref.3) | copy-start | bytes 1769476
  4.6 18.7 %copy-start.3 = (bf16[192,768]{1,0:T(8,128)(2,1)S(1)}, bf16[192,768]{1,0:T(8,128)(2,1)}, u32[]{:S(2)}) copy-start(bf16[192,768]{1,0:T(8,128)(2,1)} %up_ref.1) | copy-start | bytes 884740
  4.6 18.7 %copy-start.4 = (bf16[768,192]{0,1:T(8,128)(2,1)S(1)}, bf16[768,192]{0,1:T(8,128)(2,1)}, u32[]{:S(2)}) copy-start(bf16[768,192]{0,1:T(8,128)(2,1)} %param.22) | copy-start | bytes 884740
  4.6 18.7 %copy-start.5 = (bf16[192,576]{1,0:T(8,128)(2,1)S(1)}, bf16[192,576]{1,0:T(8,128)(2,1)}, u32[]{:S(2)}) copy-start(bf16[192,576]{1,0:T(8,128)(2,1)} %qkv_ref.3) | copy-start | bytes 663556
  4.6 18.7 %copy-start.6 = (bf16[192,192]{1,0:T(8,128)(2,1)S(1)}, bf16[192,192]{1,0:T(8,128)(2,1)}, u32[]{:S(2)}) copy-start(bf16[192,192]{1,0:T(8,128)(2,1)} %proj_ref.1) | copy-start | bytes 221188
  4.6 18.7 %copy-start.7 = (f32[192]{0:T(256)S(1)}, f32[192]{0:T(256)}, u32[]{:S(2)}) copy-start(f32[192]{0:T(256)} %param.20) | copy-start | bytes 2308
  4.6 18.7 %copy-start.8 = (f32[192]{0:T(256)S(1)}, f32[192]{0:T(256)}, u32[]{:S(2)}) copy-start(f32[192]{0:T(256)} %param.14) | copy-start | bytes 2308
  32.5 10.1 %collective-permute-start.2 = (bf16[4224,128]{1,0:T(8,128)(2,1)S(1)}, bf16[4224,128]{1,0:T(8,128)(2,1)S(1)}, u32[]{:S(2)}, u32[]{:S(2)}) collective-permute-start(bf16[4224,128]{1,0:T(8,128)(2,1)S(1)} %get-tuple-element.60.own_ref), channel_id=1, source_target_pairs={{0,1},{1,0},{2,3},{3,2},{4,5},{5,4},{6,7},{7,6},{8,9},{9,8},{10,11... | collective-permute-start | bytes 3244040 | tf_op jit(solution)/shard_map/ppermute | solution.py:886
  40.9 2.9 %collective-permute-start.1 = (bf16[3200,128]{1,0:T(8,128)(2,1)S(1)}, bf16[3200,128]{1,0:T(8,128)(2,1)S(1)}, u32[]{:S(2)}, u32[]{:S(2)}) collective-permute-start(bf16[3200,128]{1,0:T(8,128)(2,1)S(1)} %get-tuple-element.59), channel_id=1, source_target_pairs={{0,1},{1,0},{2,3},{3,2},{4,5},{5,4},{6,7},{7,6},{8,9},{9,8},{10,11... | collective-permute-start | bytes 2457608 | tf_op jit(solution)/shard_map/ppermute | solution.py:821
  44.9 13.8 %all-to-all-start = ((bf16[4,800,128]{2,1,0:T(8,128)(2,1)}), bf16[4,800,128]{2,1,0:T(8,128)(2,1)}, u32[]{:S(2)}, u32[]{:S(2)}) async-start(bf16[4,800,128]{2,1,0:T(8,128)(2,1)} %bitcast.7), calls=%async_computation | async-start | bytes 1638400 | tf_op jit(solution)/shard_map/all_to_all | solution.py:825
  50.5 9.4 %collective-permute-start.3 = (bf16[9,24,384]{2,1,0:T(8,128)(2,1)S(1)}, bf16[9,24,384]{2,1,0:T(8,128)(2,1)S(1)}, u32[]{:S(2)}, u32[]{:S(2)}) collective-permute-start(bf16[9,24,384]{2,1,0:T(8,128)(2,1)S(1)} %get-tuple-element.65), channel_id=1, source_target_pairs={{0,1},{1,0},{2,3},{3,2},{4,5},{5,4},{6,7},{7,6},{8,9},{9,8},{10,11... | collective-permute-start | bytes 497672 | tf_op jit(solution)/shard_map/ppermute | solution.py:889
  103.7 17.4 %collective-permute-start.5 = (bf16[3200,128]{1,0:T(8,128)(2,1)S(1)}, bf16[3200,128]{1,0:T(8,128)(2,1)S(1)}, u32[]{:S(2)}, u32[]{:S(2)}) collective-permute-start(bf16[3200,128]{1,0:T(8,128)(2,1)S(1)} %bitcast.15), channel_id=1, source_target_pairs={{0,1},{1,0},{2,3},{3,2},{4,5},{5,4},{6,7},{7,6},{8,9},{9,8},{10,11... | collective-permute-start | bytes 2457608 | tf_op jit(solution)/shard_map/ppermute | solution.py:840
  111.4 8.2 %collective-permute-start.4 = (bf16[9,24,384]{2,1,0:T(8,128)(2,1)S(1)}, bf16[9,24,384]{2,1,0:T(8,128)(2,1)S(1)}, u32[]{:S(2)}, u32[]{:S(2)}) collective-permute-start(bf16[9,24,384]{2,1,0:T(8,128)(2,1)S(1)} %collective-permute-done.3.refs_2_), channel_id=1, source_target_pairs={{1,127},{3,1},{5,3},{7,5},{9,7},{11,9},{13,11},{15,13},{17,15},{19... | collective-permute-start | bytes 497672 | tf_op jit(solution)/shard_map/ppermute | solution.py:893
